TPU v7x, 32 devices: a whole 2x2x4 slice. The times are simulated.
32 devices in a mesh: px: 4 (over x, core), py: 8 (over z, y).
Axes of the slice: x: 2, y: 2, z: 4, core: 2. Of those that a mesh axis runs over, the one named last changes fastest.
Arguments:
- root_density: float32 [384, 384, 384], P('px', 'py'), may hold values from -6 to 6
- subgrid_density: float32 [256, 32, 1024], P(('px', 'py')), may hold values from -24 to 24
- velocity: float32 [3, 256, 32, 1024], P(None, ('px', 'py')), may hold values from -6 to 6
- slot_anchor: int32 [3, 256], replicated, may hold values from 0 to 376, as said below
- slot_count: int32 [32], replicated, may hold values from 1 to 8, as said below
- neighbour: int32 [2, 256], replicated, may hold values from -1 to 255, as said below
Outputs:
- coarse_potential: float32 [384, 384, 384], P('px', 'py')
- subgrid_potential: float32 [256, 32, 1024], P(('px', 'py'))
- kicked_velocity: float32 [3, 256, 32, 1024], P(None, ('px', 'py'))
Inputs may be any that keep to these rules, and one draw needn't show every extreme that they name: Slot j of device d is slot d * 8 + j, devices numbered in the order of px+py; it is live when j < slot_count[d]. Some device has every slot live. `slot_anchor`: entries are multiples of 8; live slots cover distinct regions of 8^3 root cells; empty slots hold 0. The region of live slot j of the device at px = p, py = q has its lower corner among the root cells that the device at px = p, py = (q + j) mod 8 holds of root_density. neighbour[0, s] is s - 8 or -1 and neighbour[1, s] is s + 8 or -1, the same slot of the device one index lower or higher along py with the same px; where set, both slots are live and the two regions lie next to each other along the second dimension, the lower one below. Empty slots hold -1.
All inputs are finite; a program needn't handle non-finite values.
Results may differ from a plain program's by a relative error of at most 0.000094.
Values sent between devices are 32-bit elements; how exact they have to be, the bound alone decides.
A program may use at most 192 MiB of HBM per device.

v0:
```python
import jax
import jax.numpy as jnp
import numpy as np
from jax import lax
from jax.experimental import pallas as pl
from jax.experimental.pallas import tpu as pltpu
from jax.sharding import PartitionSpec as P

NR = 384
REG = 8
REF = 4
SWEEPS = 4
CELLS = REG * REF
EDGE = SWEEPS
LAYERS = CELLS + 2 * EDGE
WIDE = LAYERS * CELLS
RELAXATION = 6.0 / 7.0
HIGHEST = lax.Precision.HIGHEST
HIGH = lax.Precision.HIGH
F32 = jnp.float32


def fourier_basis(length):
    cell = np.arange(length)
    rows = []
    for k in range(length):
        if k in (0, length // 2):
            rows.append(np.cos(2 * np.pi * (k * cell % length) / length) / np.sqrt(length))
        elif k < length // 2:
            rows.append(np.cos(2 * np.pi * (k * cell % length) / length) * np.sqrt(2 / length))
        else:
            rows.append(
                np.sin(2 * np.pi * ((length - k) * cell % length) / length) * np.sqrt(2 / length)
            )
    return np.stack(rows)


def pseudo_inverse(length):
    basis = fourier_basis(length)
    eig = -4 * np.sin(np.pi * np.arange(length) / length) ** 2
    scale = np.where(np.arange(length) == 0, 0.0, 1 / np.where(eig == 0, -1.0, eig))
    return (basis.T * scale) @ basis


def axis_weights(cells, first, count):
    table = np.zeros((len(cells), count))
    for row, cell in enumerate(cells):
        mark = 2 * cell - 1 + REF
        low = mark // (2 * REF)
        frac = (mark - 2 * REF * low) / (2 * REF)
        table[row, low - first] += 1 - frac
        if frac:
            table[row, low + 1 - first] += frac
    return table


PATCH_X = REG + 2
PATCH_Y = REG + 4
PATCH_Z = REG + 2


def patch_tables():
    inner = np.arange(1, CELLS + 1)
    x_side = axis_weights(np.concatenate([inner, [0, CELLS + 1]]), 0, PATCH_X)
    x_table = np.zeros((CELLS + 8, 16))
    x_table[: CELLS + 2, :PATCH_X] = x_side
    y_cells = np.arange(1 - EDGE, CELLS + EDGE + 1)
    y_side = axis_weights(y_cells, -1, PATCH_Y)
    y_out = axis_weights(np.array([-EDGE, CELLS + EDGE + 1]), -1, PATCH_Y)
    z_side = axis_weights(np.arange(CELLS + 2), 0, PATCH_Z)
    z_edge = np.zeros((CELLS, PATCH_Z))
    z_edge[0] = z_side[0]
    z_edge[-1] = z_side[-1]
    y_edge = np.zeros((LAYERS, PATCH_Y))
    y_edge[0] = y_out[0]
    y_edge[-1] = y_out[1]

    def both(ys, zs):
        return np.einsum("jb,kc->bcjk", ys, zs).reshape(PATCH_Y * PATCH_Z, WIDE)

    table = np.zeros((128, 3 * WIDE))
    table[: PATCH_Y * PATCH_Z] = np.concatenate(
        [both(y_side, z_side[1:-1]), both(y_side, z_edge), both(y_edge, z_side[1:-1])], axis=1
    )
    return x_table.astype(np.float32), table.astype(np.float32)


def from_behind(value, axis, steps):
    count = lax.axis_size(axis)
    initial, last = (max(0, -steps), min(count, count - steps))
    return lax.ppermute(value, axis, [(source, source + steps) for source in range(initial, last)])


def extended(block, axis, dim, width):
    count = lax.axis_size(axis)
    forward = [(i, (i + 1) % count) for i in range(count)]
    backward = [(target, source) for source, target in forward]
    low = lax.ppermute(
        lax.slice_in_dim(block, block.shape[dim] - width, None, axis=dim), axis, forward
    )
    high = lax.ppermute(lax.slice_in_dim(block, 0, width, axis=dim), axis, backward)
    return jnp.concatenate([low, block, high], axis=dim)


def decay(length, eig_first, eig_second):
    delta = -(eig_first + eig_second)
    delta = jnp.where(delta <= 0.0, 1.0, delta)
    q = 0.5 * delta + jnp.sqrt(delta + 0.25 * delta * delta)
    return 1.0 / (1.0 + q)


def moments_kernel(f_ref, eb_ref, ec_ref, out_ref):
    rows = f_ref.shape[0]
    r = decay(NR, eb_ref[...], ec_ref[...])
    up = f_ref[0]
    down = f_ref[rows - 1]
    for i in range(1, rows):
        up = r * up + f_ref[i]
        down = r * down + f_ref[rows - 1 - i]
    out_ref[0] = up
    out_ref[1] = down


def carry_kernel(rows, order, mom_ref, eb_ref, ec_ref, out_ref):
    blocks = mom_ref.shape[0]
    band = out_ref.shape[1] // 2
    r = decay(NR, eb_ref[...], ec_ref[...])
    ratio = r
    for _ in range(rows - 1):
        ratio = ratio * r
    total = jnp.ones_like(ratio)
    up = jnp.zeros_like(ratio)
    down = jnp.zeros_like(ratio)
    for k in range(blocks):
        total = total * ratio
        up = ratio * up + mom_ref[order[k], :band]
        down = ratio * down + mom_ref[order[blocks - 1 - k], band : 2 * band]
    norm = 1.0 / (1.0 - total)
    up = up * norm
    down = down * norm
    for k in range(blocks):
        out_ref[order[k], :band] = up
        up = ratio * up + mom_ref[order[k], :band]
        other = order[blocks - 1 - k]
        out_ref[other, band : 2 * band] = down
        down = ratio * down + mom_ref[other, band : 2 * band]


def solve_kernel(f_ref, carry_ref, eb_ref, ec_ref, zero_ref, out_ref):
    rows = f_ref.shape[0]
    r = decay(NR, eb_ref[...], ec_ref[...])
    scale = -r / ((1.0 - r) * (1.0 + r))
    tile = f_ref.shape[1]
    first = lax.broadcasted_iota(jnp.int32, r.shape, 0) + pl.program_id(0) * tile
    second = lax.broadcasted_iota(jnp.int32, r.shape, 1)
    zero_mode = (first == 0) & (second == 0)
    up = carry_ref[0]
    for i in range(rows):
        up = r * up + f_ref[i]
        out_ref[i] = up
    down = carry_ref[1]
    for i in range(rows - 1, -1, -1):
        down = r * down
        value = (out_ref[i] + down) * scale
        out_ref[i] = jnp.where(zero_mode, zero_ref[i][None, :], value)
        down = down + f_ref[i]


def subgrid_kernel(
    flag_ref, patch_ref, xt_ref, yz_ref, mid_ref, low_ref, high_ref, vel_ref, pot_ref, kick_ref
):
    slot = pl.program_id(0)
    live = flag_ref[0, slot] > 0
    has_below = flag_ref[1, slot] > 0
    has_above = flag_ref[2, slot] > 0
    back_below = flag_ref[3, slot] > 0
    back_above = flag_ref[4, slot] > 0
    planes = jnp.dot(patch_ref[0], yz_ref[...], precision=HIGHEST, preferred_element_type=F32)
    coarse = jnp.dot(xt_ref[...], planes, precision=HIGHEST, preferred_element_type=F32)
    start = coarse[:CELLS, :WIDE]
    x_low = coarse[CELLS : CELLS + 1, :WIDE]
    x_high = coarse[CELLS + 1 : CELLS + 2, :WIDE]
    z_edge = coarse[:CELLS, WIDE : 2 * WIDE]
    y_edge = coarse[:CELLS, 2 * WIDE :]
    shape = (CELLS, WIDE)
    row = lax.broadcasted_iota(jnp.int32, shape, 0)
    lane = lax.broadcasted_iota(jnp.int32, shape, 1)
    third = lane % CELLS
    side = EDGE * CELLS
    end = WIDE - side
    y_above = jnp.where(lane >= WIDE - CELLS, y_edge, pltpu.roll(start, WIDE - CELLS, 1))
    y_below = jnp.where(lane < CELLS, y_edge, pltpu.roll(start, CELLS, 1))
    cut_above = (lane >= WIDE - CELLS) | (
        (lane >= side - CELLS) & (lane < side) & jnp.logical_not(back_below)
    )
    cut_below = (lane < CELLS) | (
        (lane >= end) & (lane < end + CELLS) & jnp.logical_not(back_above)
    )
    fixed = ((lane < side) & jnp.logical_not(has_below)) | (
        (lane >= end) & jnp.logical_not(has_above)
    )
    rho = jnp.concatenate([low_ref[0], mid_ref[0], high_ref[0]], axis=1) * (1.0 / (REF * REF))

    def beside(v):
        return (
            (
                jnp.where(row == 0, x_low, pltpu.roll(v, 1, 0)),
                jnp.where(row == CELLS - 1, x_high, pltpu.roll(v, CELLS - 1, 0)),
            ),
            (
                jnp.where(cut_below, y_below, pltpu.roll(v, CELLS, 1)),
                jnp.where(cut_above, y_above, pltpu.roll(v, WIDE - CELLS, 1)),
            ),
            (
                jnp.where(third == 0, z_edge, pltpu.roll(v, 1, 1)),
                jnp.where(third == CELLS - 1, z_edge, pltpu.roll(v, WIDE - 1, 1)),
            ),
        )

    v = start
    for _ in range(SWEEPS):
        first, second, last = beside(v)
        total = first[1] + first[0] + second[1] + second[0] + last[1] + last[0]
        new = (1.0 - RELAXATION) * v + RELAXATION * (total - rho) / 6.0
        v = jnp.where(fixed, v, new)
    pot_ref[0] = jnp.where(live, v[:, side:end], 0.0)
    for q, (below, above) in enumerate(beside(v)):
        slope = (above[:, side:end] - below[:, side:end]) * (REF / 2.0)
        kick_ref[q, 0] = jnp.where(live, vel_ref[q, 0] - slope, 0.0)


def poisson(root_density, beside_work):
    size_first = lax.axis_size("px")
    size_second = lax.axis_size("py")
    devices = size_first * size_second
    device = lax.axis_index("px") * size_second + lax.axis_index("py")
    block = lax.axis_index("py") * size_first + lax.axis_index("px")
    order = [(k % size_first) * size_second + k // size_first for k in range(devices)]
    basis = jnp.asarray(fourier_basis(NR), F32)
    eig = -4.0 * np.sin(np.pi / NR * np.arange(NR)) ** 2
    eig_first = jnp.asarray(eig[:, None], F32)
    eig_second = jnp.asarray(eig[None, :], F32)
    rows = NR // devices
    band = NR // devices
    planes = lax.all_to_all(
        jnp.transpose(root_density, (1, 0, 2)), "px", split_axis=0, concat_axis=1, tiled=True
    )
    f = jnp.einsum("yxz,cz->yxc", planes, basis, precision=HIGH)
    f = jnp.einsum("yxc,ax->yac", f, basis, precision=HIGH)
    f, beside = lax.optimization_barrier((f, beside_work[0]))
    beside = beside_work[1](*beside)
    tile = 48
    grid = NR // tile
    f_spec = pl.BlockSpec((rows, tile, NR), lambda t: (0, t, 0))
    pair_spec = pl.BlockSpec((2, tile, NR), lambda t: (0, t, 0))
    eb_spec = pl.BlockSpec((tile, 1), lambda t: (t, 0))
    ec_spec = pl.BlockSpec((1, NR), lambda t: (0, 0))
    params = pltpu.CompilerParams(
        dimension_semantics=("arbitrary",), vmem_limit_bytes=60 * 1024 * 1024
    )
    moments = pl.pallas_call(
        moments_kernel,
        grid=(grid,),
        in_specs=[f_spec, eb_spec, ec_spec],
        out_specs=pair_spec,
        out_shape=jax.ShapeDtypeStruct((2, NR, NR), F32),
        compiler_params=params,
    )(f, eig_first, eig_second)
    column = jnp.pad(f[:, 0, 0], (0, NR - rows))
    sent = jnp.concatenate(
        [
            moments.reshape(2, devices, band, NR).transpose(1, 0, 2, 3).reshape(
                devices, 2 * band, NR
            ),
            jnp.broadcast_to(column[None, None, :], (devices, 8, NR)),
        ],
        axis=1,
    )
    got = lax.all_to_all(sent, ("px", "py"), split_axis=0, concat_axis=0, tiled=True)
    carries = pl.pallas_call(
        lambda *refs: carry_kernel(rows, order, *refs),
        out_shape=jax.ShapeDtypeStruct((devices, 2 * band, NR), F32),
        compiler_params=pltpu.CompilerParams(vmem_limit_bytes=60 * 1024 * 1024),
    )(got, lax.dynamic_slice_in_dim(eig_first, device * band, band, 0), eig_second)
    back = lax.all_to_all(carries, ("px", "py"), split_axis=0, concat_axis=0, tiled=True)
    back = back.reshape(devices, 2, band, NR).transpose(1, 0, 2, 3).reshape(2, NR, NR)
    back, beside = lax.optimization_barrier((back, beside))
    whole_column = got[:, 2 * band, :rows].reshape(size_first, size_second, rows)
    whole_column = whole_column.transpose(1, 0, 2).reshape(NR)
    own = lax.dynamic_slice_in_dim(
        jnp.asarray(pseudo_inverse(NR), F32), block * rows, rows, 0
    )
    zero_values = jnp.sum(own * whole_column[None, :], axis=1)
    zero_wide = jnp.broadcast_to(zero_values[:, None], (rows, NR))
    u = pl.pallas_call(
        solve_kernel,
        grid=(grid,),
        in_specs=[f_spec, pair_spec, eb_spec, ec_spec, pl.BlockSpec((rows, NR), lambda t: (0, 0))],
        out_specs=f_spec,
        out_shape=jax.ShapeDtypeStruct((rows, NR, NR), F32),
        compiler_params=params,
    )(f, back, eig_first, eig_second, zero_wide)
    u = jnp.einsum("yac,ax->yxc", u, basis, precision=HIGH)
    u = jnp.einsum("yxc,cz->yxz", u, basis, precision=HIGH)
    u = u.reshape(rows, size_first, NR // size_first, NR).transpose(1, 0, 2, 3)
    u = lax.all_to_all(u, "px", split_axis=0, concat_axis=0, tiled=True)
    return u.reshape(size_first * rows, NR // size_first, NR), beside


def local(root_density, subgrid_density, velocity, slot_anchor, slot_count, neighbour):
    first_rows, second_rows = root_density.shape[:2]
    size_second = lax.axis_size("py")
    place_first = lax.axis_index("px")
    place_second = lax.axis_index("py")
    device = place_first * size_second + place_second
    per_device = subgrid_density.shape[0]
    side = EDGE * CELLS
    inner = CELLS * CELLS
    positions = jnp.arange(per_device, dtype=jnp.int32)

    def early(density, anchors, counts, near):
        low_density = from_behind(density[:, :, inner - side :], "py", 1)
        high_density = from_behind(density[:, :, :side], "py", -1)
        owner = place_first * size_second + jnp.arange(size_second, dtype=jnp.int32)
        wanted = (place_second - jnp.arange(size_second, dtype=jnp.int32)) % size_second
        anchor = anchors[:, owner * per_device + wanted]
        x = jnp.clip(anchor[0] - place_first * first_rows, 0, first_rows - REG)
        y = jnp.clip(anchor[1] - place_second * second_rows, 0, second_rows - REG)
        columns = (anchor[2][:, None] - 1 + jnp.arange(PATCH_Z, dtype=jnp.int32)) % NR
        pick = (jnp.arange(NR, dtype=jnp.int32)[None, :, None] == columns[:, None, :]).astype(F32)
        slots = device * per_device + positions
        below, above = near[0][slots], near[1][slots]
        flags = jnp.stack(
            [
                positions < counts[device],
                below >= 0,
                above >= 0,
                near[1][jnp.maximum(below, 0)] >= 0,
                near[0][jnp.maximum(above, 0)] >= 0,
            ]
        ).astype(jnp.int32)
        return low_density, high_density, x, y, pick, flags

    held, (low_density, high_density, x, y, pick, flags) = poisson(
        root_density, ((subgrid_density, slot_anchor, slot_count, neighbour), early)
    )
    coarse_potential = jnp.transpose(held, (1, 0, 2))
    padded = extended(extended(held, "px", 1, 1), "py", 0, 2)
    cuts = jnp.stack(
        [
            lax.dynamic_slice(padded, (y[t], x[t], 0), (PATCH_Y, PATCH_X, NR))
            for t in range(size_second)
        ]
    )
    patches = jnp.einsum("tyxn,tnz->txyz", cuts, pick, precision=HIGHEST)
    patches = patches.reshape(size_second, -1)
    arrived = lax.all_to_all(
        patches, "py", split_axis=0, concat_axis=0, tiled=True
    )
    patch = arrived[(place_second + positions) % size_second]
    patch = patch.reshape(per_device, PATCH_X, PATCH_Y * PATCH_Z)
    patch = jnp.pad(
        patch, ((0, 0), (0, 16 - PATCH_X), (0, 128 - PATCH_Y * PATCH_Z))
    )
    x_table, yz_table = patch_tables()
    slot_spec = lambda width: pl.BlockSpec((1, CELLS, width), lambda s: (s, 0, 0))
    vel_spec = pl.BlockSpec((3, 1, CELLS, inner), lambda s: (0, s, 0, 0))
    potential, kicked = pl.pallas_call(
        subgrid_kernel,
        grid=(per_device,),
        in_specs=[
            pl.BlockSpec(memory_space=pltpu.SMEM),
            pl.BlockSpec((1, 16, 128), lambda s: (s, 0, 0)),
            pl.BlockSpec(x_table.shape, lambda s: (0, 0)),
            pl.BlockSpec(yz_table.shape, lambda s: (0, 0)),
            slot_spec(inner),
            slot_spec(side),
            slot_spec(side),
            vel_spec,
        ],
        out_specs=[slot_spec(inner), vel_spec],
        out_shape=[
            jax.ShapeDtypeStruct(subgrid_density.shape, F32),
            jax.ShapeDtypeStruct(velocity.shape, F32),
        ],
        compiler_params=pltpu.CompilerParams(
            dimension_semantics=("arbitrary",), vmem_limit_bytes=60 * 1024 * 1024
        ),
    )(
        flags,
        patch,
        jnp.asarray(x_table),
        jnp.asarray(yz_table),
        subgrid_density,
        low_density,
        high_density,
        velocity,
    )
    return (coarse_potential, potential, kicked)


def solution(mesh):
    return jax.shard_map(
        local,
        mesh=mesh,
        in_specs=(
            P("px", "py", None),
            P(("px", "py"), None, None),
            P(None, ("px", "py"), None, None),
            P(),
            P(),
            P(),
        ),
        out_specs=(
            P("px", "py", None),
            P(("px", "py"), None, None),
            P(None, ("px", "py"), None, None),
        ),
        check_vma=False,
    )
```

profile of v0, /device:TPU:0, one launch (start us, length us, event | category | flops | bytes accessed | tf_op | source)
XLA Modules:
  0.0 400.9 jit_solution(14443892376528291641)
XLA Ops:
  0.6 5.3 %copy.110 = f32[96,48,384]{2,0,1:T(8,128)S(1)} copy(f32[96,48,384]{2,1,0:T(8,128)} %param.12) | data formatting | bytes 14155776 | tf_op args[0]
  5.9 83.1 %all_to_all.46 = f32[48,96,384]{2,1,0:T(8,128)S(1)} all-to-all(f32[48,96,384]{2,1,0:T(8,128)S(1)} %bitcast.116), channel_id=1, replica_groups=mesh['px'=4,'py'=8] {'px'}, dimensions={0} | all-to-all | bytes 14155776 | tf_op jit(solution)/shard_map/all_to_all | solution.py:245
  89.0 0.6 copy.68
  89.6 0.5 copy-done.2
  90.1 6.1 %fusion.23 = f32[384,12,384]{2,0,1:T(8,128)S(1)} fusion(f32[384,384,1]{1,0,2:T(8,128)S(1)} %copy-done.2, f32[12,384,384]{2,1,0:T(8,128)S(1)} %bitcast.113), kind=kOutput, calls=%fused_computation.83 | convolution fusion | flops 4076863488 | bytes 14745600 | tf_op jit(solution)/shard_map/yxz,cz->yxc/dot_general | solution.py:248
  96.2 6.2 %fusion.4.f_ref = f32[12,384,384]{2,1,0:T(8,128)S(1)} fusion(f32[384,384,1]{1,0,2:T(8,128)S(1)} %copy-done.2, f32[384,12,384]{2,0,1:T(8,128)S(1)} %fusion.23), kind=kOutput, calls=%fused_computation.13 | convolution fusion | flops 4076863488 | bytes 14745600 | tf_op jit(solution)/shard_map/yxc,ax->yac/dot_general | solution.py:249
  102.4 3.0 copy-done.1
  105.4 0.2 slice_reduce_fusion
  105.6 7.4 %shard_map.139 = f32[2,384,384]{2,1,0:T(8,128)} custom-call(f32[12,384,384]{2,1,0:T(8,128)} %copy-done.1, f32[384,1]{1,0:T(8,128)} %constant.83.clone.eb_ref, f32[1,384]{1,0:T(1,128)} %constant.84.clone.ec_ref.refs_2_), custom_call_target="tpu_custom_call" | custom-call | tf_op jit(solution)/shard_map/pallas_call | solution.py:261
  112.9 2.2 copy.70
  115.1 0.2 copy.71
  115.3 0.7 copy.72
  116.1 1.3 pad_maximum_fusion.1
  117.4 5.1 %all-to-all-start.1 = ((f32[32,32,384]{2,1,0:T(8,128)}), f32[32,32,384]{2,1,0:T(8,128)S(1)}, u32[]{:S(2)}, u32[]{:S(2)}) async-start(f32[32,32,384]{2,1,0:T(8,128)} %pad_maximum_fusion.1), calls=%async_computation.1 | async-start | bytes 3145728 | tf_op jit(solution)/shard_map/all_to_all | solution.py:279
  122.5 1.3 constant_dynamic-slice_fusion.8.refs_1_
  123.9 37.4 %all-to-all-done.1.refs_0_ = f32[32,32,384]{2,1,0:T(8,128)S(1)} async-done(((f32[32,32,384]{2,1,0:T(8,128)}), f32[32,32,384]{2,1,0:T(8,128)S(1)}, u32[]{:S(2)}, u32[]{:S(2)}) %all-to-all-start.1) | async-done | bytes 1572896 | tf_op jit(solution)/shard_map/all_to_all | solution.py:279
  161.2 1.1 copy-done.3
  162.4 2.9 shard_map.140
  165.3 2.8 all-to-all-start.2
  168.1 0.6 gather_fusion.1
  168.8 0.6 gather_fusion.2
  169.4 0.6 gather_fusion.3
  170.1 0.6 gather_fusion.4
  170.7 0.1 copy.75
  170.9 1.0 fusion.19
  171.9 3.6 collective-permute-start
  175.5 1.3 collective-permute-start.1
  176.8 0.6 dynamic_slice.34
  177.4 0.6 gather_fusion
  177.9 0.2 add_reduce_fusion
  178.2 0.1 fusion.8
  178.3 0.7 iota_compare_fusion.1
  179.0 0.6 convert_element_type.11.flag_ref
  179.6 0.9 slice.130
  180.6 0.1 mul.51
  180.7 0.9 multiply_reduce_fusion
  181.6 16.8 %all-to-all-done.2 = f32[32,24,384]{2,1,0:T(8,128)S(1)} async-done(((f32[32,24,384]{2,1,0:T(8,128)}), f32[32,24,384]{2,1,0:T(8,128)S(1)}, u32[]{:S(2)}, u32[]{:S(2)}) %all-to-all-start.2) | async-done | bytes 1179680 | tf_op jit(solution)/shard_map/all_to_all | solution.py:285
  198.4 0.2 copy.73
  198.6 0.9 copy.74
  199.6 1.1 copy.77.carry_ref
  200.7 0.7 broadcast_in_dim.5.zero_ref
  201.4 9.4 %shard_map.141 = f32[12,384,384]{2,1,0:T(8,128)} custom-call(f32[12,384,384]{2,1,0:T(8,128)} %copy-done.1, f32[2,384,384]{2,1,0:T(8,128)} %copy.77.carry_ref, f32[384,1]{1,0:T(8,128)} %constant.83.clone.eb_ref, f32[1,384]{1,0:T(1,128)} %constant.84.clone.ec_ref.refs_2_, f32[12,384]{1,0:T(8,128)} %broadcast_in_dim.5.zero_ref), custom_call_target="tpu_custom_call" | custom-call | tf_op jit(solution)/shard_map/pallas_call | solution.py:295
  210.8 9.2 %fusion.24 = f32[12,384,384]{2,1,0:T(8,128)S(1)} fusion(f32[12,384,384]{2,1,0:T(8,128)} %shard_map.141, f32[384,384,1]{1,0,2:T(8,128)S(1)} %copy-done.2), kind=kOutput, calls=%fused_computation.84 | convolution fusion | flops 4076863488 | bytes 14745600 | tf_op jit(solution)/shard_map/yac,ax->yxc/dot_general | solution.py:303
  220.0 7.8 %fusion = f32[12,384,384]{2,1,0:T(8,128)S(1)} fusion(f32[384,384,1]{1,0,2:T(8,128)S(1)} %copy-done.2, f32[12,384,384]{2,1,0:T(8,128)S(1)} %fusion.24), kind=kOutput, calls=%fused_computation.7 | convolution fusion | flops 4076863488 | bytes 14745600 | tf_op jit(solution)/shard_map/yxc,cz->yxz/dot_general | solution.py:304
  227.8 0.6 copy.109
  228.3 81.9 %all_to_all.47 = f32[4,12,96,384]{3,2,1,0:T(8,128)S(1)} all-to-all(f32[4,12,96,384]{3,2,1,0:T(8,128)S(1)} %bitcast.115), channel_id=1, replica_groups=mesh['px'=4,'py'=8] {'px'}, dimensions={0} | all-to-all | bytes 14155776 | tf_op jit(solution)/shard_map/all_to_all | solution.py:306
  310.2 0.1 fusion.18
  310.4 1.7 collective-permute-start.3
  312.1 2.1 collective-permute-done.2
  314.3 0.8 collective-permute-start.4
  315.1 4.0 collective-permute-start.5
  319.1 0.7 fusion.21
  322.3 0.7 fusion.22
  350.8 4.6 %pad_maximum_fusion = f32[52,98,384]{2,1,0:T(8,128)S(1)} fusion(f32[2,98,384]{2,1,0:T(8,128)S(1)} %collective-permute-done.5, f32[48,1,384]{2,1,0:T(1,128)S(1)} %collective-permute-done.3, f32[48,96,384]{2,1,0:T(8,128)} %bitcast.110, f32[48,1,384]{2,1,0:T(1,128)S(1)} %collective-permute-done.2, f32[2,98,384]{2,1,0:T(8,128)S(1)} %collective-permute-done.4), kind=kLoop, calls=%fused_computation.6 | loop fusion | flops 7827456 | bytes 15654912 | tf_op jit(solution)/shard_map/concatenate | solution.py:102
  355.4 0.4 constant_dynamic-slice_fusion
  356.3 9.2 %convolution_bitcast_fusion = f32[8,10,12,10]{2,3,1,0:T(8,128)S(1)} fusion(f32[8,12,10,384]{3,1,2,0:T(8,128)S(1)} %bitcast_dynamic-update-slice_fusion, f32[8,384,10]{1,2,0:T(8,128)S(1)} %fusion.8), kind=kOutput, calls=%fused_computation.15 | convolution fusion | flops 44236800 | bytes 1635840 | tf_op jit(solution)/shard_map/tyxn,tnz->txyz/dot_general | solution.py:355
  365.5 0.6 copy.89
  366.1 0.9 all_to_all.40
  367.1 3.6 all-to-all-start.4
  370.6 10.1 %copy.91 = f32[96,48,384]{2,1,0:T(8,128)} copy(f32[96,48,384]{2,0,1:T(8,128)} %bitcast.111) | data formatting | bytes 14155776
  380.7 0.6 gather_fusion.5
  381.3 0.1 reshape.270
  381.4 0.6 pad.9.patch_ref
  382.0 18.6 %shard_map.142 = (f32[8,32,1024]{2,1,0:T(8,128)}, f32[3,8,32,1024]{3,2,1,0:T(8,128)}) custom-call(s32[5,8]{1,0:T(8,128)} %convert_element_type.11.flag_ref, f32[8,16,128]{2,1,0:T(8,128)} %pad.9.patch_ref, f32[40,16]{1,0:T(8,128)} %constant.86.clone.xt_ref, f32[128,3840]{1,0:T(8,128)} %constant.87.clone.yz_ref, f32[8,32,1024]{2,1,0:T(8,128)} %mid_ref.1, ...), custom_call_target="tpu_custom_call" | custom-call | tf_op jit(solution)/shard_map/pallas_call | solution.py:368
  (50 shorter events, 0.9 us)
Async XLA Ops:
  89.0 1.1 copy-start.2
  102.4 3.0 copy-start.1
  117.4 43.9 %all-to-all-start.1 = ((f32[32,32,384]{2,1,0:T(8,128)}), f32[32,32,384]{2,1,0:T(8,128)S(1)}, u32[]{:S(2)}, u32[]{:S(2)}) async-start(f32[32,32,384]{2,1,0:T(8,128)} %pad_maximum_fusion.1), calls=%async_computation.1 | async-start | bytes 3145728 | tf_op jit(solution)/shard_map/all_to_all | solution.py:279
  122.4 45.6 %copy-start.7 = (s32[2,256]{1,0:T(2,128)S(1)}, s32[2,256]{1,0:T(2,128)}, u32[]{:S(2)}) copy-start(s32[2,256]{1,0:T(2,128)} %param.17) | copy-start | bytes 6148
  123.8 46.9 %copy-start.6 = (s32[3,256]{1,0:T(4,128)S(1)}, s32[3,256]{1,0:T(4,128)}, u32[]{:S(2)}) copy-start(s32[3,256]{1,0:T(4,128)} %param.15) | copy-start | bytes 9220
  161.2 1.1 copy-start.3
  165.3 11.5 %copy-start.8 = (s32[32]{0:T(128)S(1)}, s32[32]{0:T(128)}, u32[]{:S(2)}) copy-start(s32[32]{0:T(128)} %param.16) | copy-start | bytes 388
  165.3 33.1 %all-to-all-start.2 = ((f32[32,24,384]{2,1,0:T(8,128)}), f32[32,24,384]{2,1,0:T(8,128)S(1)}, u32[]{:S(2)}, u32[]{:S(2)}) async-start(f32[32,24,384]{2,1,0:T(8,128)} %shard_map.140), calls=%async_computation.2 | async-start | bytes 2359296 | tf_op jit(solution)/shard_map/all_to_all | solution.py:285
  171.9 27.7 %collective-permute-start = (f32[8,32,128]{2,1,0:T(8,128)S(1)}, f32[8,32,128]{2,1,0:T(8,128)S(1)}, u32[]{:S(2)}, u32[]{:S(2)}) collective-permute-start(f32[8,32,128]{2,1,0:T(8,128)S(1)} %get-tuple-element.56), channel_id=1, source_target_pairs={{0,1},{1,2},{2,3},{3,4},{4,5},{5,6},{6,7},{8,9},{9,10},{10,11},{11... | collective-permute-start | bytes 393224 | tf_op jit(solution)/shard_map/ppermute | solution.py:91
  175.5 24.1 %collective-permute-start.1 = (f32[8,32,128]{2,1,0:T(8,128)S(1)}, f32[8,32,128]{2,1,0:T(8,128)S(1)}, u32[]{:S(2)}, u32[]{:S(2)}) collective-permute-start(f32[8,32,128]{2,1,0:T(8,128)S(1)} %get-tuple-element.55), channel_id=1, source_target_pairs={{1,0},{2,1},{3,2},{4,3},{5,4},{6,5},{7,6},{9,8},{10,9},{11,10},{12... | collective-permute-start | bytes 393224 | tf_op jit(solution)/shard_map/ppermute | solution.py:91
  199.6 11.2 %copy-start.4 = (f32[8,32,128]{2,1,0:T(8,128)}, f32[8,32,128]{2,1,0:T(8,128)S(1)}, u32[]{:S(2)}) copy-start(f32[8,32,128]{2,1,0:T(8,128)S(1)} %collective-permute-done.low_ref) | copy-start | bytes 393220
  199.6 11.2 %copy-start.5 = (f32[8,32,128]{2,1,0:T(8,128)}, f32[8,32,128]{2,1,0:T(8,128)S(1)}, u32[]{:S(2)}) copy-start(f32[8,32,128]{2,1,0:T(8,128)S(1)} %collective-permute-done.1.high_ref) | copy-start | bytes 393220
  310.2 4.1 %copy-start = (f32[4,12,96,384]{3,2,1,0:T(8,128)}, f32[4,12,96,384]{3,2,1,0:T(8,128)S(1)}, u32[]{:S(2)}) copy-start(f32[4,12,96,384]{3,2,1,0:T(8,128)S(1)} %all_to_all.47) | copy-start | bytes 21233668
  310.3 3.9 collective-permute-start.2
  310.4 3.9 collective-permute-start.3
  314.3 36.4 %collective-permute-start.4 = (f32[2,98,384]{2,1,0:T(8,128)S(1)}, f32[2,98,384]{2,1,0:T(8,128)S(1)}, u32[]{:S(2)}, u32[]{:S(2)}) collective-permute-start(f32[2,98,384]{2,1,0:T(8,128)S(1)} %get-tuple-element.51), channel_id=1, source_target_pairs={{0,1},{1,2},{2,3},{3,4},{4,5},{5,6},{6,7},{7,0},{8,9},{9,10},{10,1... | collective-permute-start | bytes 903176 | tf_op jit(solution)/shard_map/ppermute | solution.py:98
  315.1 35.7 %collective-permute-start.5 = (f32[2,98,384]{2,1,0:T(8,128)S(1)}, f32[2,98,384]{2,1,0:T(8,128)S(1)}, u32[]{:S(2)}, u32[]{:S(2)}) collective-permute-start(f32[2,98,384]{2,1,0:T(8,128)S(1)} %get-tuple-element.52), channel_id=1, source_target_pairs={{1,0},{2,1},{3,2},{4,3},{5,4},{6,5},{7,6},{0,7},{9,8},{10,9},{11,1... | collective-permute-start | bytes 903176 | tf_op jit(solution)/shard_map/ppermute | solution.py:101
  367.1 13.6 %all-to-all-start.4 = ((f32[8,1,1200]{2,1,0:T(1,128)}), f32[8,1,1200]{2,1,0:T(1,128)S(1)}, u32[]{:S(2)}, u32[]{:S(2)}) async-start(f32[8,1,1200]{2,1,0:T(1,128)} %all_to_all.40), calls=%async_computation.4 | async-start | bytes 81920 | tf_op jit(solution)/shard_map/all_to_all | solution.py:357
where the time goes:
time: 405 us; the launch traced here: 401 us
  blocking collectives  165 us (41%)
  waiting for transfers between devices  56.4 us (14%)
  local copies, waits for them, and re-layouts  39.7 us (10%)
  matrix products  38.5 us (10%)
  Pallas kernels  38.3 us (9%)
  between operations  31.6 us (8%)
  starting transfers between devices  22.8 us (6%)
  other arithmetic  8.55 us (2%)
    all_to_all x1, blocking collectives, poisson(): lax.all_to_all(jnp.transpose(root_density, (1, 0, 2)), 'px', split_axis=0...  83.1 us
    all_to_all x1, blocking collectives, poisson(): u = lax.all_to_all(u, 'px', split_axis=0, concat_axis=0, tiled=True)  81.9 us
    all_to_all x1, waiting for transfers between devices, poisson(): lax.all_to_all(sent, ('px', 'py'), split_axis=0, concat_axis=0, tiled=True)  37.4 us
    unnamed x28, local copies, waits for them, and re-layouts  20.4 us
    pallas_call x1, Pallas kernels, local(): pl.pallas_call(subgrid_kernel, grid=(per_device,), in_specs=[pl.BlockSpec...  18.6 us
    all_to_all x1, waiting for transfers between devices, poisson(): lax.all_to_all(carries, ('px', 'py'), split_axis=0, concat_axis=0, tiled=...  16.8 us
    pallas_call x1, Pallas kernels, poisson(): pl.pallas_call(solve_kernel, grid=(grid,), in_specs=[f_spec, pair_spec, e...  9.4 us
    dot_general x1, matrix products, local(): patches = jnp.einsum('tyxn,tnz->txyz', cuts, pick, precision=HIGHEST)  9.21 us
  transfers between devices with their start and end apart: 9, of which 3 were waited for; matrix products, arithmetic and copies ran while one was open for 6% of the time, Pallas kernels for 0%

commit v1 on v0

--- a/solution.py
+++ b/solution.py
@@ -35,11 +35,27 @@
     return np.stack(rows)
 
 
-def pseudo_inverse(length):
-    basis = fourier_basis(length)
-    eig = -4 * np.sin(np.pi * np.arange(length) / length) ** 2
-    scale = np.where(np.arange(length) == 0, 0.0, 1 / np.where(eig == 0, -1.0, eig))
-    return (basis.T * scale) @ basis
+def strip_basis(cells):
+    place = np.arange(cells) - (cells - 1) / 2
+    mode = 2 * np.arange(cells // 2) + 1
+    angle = np.pi * mode[:, None] * place[None, :] / cells
+    basis = np.concatenate([np.cos(angle), np.sin(angle)]) * np.sqrt(2 / cells)
+    eig = 4 * np.sin(np.pi * mode / (2 * cells)) ** 2
+    return basis, np.concatenate([eig, eig])
+
+
+def strip_coupling(count, rows):
+    basis = fourier_basis(count)
+    turn = np.zeros((count, count))
+    theta = 2 * np.pi * np.arange(count) / count
+    for k in range(1, (count + 1) // 2):
+        turn[k, count - k] = np.sin(theta[k])
+        turn[count - k, k] = -np.sin(theta[k])
+    wide = lambda matrix: np.kron(matrix, np.eye(rows))
+    mixes = np.stack([wide(basis), wide(turn @ basis), wide(basis.T)])
+    half_sine = np.sin(theta / 2) ** 2
+    factors = np.stack([half_sine, 4 * (1 - half_sine)])
+    return mixes, np.repeat(factors, rows, axis=1)[:, :, None]
 
 
 def axis_weights(cells, first, count):
@@ -102,68 +118,362 @@
     return jnp.concatenate([low, block, high], axis=dim)
 
 
-def decay(length, eig_first, eig_second):
-    delta = -(eig_first + eig_second)
-    delta = jnp.where(delta <= 0.0, 1.0, delta)
-    q = 0.5 * delta + jnp.sqrt(delta + 0.25 * delta * delta)
-    return 1.0 / (1.0 + q)
-
-
-def moments_kernel(f_ref, eb_ref, ec_ref, out_ref):
-    rows = f_ref.shape[0]
-    r = decay(NR, eb_ref[...], ec_ref[...])
-    up = f_ref[0]
-    down = f_ref[rows - 1]
-    for i in range(1, rows):
-        up = r * up + f_ref[i]
-        down = r * down + f_ref[rows - 1 - i]
-    out_ref[0] = up
-    out_ref[1] = down
-
-
-def carry_kernel(rows, order, mom_ref, eb_ref, ec_ref, out_ref):
-    blocks = mom_ref.shape[0]
-    band = out_ref.shape[1] // 2
-    r = decay(NR, eb_ref[...], ec_ref[...])
-    ratio = r
-    for _ in range(rows - 1):
-        ratio = ratio * r
-    total = jnp.ones_like(ratio)
-    up = jnp.zeros_like(ratio)
-    down = jnp.zeros_like(ratio)
-    for k in range(blocks):
-        total = total * ratio
-        up = ratio * up + mom_ref[order[k], :band]
-        down = ratio * down + mom_ref[order[blocks - 1 - k], band : 2 * band]
-    norm = 1.0 / (1.0 - total)
-    up = up * norm
-    down = down * norm
-    for k in range(blocks):
-        out_ref[order[k], :band] = up
-        up = ratio * up + mom_ref[order[k], :band]
-        other = order[blocks - 1 - k]
-        out_ref[other, band : 2 * band] = down
-        down = ratio * down + mom_ref[other, band : 2 * band]
-
-
-def solve_kernel(f_ref, carry_ref, eb_ref, ec_ref, zero_ref, out_ref):
-    rows = f_ref.shape[0]
-    r = decay(NR, eb_ref[...], ec_ref[...])
-    scale = -r / ((1.0 - r) * (1.0 + r))
-    tile = f_ref.shape[1]
-    first = lax.broadcasted_iota(jnp.int32, r.shape, 0) + pl.program_id(0) * tile
-    second = lax.broadcasted_iota(jnp.int32, r.shape, 1)
-    zero_mode = (first == 0) & (second == 0)
-    up = carry_ref[0]
-    for i in range(rows):
-        up = r * up + f_ref[i]
-        out_ref[i] = up
-    down = carry_ref[1]
-    for i in range(rows - 1, -1, -1):
-        down = r * down
-        value = (out_ref[i] + down) * scale
-        out_ref[i] = jnp.where(zero_mode, zero_ref[i][None, :], value)
-        down = down + f_ref[i]
+def decay(delta):
+    return 1.0 / (1.0 + 0.5 * delta + jnp.sqrt(delta + 0.25 * delta * delta))
+
+
+def power(value, exponent):
+    result = None
+    while exponent:
+        if exponent & 1:
+            result = value if result is None else result * value
+        exponent >>= 1
+        if exponent:
+            value = value * value
+    return result
+
+
+def grid_kernel(
+    sizes,
+    f_ref,
+    eig_b_ref,
+    eig_ref,
+    own_ref,
+    vec_ref,
+    basis_ref,
+    mix_ref,
+    angle_ref,
+    out_ref,
+    held,
+    lines,
+    sent,
+    got,
+    answer,
+    back,
+    mom_one,
+    mom_two,
+    part,
+    table,
+    weight,
+    send_one,
+    recv_one,
+    send_two,
+    recv_two,
+    send_line,
+    recv_line,
+    send_back,
+    recv_back,
+    self_sem,
+):
+    count_first, count_second, owners = sizes
+    devices = count_first * count_second
+    rows, strip, wave = f_ref.shape
+    groups = strip // 8
+    half = strip // 2
+    chunk = sent.shape[0] // owners
+    width = lines.shape[0]
+    mesh = pl.DeviceIdType.MESH
+    place_first = lax.axis_index("px")
+    place_second = lax.axis_index("py")
+    me = place_first * count_second + place_second
+    barrier = pltpu.get_barrier_semaphore()
+
+    def greet(step, carry):
+        other = lax.rem(me + step, devices)
+        pl.semaphore_signal(
+            barrier,
+            inc=1,
+            device_id=(other // count_second, lax.rem(other, count_second)),
+            device_id_type=mesh,
+        )
+        return carry
+
+    lax.fori_loop(1, devices, greet, 0)
+
+    def split(value):
+        return tuple(value[8 * g : 8 * g + 8] for g in range(groups))
+
+    r_all = decay(eig_b_ref[...] + eig_ref[...])
+    scale_all = -r_all / ((1.0 - r_all) * (1.0 + r_all))
+    ratio = power(r_all, rows)
+    norm = 1.0 / (1.0 - power(ratio, count_first))
+    weight[0] = r_all
+    weight[1] = scale_all
+    weight[2] = 2.0 * vec_ref[0] * scale_all
+    weight[3] = -2.0 * vec_ref[1] * scale_all
+    r = split(r_all)
+    zeros = tuple(jnp.zeros((8, wave), F32) for _ in range(groups))
+    even_groups = [g for g in range(groups) if 8 * g < half]
+    odd_groups = [g for g in range(groups) if 8 * g + 8 > half]
+
+    table[...] = jnp.zeros_like(table)
+    for i in range(count_first):
+        block = basis_ref[i * rows : (i + 1) * rows, :]
+        table[i, :rows, :wave] = block
+        table[i, rows : 2 * rows, wave:] = block
+
+    def row_of(ref, i):
+        return tuple(ref[i, 8 * g : 8 * g + 8, :] for g in range(groups))
+
+    def up_first(i, carry):
+        up, total = carry
+        f = row_of(f_ref, i)
+        up = tuple(r[g] * up[g] + f[g] for g in range(groups))
+        return up, tuple(total[g] + f[g] for g in range(groups))
+
+    def down_first(i, down):
+        f = row_of(f_ref, rows - 1 - i)
+        return tuple(r[g] * down[g] + f[g] for g in range(groups))
+
+    up, total = lax.fori_loop(0, rows, up_first, (zeros, zeros))
+    down = lax.fori_loop(0, rows, down_first, zeros)
+    for g in range(groups):
+        mom_one[0, 0, 8 * g : 8 * g + 8, :] = up[g]
+        mom_one[0, 1, 8 * g : 8 * g + 8, :] = down[g]
+    whole = jnp.concatenate(total, axis=0)
+
+    def shares(buffer, send, recv):
+        return [
+            pltpu.make_async_remote_copy(
+                src_ref=buffer.at[0],
+                dst_ref=buffer.at[d],
+                send_sem=send.at[d],
+                recv_sem=recv.at[d],
+                device_id=(lax.rem(place_first + d, count_first), place_second),
+                device_id_type=mesh,
+            )
+            for d in range(1, count_first)
+        ]
+
+    def carries(buffer):
+        up = jnp.zeros((strip, wave), F32)
+        down = jnp.zeros((strip, wave), F32)
+        for d in [0] + list(range(count_first - 1, 0, -1)):
+            up = ratio * up + buffer[d, 0]
+        for d in range(count_first):
+            down = ratio * down + buffer[d, 1]
+        return split(up * norm), split(down * norm)
+
+    pl.semaphore_wait(barrier, devices - 1)
+    first = shares(mom_one, send_one, recv_one)
+    for copy in first:
+        copy.start()
+    lines[2 * rows :, :] = jnp.zeros((width - 2 * rows, wave), F32)
+    lines[2 * rows : 2 * rows + 1, :] = jnp.sum(vec_ref[2] * whole, axis=0, keepdims=True)
+    lines[2 * rows + 1 : 2 * rows + 2, :] = jnp.sum(vec_ref[3] * whole, axis=0, keepdims=True)
+    for copy in first:
+        copy.wait()
+    carry_up, carry_down = carries(mom_one)
+
+    def weighed(which, members, value):
+        total = None
+        for g in members:
+            term = weight[which, 8 * g : 8 * g + 8, :] * value[g]
+            total = term if total is None else total + term
+        return total
+
+    def up_lines(i, up):
+        f = row_of(f_ref, i)
+        up = tuple(r[g] * up[g] + f[g] for g in range(groups))
+        part[0, i] = weighed(2, even_groups, up)
+        part[1, i] = weighed(3, odd_groups, up)
+        return up
+
+    def down_lines(step, down):
+        i = rows - 1 - step
+        f = row_of(f_ref, i)
+        down = tuple(r[g] * down[g] for g in range(groups))
+        part[0, i] += weighed(2, even_groups, down)
+        part[1, i] += weighed(3, odd_groups, down)
+        return tuple(down[g] + f[g] for g in range(groups))
+
+    lax.fori_loop(0, rows, up_lines, carry_up)
+    lax.fori_loop(0, rows, down_lines, carry_down)
+    lines[:rows, :] = jnp.sum(part[0], axis=1)
+    lines[rows : 2 * rows, :] = jnp.sum(part[1], axis=1)
+    sent[...] = lines[...].T
+
+    def line_copy(o):
+        return pltpu.make_async_remote_copy(
+            src_ref=sent.at[pl.ds(o * chunk, chunk)],
+            dst_ref=got.at[me],
+            send_sem=send_line.at[o],
+            recv_sem=recv_line.at[me],
+            device_id=(o // count_second, lax.rem(o, count_second)),
+            device_id_type=mesh,
+        )
+
+    def line_from(d):
+        return pltpu.make_async_remote_copy(
+            src_ref=sent.at[pl.ds(0, chunk)],
+            dst_ref=got.at[d],
+            send_sem=self_sem.at[1],
+            recv_sem=recv_line.at[d],
+            device_id=(d // count_second, lax.rem(d, count_second)),
+            device_id_type=mesh,
+        )
+
+    def back_copy(d):
+        return pltpu.make_async_remote_copy(
+            src_ref=answer.at[d],
+            dst_ref=back.at[pl.ds(me * chunk, chunk)],
+            send_sem=send_back.at[d],
+            recv_sem=recv_back.at[me],
+            device_id=(d // count_second, lax.rem(d, count_second)),
+            device_id_type=mesh,
+        )
+
+    def back_from(o):
+        return pltpu.make_async_remote_copy(
+            src_ref=answer.at[0],
+            dst_ref=back.at[pl.ds(o * chunk, chunk)],
+            send_sem=self_sem.at[1],
+            recv_sem=recv_back.at[o],
+            device_id=(o // count_second, lax.rem(o, count_second)),
+            device_id_type=mesh,
+        )
+
+    def over(count, action):
+        def body(k, carry):
+            @pl.when(k != me)
+            def _():
+                action(k)
+
+            return carry
+
+        lax.fori_loop(0, count, body, 0)
+
+    over(owners, lambda o: line_copy(o).start())
+
+    @pl.when(me < owners)
+    def _():
+        own = pltpu.make_async_copy(
+            sent.at[pl.ds(me * chunk, chunk)], got.at[me], self_sem.at[0]
+        )
+        own.start()
+        over(devices, lambda d: line_from(d).wait_recv())
+        own.wait()
+        modes = None
+        for i in range(count_first):
+            piece = got[i * count_second : (i + 1) * count_second]
+            piece = piece.reshape(count_second * chunk, width)
+            term = jnp.dot(piece, table[i], precision=HIGHEST, preferred_element_type=F32)
+            modes = term if modes is None else modes + term
+        straight = jnp.dot(mix_ref[0], modes, precision=HIGHEST, preferred_element_type=F32)
+        turned = jnp.dot(mix_ref[1], modes, precision=HIGHEST, preferred_element_type=F32)
+        s, t = straight[:, :wave], straight[:, wave:]
+        s_turned, t_turned = turned[:, :wave], turned[:, wave:]
+        own_eig = own_ref[...]
+        lam = own_eig + eig_ref[...]
+        sinh = jnp.sqrt(lam + 0.25 * lam * lam)
+        flat = lam <= 0.0
+        far = power(decay(lam), strip)
+        tanh = (1.0 - far) / (1.0 + far)
+        green = jnp.where(flat, strip / 4.0, tanh / jnp.where(flat, 1.0, 2.0 * sinh))
+        square = tanh * tanh
+        half_sine = angle_ref[0]
+        det = half_sine * (1.0 - square) + square
+        zero = flat & (half_sine <= 0.0)
+        inverse = 1.0 / jnp.where(zero, 1.0, det)
+        gain = angle_ref[1] * green * inverse
+        sums = jnp.sum(got[...], axis=0)
+        lane = lax.broadcasted_iota(jnp.int32, sums.shape, 1)
+        sigma = jnp.sum(jnp.where(lane == 2 * rows, sums, 0.0), axis=1, keepdims=True)
+        lever = jnp.sum(jnp.where(lane == 2 * rows + 1, sums, 0.0), axis=1, keepdims=True)
+        k = np.arange(strip)
+        bow = 0.5 * (k * k - (strip - 1) * k) - strip / 4
+        mean = jnp.where(own_eig[:chunk] <= 0.0, sigma, 0.0) * (1.0 / (wave * wave))
+        gauge = lever - mean * float(wave * count_second * bow.sum())
+        gauge = gauge * float(1.0 / (bow[0] * np.sqrt(wave * count_second)))
+        tall = lambda value: jnp.concatenate([value] * count_second, axis=0)
+        mean, gauge = tall(mean), tall(gauge)
+        new_s = gain * (2.0 + 0.5 * lam) * s - t_turned * inverse
+        new_t = gain * (0.5 * lam) * t - s_turned * inverse
+        new_s = jnp.where(zero, gauge, new_s)
+        new_t = jnp.where(zero, (2.0 / strip) * t, new_t)
+        solved = jnp.concatenate([new_s, new_t], axis=1)
+        solved = jnp.dot(mix_ref[2], solved, precision=HIGHEST, preferred_element_type=F32)
+        wide = lax.broadcasted_iota(jnp.int32, (count_second * chunk, width), 1)
+        for i in range(count_first):
+            piece = lax.dot_general(
+                solved,
+                table[i],
+                (((1,), (1,)), ((), ())),
+                precision=HIGHEST,
+                preferred_element_type=F32,
+            )
+            piece = jnp.where(wide == 2 * rows, mean, piece)
+            answer[i * count_second : (i + 1) * count_second] = piece.reshape(
+                count_second, chunk, width
+            )
+        over(devices, lambda d: back_copy(d).start())
+        kept = pltpu.make_async_copy(
+            answer.at[me], back.at[pl.ds(me * chunk, chunk)], self_sem.at[0]
+        )
+        kept.start()
+        kept.wait()
+
+    over(owners, lambda o: back_from(o).wait_recv())
+    lines[...] = back[...].T
+    mean_term = vec_ref[2] * lines[2 * rows : 2 * rows + 1, :]
+    weight[2] = mean_term
+
+    def up_second(i, up):
+        f = row_of(f_ref, i)
+        line_s = lines[pl.ds(i, 1), :]
+        line_t = lines[pl.ds(rows + i, 1), :]
+        fresh = []
+        for g in range(groups):
+            window = slice(8 * g, 8 * g + 8)
+            value = f[g] - weight[2, window, :]
+            if g in even_groups:
+                value = value - vec_ref[0, window, :] * line_s
+            if g in odd_groups:
+                value = value - vec_ref[1, window, :] * line_t
+            held[i, window, :] = value
+            fresh.append(value)
+        return tuple(r[g] * up[g] + fresh[g] for g in range(groups))
+
+    def down_second(i, down):
+        f = row_of(held, rows - 1 - i)
+        return tuple(r[g] * down[g] + f[g] for g in range(groups))
+
+    up = lax.fori_loop(0, rows, up_second, zeros)
+    down = lax.fori_loop(0, rows, down_second, zeros)
+    for g in range(groups):
+        mom_two[0, 0, 8 * g : 8 * g + 8, :] = up[g]
+        mom_two[0, 1, 8 * g : 8 * g + 8, :] = down[g]
+    second = shares(mom_two, send_two, recv_two)
+    for copy in second:
+        copy.start()
+    over(owners, lambda o: line_copy(o).wait_send())
+
+    @pl.when(me < owners)
+    def _():
+        over(devices, lambda d: back_copy(d).wait_send())
+
+    for copy in second:
+        copy.wait()
+    carry_up, carry_down = carries(mom_two)
+
+    def up_last(i, up):
+        f = row_of(held, i)
+        up = tuple(r[g] * up[g] + f[g] for g in range(groups))
+        for g in range(groups):
+            out_ref[i, 8 * g : 8 * g + 8, :] = up[g]
+        return up
+
+    def down_last(step, down):
+        i = rows - 1 - step
+        f = row_of(held, i)
+        down = tuple(r[g] * down[g] for g in range(groups))
+        for g in range(groups):
+            window = slice(8 * g, 8 * g + 8)
+            out_ref[i, window, :] = (out_ref[i, window, :] + down[g]) * weight[1, window, :]
+        return tuple(down[g] + f[g] for g in range(groups))
+
+    lax.fori_loop(0, rows, up_last, carry_up)
+    lax.fori_loop(0, rows, down_last, carry_down)
 
 
 def subgrid_kernel(
@@ -229,82 +539,82 @@
         kick_ref[q, 0] = jnp.where(live, vel_ref[q, 0] - slope, 0.0)
 
 
-def poisson(root_density, beside_work):
-    size_first = lax.axis_size("px")
-    size_second = lax.axis_size("py")
-    devices = size_first * size_second
-    device = lax.axis_index("px") * size_second + lax.axis_index("py")
-    block = lax.axis_index("py") * size_first + lax.axis_index("px")
-    order = [(k % size_first) * size_second + k // size_first for k in range(devices)]
-    basis = jnp.asarray(fourier_basis(NR), F32)
-    eig = -4.0 * np.sin(np.pi / NR * np.arange(NR)) ** 2
-    eig_first = jnp.asarray(eig[:, None], F32)
-    eig_second = jnp.asarray(eig[None, :], F32)
-    rows = NR // devices
-    band = NR // devices
-    planes = lax.all_to_all(
-        jnp.transpose(root_density, (1, 0, 2)), "px", split_axis=0, concat_axis=1, tiled=True
-    )
-    f = jnp.einsum("yxz,cz->yxc", planes, basis, precision=HIGH)
-    f = jnp.einsum("yxc,ax->yac", f, basis, precision=HIGH)
-    f, beside = lax.optimization_barrier((f, beside_work[0]))
-    beside = beside_work[1](*beside)
-    tile = 48
-    grid = NR // tile
-    f_spec = pl.BlockSpec((rows, tile, NR), lambda t: (0, t, 0))
-    pair_spec = pl.BlockSpec((2, tile, NR), lambda t: (0, t, 0))
-    eb_spec = pl.BlockSpec((tile, 1), lambda t: (t, 0))
-    ec_spec = pl.BlockSpec((1, NR), lambda t: (0, 0))
-    params = pltpu.CompilerParams(
-        dimension_semantics=("arbitrary",), vmem_limit_bytes=60 * 1024 * 1024
-    )
-    moments = pl.pallas_call(
-        moments_kernel,
-        grid=(grid,),
-        in_specs=[f_spec, eb_spec, ec_spec],
-        out_specs=pair_spec,
-        out_shape=jax.ShapeDtypeStruct((2, NR, NR), F32),
-        compiler_params=params,
-    )(f, eig_first, eig_second)
-    column = jnp.pad(f[:, 0, 0], (0, NR - rows))
-    sent = jnp.concatenate(
+def poisson(root_density):
+    count_first = lax.axis_size("px")
+    count_second = lax.axis_size("py")
+    devices = count_first * count_second
+    device = lax.axis_index("px") * count_second + lax.axis_index("py")
+    rows, strip, wave = root_density.shape
+    chunk = next(q for q in range(8, wave + 1, 8) if wave % q == 0 and wave // q <= devices)
+    owners = wave // chunk
+    width = -(-(2 * rows + 2) // 128) * 128
+    basis = fourier_basis(wave)
+    strip_table, strip_eig = strip_basis(strip)
+    eig = 4.0 * np.sin(np.pi / wave * np.arange(wave)) ** 2
+    mixes, angles = strip_coupling(count_second, chunk)
+    cell = np.arange(strip)
+    bow = 0.5 * (cell * cell - (strip - 1) * cell) - strip / 4
+    lower = cell < strip // 2
+    edge = strip_table[:, 0]
+    vectors = np.stack(
         [
-            moments.reshape(2, devices, band, NR).transpose(1, 0, 2, 3).reshape(
-                devices, 2 * band, NR
-            ),
-            jnp.broadcast_to(column[None, None, :], (devices, 8, NR)),
+            np.where(lower, edge, 0.0),
+            np.where(lower, 0.0, edge),
+            strip_table.sum(1),
+            strip_table @ bow,
+        ]
+    )[:, :, None]
+    own = lax.rem(device, owners) * chunk
+    own_eig = lax.dynamic_slice_in_dim(jnp.asarray(eig, F32), own, chunk)
+    own_eig = jnp.tile(own_eig, count_second)[:, None]
+    z_basis = jnp.asarray(basis, F32)
+    y_basis = jnp.asarray(strip_table, F32)
+    f = jnp.einsum("xyz,cz->xyc", root_density, z_basis, precision=HIGH)
+    f = jnp.einsum("xyc,by->xbc", f, y_basis, precision=HIGH)
+    moment = pltpu.VMEM((count_first, 2, strip, wave), F32)
+    dma = pltpu.SemaphoreType.DMA
+    u = pl.pallas_call(
+        lambda *refs: grid_kernel((count_first, count_second, owners), *refs),
+        in_specs=[pl.BlockSpec(memory_space=pltpu.VMEM)] * 8,
+        out_specs=pl.BlockSpec(memory_space=pltpu.VMEM),
+        out_shape=jax.ShapeDtypeStruct((rows, strip, wave), F32),
+        scratch_shapes=[
+            pltpu.VMEM((rows, strip, wave), F32),
+            pltpu.VMEM((width, wave), F32),
+            pltpu.VMEM((wave, width), F32),
+            pltpu.VMEM((devices, chunk, width), F32),
+            pltpu.VMEM((devices, chunk, width), F32),
+            pltpu.VMEM((wave, width), F32),
+            moment,
+            moment,
+            pltpu.VMEM((2, rows, 8, wave), F32),
+            pltpu.VMEM((count_first, width, 2 * wave), F32),
+            pltpu.VMEM((4, strip, wave), F32),
+            dma((count_first,)),
+            dma((count_first,)),
+            dma((count_first,)),
+            dma((count_first,)),
+            dma((owners,)),
+            dma((devices,)),
+            dma((devices,)),
+            dma((owners,)),
+            dma((2,)),
         ],
-        axis=1,
-    )
-    got = lax.all_to_all(sent, ("px", "py"), split_axis=0, concat_axis=0, tiled=True)
-    carries = pl.pallas_call(
-        lambda *refs: carry_kernel(rows, order, *refs),
-        out_shape=jax.ShapeDtypeStruct((devices, 2 * band, NR), F32),
-        compiler_params=pltpu.CompilerParams(vmem_limit_bytes=60 * 1024 * 1024),
-    )(got, lax.dynamic_slice_in_dim(eig_first, device * band, band, 0), eig_second)
-    back = lax.all_to_all(carries, ("px", "py"), split_axis=0, concat_axis=0, tiled=True)
-    back = back.reshape(devices, 2, band, NR).transpose(1, 0, 2, 3).reshape(2, NR, NR)
-    back, beside = lax.optimization_barrier((back, beside))
-    whole_column = got[:, 2 * band, :rows].reshape(size_first, size_second, rows)
-    whole_column = whole_column.transpose(1, 0, 2).reshape(NR)
-    own = lax.dynamic_slice_in_dim(
-        jnp.asarray(pseudo_inverse(NR), F32), block * rows, rows, 0
-    )
-    zero_values = jnp.sum(own * whole_column[None, :], axis=1)
-    zero_wide = jnp.broadcast_to(zero_values[:, None], (rows, NR))
-    u = pl.pallas_call(
-        solve_kernel,
-        grid=(grid,),
-        in_specs=[f_spec, pair_spec, eb_spec, ec_spec, pl.BlockSpec((rows, NR), lambda t: (0, 0))],
-        out_specs=f_spec,
-        out_shape=jax.ShapeDtypeStruct((rows, NR, NR), F32),
-        compiler_params=params,
-    )(f, back, eig_first, eig_second, zero_wide)
-    u = jnp.einsum("yac,ax->yxc", u, basis, precision=HIGH)
-    u = jnp.einsum("yxc,cz->yxz", u, basis, precision=HIGH)
-    u = u.reshape(rows, size_first, NR // size_first, NR).transpose(1, 0, 2, 3)
-    u = lax.all_to_all(u, "px", split_axis=0, concat_axis=0, tiled=True)
-    return u.reshape(size_first * rows, NR // size_first, NR), beside
+        compiler_params=pltpu.CompilerParams(
+            collective_id=1, has_side_effects=True, vmem_limit_bytes=60 * 1024 * 1024
+        ),
+    )(
+        f,
+        jnp.asarray(strip_eig[:, None], F32),
+        jnp.asarray(eig[None, :], F32),
+        own_eig,
+        jnp.asarray(vectors, F32),
+        jnp.asarray(basis.T, F32),
+        jnp.asarray(mixes, F32),
+        jnp.asarray(angles, F32),
+    )
+    u = jnp.einsum("xbc,by->xyc", u, y_basis, precision=HIGH)
+    return jnp.einsum("xyc,cz->xyz", u, z_basis, precision=HIGH)
 
 
 def local(root_density, subgrid_density, velocity, slot_anchor, slot_count, neighbour):
@@ -341,18 +651,18 @@
         ).astype(jnp.int32)
         return low_density, high_density, x, y, pick, flags
 
-    held, (low_density, high_density, x, y, pick, flags) = poisson(
-        root_density, ((subgrid_density, slot_anchor, slot_count, neighbour), early)
-    )
-    coarse_potential = jnp.transpose(held, (1, 0, 2))
-    padded = extended(extended(held, "px", 1, 1), "py", 0, 2)
+    low_density, high_density, x, y, pick, flags = early(
+        subgrid_density, slot_anchor, slot_count, neighbour
+    )
+    coarse_potential = poisson(root_density)
+    padded = extended(extended(coarse_potential, "px", 0, 1), "py", 1, 2)
     cuts = jnp.stack(
         [
-            lax.dynamic_slice(padded, (y[t], x[t], 0), (PATCH_Y, PATCH_X, NR))
+            lax.dynamic_slice(padded, (x[t], y[t], 0), (PATCH_X, PATCH_Y, NR))
             for t in range(size_second)
         ]
     )
-    patches = jnp.einsum("tyxn,tnz->txyz", cuts, pick, precision=HIGHEST)
+    patches = jnp.einsum("txyn,tnz->txyz", cuts, pick, precision=HIGHEST)
     patches = patches.reshape(size_second, -1)
     arrived = lax.all_to_all(
         patches, "py", split_axis=0, concat_axis=0, tiled=True

time: 405 us -> 213 us (0.53)
  blocking collectives: 165 us -> 0 us
  Pallas kernels: 38.3 us -> 88.5 us
  waiting for transfers between devices: 56.4 us -> 19 us
  local copies, waits for them, and re-layouts: 39.7 us -> 13.8 us
  starting transfers between devices: 22.8 us -> 18 us
    all_to_all x2 -> x0, blocking collectives: 165 us -> none  [the longest x1 83.1 us: poisson(): lax.all_to_all(jnp.transpose(root_density, (1, 0, 2)), 'px', split_axis=0...]
    all_to_all x2 -> x0, waiting for transfers between devices: 54.2 us -> none  [the longest x1 37.4 us: poisson(): lax.all_to_all(sent, ('px', 'py'), split_axis=0, concat_axis=0, tiled=True)]
    pallas_call x3 -> x1, Pallas kernels: 19.7 us -> 69.8 us  [poisson(): pl.pallas_call(lambda *refs: grid_kernel((count_first, count_second, owne...]
    unnamed x28 -> x27, local copies, waits for them, and re-layouts: 20.4 us -> 4.68 us
    all_to_all x2 -> x0, starting transfers between devices: 7.84 us -> none  [the longest x1 5.06 us: poisson(): lax.all_to_all(sent, ('px', 'py'), split_axis=0, concat_axis=0, tiled=True)]
    ppermute x2, waiting for transfers between devices: 2.14 us -> 9.94 us  [extended(): lax.ppermute(lax.slice_in_dim(block, block.shape[dim] - width, None, axis...]
    all_to_all x1, waiting for transfers between devices: 0.01 us -> 6.73 us  [local(): lax.all_to_all(patches, 'py', split_axis=0, concat_axis=0, tiled=True)]
    ppermute x2, starting transfers between devices: 0.85 us -> 5.56 us  [extended(): lax.ppermute(lax.slice_in_dim(block, block.shape[dim] - width, None, axis...]
  transfers between devices with their start and end apart: 9 -> 7, of which waited for: 3 -> 3; matrix products, arithmetic and copies ran while one was open for 6% -> 6% of each run, Pallas kernels for 0% -> 0%
where the time goes in v1:
time: 213 us; the launch traced here: 212 us
  Pallas kernels  88.5 us (42%)
  matrix products  36.5 us (17%)
  between operations  31.5 us (15%)
  waiting for transfers between devices  19 us (9%)
  starting transfers between devices  18 us (8%)
  local copies, waits for them, and re-layouts  13.8 us (6%)
  other arithmetic  4.97 us (2%)
    pallas_call x1, Pallas kernels, poisson(): pl.pallas_call(lambda *refs: grid_kernel((count_first, count_second, owne...  69.8 us
    pallas_call x1, Pallas kernels, local(): pl.pallas_call(subgrid_kernel, grid=(per_device,), in_specs=[pl.BlockSpec...  18.6 us
    dot_general x1, matrix products, poisson(): f = jnp.einsum('xyz,cz->xyc', root_density, z_basis, precision=HIGH)  11.8 us
    dot_general x1, matrix products, poisson(): f = jnp.einsum('xyc,by->xbc', f, y_basis, precision=HIGH)  11.8 us
    ppermute x2, waiting for transfers between devices, extended(): lax.ppermute(lax.slice_in_dim(block, block.shape[dim] - width, None, axis...  9.94 us
    all_to_all x1, waiting for transfers between devices, local(): lax.all_to_all(patches, 'py', split_axis=0, concat_axis=0, tiled=True)  6.73 us
    dot_general x1, matrix products, poisson(): return jnp.einsum('xyc,cz->xyz', u, z_basis, precision=HIGH)  6.58 us
    ppermute x2, starting transfers between devices, extended(): lax.ppermute(lax.slice_in_dim(block, block.shape[dim] - width, None, axis...  5.56 us
  transfers between devices with their start and end apart: 7, of which 3 were waited for; matrix products, arithmetic and copies ran while one was open for 6% of the time, Pallas kernels for 0%

profile of v1, /device:TPU:0, one launch (start us, length us, event | category | flops | bytes accessed | tf_op | source)
XLA Modules:
  0.0 212.4 jit_solution(15618042738233330680)
XLA Ops:
  0.6 0.8 dynamic_slice.30
  1.4 0.7 broadcast_in_dim_tile.4.refs_3_
  2.1 0.0 copy-start.5
  2.1 11.8 %fusion.9 = f32[96,48,384]{2,0,1:T(8,128)S(1)} fusion(f32[384,384,1]{1,0,2:T(8,128)} %constant.106, f32[96,48,384]{2,1,0:T(8,128)} %param.17), kind=kOutput, calls=%fused_computation.14 | convolution fusion | flops 4076863488 | bytes 14745600 | tf_op jit(solution)/shard_map/xyz,cz->xyc/dot_general | solution.py:572
  14.0 0.0 copy-done.5
  14.0 11.8 %fusion.6.refs_0_ = f32[96,48,384]{2,1,0:T(8,128)} fusion(f32[48,48,1]{1,0,2:T(8,128)S(1)} %copy-done.5, f32[96,48,384]{2,0,1:T(8,128)S(1)} %fusion.9), kind=kOutput, calls=%fused_computation.13 | convolution fusion | flops 509607936 | bytes 14164992 | tf_op jit(solution)/shard_map/xyc,by->xbc/dot_general | solution.py:573
  25.8 69.8 %shard_map.184 = f32[96,48,384]{2,1,0:T(8,128)} custom-call(f32[96,48,384]{2,1,0:T(8,128)} %fusion.6.refs_0_, f32[48,1]{1,0:T(8,128)} %constant.94.clone.refs_1_, f32[1,384]{1,0:T(1,128)} %constant.95.clone.refs_2_, f32[128,1]{1,0:T(8,128)} %broadcast_in_dim_tile.4.refs_3_, f32[4,48,1]{2,1,0:T(8,128)} %constant.96.clone.refs_4_, ...), custom_call_target="tpu_custom_call" | custom-call | tf_op jit(solution)/shard_map/pallas_call | solution.py:576
  95.6 0.0 copy-start.2
  95.6 5.3 %fusion.30 = f32[96,384,48]{1,2,0:T(8,128)S(1)} fusion(f32[96,48,384]{2,1,0:T(8,128)} %shard_map.184, f32[48,48,1]{1,0,2:T(8,128)S(1)} %copy-done.5), kind=kOutput, calls=%fused_computation.71 | convolution fusion | flops 509607936 | bytes 14164992 | tf_op jit(solution)/shard_map/xbc,by->xyc/dot_general | solution.py:616
  100.9 0.0 copy-done.2
  100.9 0.0 copy-start.6
  100.9 0.0 copy-start.7
  101.0 0.0 copy-start.8
  101.0 6.6 %fusion = f32[96,48,384]{2,1,0:T(8,128)S(1)} fusion(f32[384,384,1]{1,0,2:T(8,128)S(1)} %copy-done.2, f32[96,384,48]{1,2,0:T(8,128)S(1)} %fusion.30), kind=kOutput, calls=%fused_computation.7 | convolution fusion | flops 4076863488 | bytes 14745600 | tf_op jit(solution)/shard_map/xyc,cz->xyz/dot_general | solution.py:617
  107.5 0.0 copy-start
  107.6 3.0 %copy-done = f32[96,48,384]{2,1,0:T(8,128)} copy-done((f32[96,48,384]{2,1,0:T(8,128)}, f32[96,48,384]{2,1,0:T(8,128)S(1)}, u32[]{:S(2)}) %copy-start) | copy-done | bytes 7077912
  110.5 2.9 %collective-permute-start = (f32[1,48,384]{2,1,0:T(8,128)S(1)}, f32[1,48,384]{2,1,0:T(8,128)S(1)}, u32[]{:S(2)}, u32[]{:S(2)}) collective-permute-start(f32[1,48,384]{2,1,0:T(8,128)S(1)} %get-tuple-element.9), channel_id=1, source_target_pairs={{0,8},{8,16},{16,24},{24,0},{1,9},{9,17},{17,25},{25,1},{2,10},{10... | collective-permute-start | bytes 221192 | tf_op jit(solution)/shard_map/ppermute | solution.py:114
  113.4 0.0 collective-permute-start.1
  113.4 1.0 fusion.26
  114.4 3.3 %collective-permute-start.4 = (f32[8,32,128]{2,1,0:T(8,128)S(1)}, f32[8,32,128]{2,1,0:T(8,128)S(1)}, u32[]{:S(2)}, u32[]{:S(2)}) collective-permute-start(f32[8,32,128]{2,1,0:T(8,128)S(1)} %get-tuple-element.12), channel_id=1, source_target_pairs={{0,1},{1,2},{2,3},{3,4},{4,5},{5,6},{6,7},{8,9},{9,10},{10,11},{11... | collective-permute-start | bytes 393224 | tf_op jit(solution)/shard_map/ppermute | solution.py:107
  117.7 1.3 collective-permute-start.5
  119.0 0.0 copy-done.6
  119.0 0.1 copy.28
  119.2 0.6 gather_fusion.4
  119.7 0.2 add_reduce_fusion
  119.9 0.6 fusion.27
  141.0 0.0 copy-done.7
  141.0 0.6 gather_fusion
  141.6 0.6 gather_fusion.1
  142.3 0.6 gather_fusion.2
  143.0 0.6 gather_fusion.3
  143.6 0.0 copy-done.8
  143.6 0.6 dynamic_slice.31
  144.2 0.7 iota_compare_fusion.1
  144.9 0.6 convert_element_type.6.flag_ref
  155.7 0.0 copy-start.1
  155.7 0.0 collective-permute-done
  155.7 0.0 collective-permute-done.1
  155.7 2.0 pad_maximum_fusion.3
  157.7 2.7 %collective-permute-start.2 = (f32[98,2,384]{2,1,0:T(2,128)S(1)}, f32[98,2,384]{2,1,0:T(2,128)S(1)}, u32[]{:S(2)}, u32[]{:S(2)}) collective-permute-start(f32[98,2,384]{2,1,0:T(2,128)S(1)} %get-tuple-element.7), channel_id=1, source_target_pairs={{0,1},{1,2},{2,3},{3,4},{4,5},{5,6},{6,7},{7,0},{8,9},{9,10},{10,1... | collective-permute-start | bytes 903176 | tf_op jit(solution)/shard_map/ppermute | solution.py:114
  160.4 2.9 %collective-permute-start.3 = (f32[98,2,384]{2,1,0:T(2,128)S(1)}, f32[98,2,384]{2,1,0:T(2,128)S(1)}, u32[]{:S(2)}, u32[]{:S(2)}) collective-permute-start(f32[98,2,384]{2,1,0:T(2,128)S(1)} %get-tuple-element.8), channel_id=1, source_target_pairs={{1,0},{2,1},{3,2},{4,3},{5,4},{6,5},{7,6},{0,7},{9,8},{10,9},{11,1... | collective-permute-start | bytes 903176 | tf_op jit(solution)/shard_map/ppermute | solution.py:117
  163.3 0.1 add_select_fusion
  163.4 9.9 %collective-permute-done.2 = f32[98,2,384]{2,1,0:T(2,128)S(1)} collective-permute-done((f32[98,2,384]{2,1,0:T(2,128)S(1)}, f32[98,2,384]{2,1,0:T(2,128)S(1)}, u32[]{:S(2)}, u32[]{:S(2)}) %collective-permute-start.2) | collective-permute-done | bytes 301088 | tf_op jit(solution)/shard_map/ppermute | solution.py:114
  173.4 2.3 %collective-permute-done.3 = f32[98,2,384]{2,1,0:T(2,128)S(1)} collective-permute-done((f32[98,2,384]{2,1,0:T(2,128)S(1)}, f32[98,2,384]{2,1,0:T(2,128)S(1)}, u32[]{:S(2)}, u32[]{:S(2)}) %collective-permute-start.3) | collective-permute-done | bytes 301088 | tf_op jit(solution)/shard_map/ppermute | solution.py:117
  175.7 0.0 copy-done.1
  175.7 1.4 pad_maximum_fusion
  177.4 1.1 fusion.13
  178.5 0.9 all_to_all.11
  179.4 4.9 %all-to-all-start = ((f32[8,1,1200]{2,1,0:T(1,128)}), f32[8,1,1200]{2,1,0:T(1,128)S(1)}, u32[]{:S(2)}, u32[]{:S(2)}) async-start(f32[8,1,1200]{2,1,0:T(1,128)} %all_to_all.11), calls=%async_computation | async-start | bytes 81920 | tf_op jit(solution)/shard_map/all_to_all | solution.py:667
  184.4 6.7 %all-to-all-done = f32[8,1,1200]{2,1,0:T(1,128)S(1)} async-done(((f32[8,1,1200]{2,1,0:T(1,128)}), f32[8,1,1200]{2,1,0:T(1,128)S(1)}, u32[]{:S(2)}, u32[]{:S(2)}) %all-to-all-start) | async-done | bytes 38432 | tf_op jit(solution)/shard_map/all_to_all | solution.py:667
  191.1 0.6 gather_fusion.5
  191.7 0.1 reshape.276
  191.8 0.6 pad.4.patch_ref
  192.4 0.0 collective-permute-done.4.low_ref
  192.4 0.0 copy-start.3
  192.4 0.0 collective-permute-done.5.high_ref
  192.4 0.6 copy-done.3
  193.1 0.0 copy-start.4
  193.1 0.6 copy-done.4
  193.7 18.6 %shard_map.185 = (f32[8,32,1024]{2,1,0:T(8,128)}, f32[3,8,32,1024]{3,2,1,0:T(8,128)}) custom-call(s32[5,8]{1,0:T(8,128)} %convert_element_type.6.flag_ref, f32[8,16,128]{2,1,0:T(8,128)} %pad.4.patch_ref, f32[40,16]{1,0:T(8,128)} %constant.100.clone.xt_ref, f32[128,3840]{1,0:T(8,128)} %constant.101.clone.yz_ref, f32[8,32,1024]{2,1,0:T(8,128)} %mid_ref.1, ...), custom_call_target="tpu_custom_call" | custom-call | tf_op jit(solution)/shard_map/pallas_call | solution.py:678
  (25 shorter events, 0.4 us)
Async XLA Ops:
  2.1 11.8 %copy-start.5 = (f32[48,48,1]{1,0,2:T(8,128)S(1)}, f32[48,48,1]{1,0,2:T(8,128)}, u32[]{:S(2)}) copy-start(f32[48,48,1]{1,0,2:T(8,128)} %constant.107) | copy-start | bytes 27652
  95.6 5.3 %copy-start.2 = (f32[384,384,1]{1,0,2:T(8,128)S(1)}, f32[384,384,1]{1,0,2:T(8,128)}, u32[]{:S(2)}) copy-start(f32[384,384,1]{1,0,2:T(8,128)} %constant.106) | copy-start | bytes 1769476
  100.9 18.1 %copy-start.6 = (s32[3,256]{1,0:T(4,128)S(1)}, s32[3,256]{1,0:T(4,128)}, u32[]{:S(2)}) copy-start(s32[3,256]{1,0:T(4,128)} %param.20) | copy-start | bytes 9220
  100.9 40.0 %copy-start.7 = (s32[2,256]{1,0:T(2,128)S(1)}, s32[2,256]{1,0:T(2,128)}, u32[]{:S(2)}) copy-start(s32[2,256]{1,0:T(2,128)} %param.22) | copy-start | bytes 6148
  101.0 42.7 %copy-start.8 = (s32[32]{0:T(128)S(1)}, s32[32]{0:T(128)}, u32[]{:S(2)}) copy-start(s32[32]{0:T(128)} %param.21) | copy-start | bytes 388
  107.5 3.0 %copy-start = (f32[96,48,384]{2,1,0:T(8,128)}, f32[96,48,384]{2,1,0:T(8,128)S(1)}, u32[]{:S(2)}) copy-start(f32[96,48,384]{2,1,0:T(8,128)S(1)} %fusion) | copy-start | bytes 21233668
  110.5 45.2 %collective-permute-start = (f32[1,48,384]{2,1,0:T(8,128)S(1)}, f32[1,48,384]{2,1,0:T(8,128)S(1)}, u32[]{:S(2)}, u32[]{:S(2)}) collective-permute-start(f32[1,48,384]{2,1,0:T(8,128)S(1)} %get-tuple-element.9), channel_id=1, source_target_pairs={{0,8},{8,16},{16,24},{24,0},{1,9},{9,17},{17,25},{25,1},{2,10},{10... | collective-permute-start | bytes 221192 | tf_op jit(solution)/shard_map/ppermute | solution.py:114
  113.4 42.3 %collective-permute-start.1 = (f32[1,48,384]{2,1,0:T(8,128)S(1)}, f32[1,48,384]{2,1,0:T(8,128)S(1)}, u32[]{:S(2)}, u32[]{:S(2)}) collective-permute-start(f32[1,48,384]{2,1,0:T(8,128)S(1)} %get-tuple-element.10), channel_id=1, source_target_pairs={{8,0},{16,8},{24,16},{0,24},{9,1},{17,9},{25,17},{1,25},{10,2},{18... | collective-permute-start | bytes 221192 | tf_op jit(solution)/shard_map/ppermute | solution.py:117
  114.4 78.0 %collective-permute-start.4 = (f32[8,32,128]{2,1,0:T(8,128)S(1)}, f32[8,32,128]{2,1,0:T(8,128)S(1)}, u32[]{:S(2)}, u32[]{:S(2)}) collective-permute-start(f32[8,32,128]{2,1,0:T(8,128)S(1)} %get-tuple-element.12), channel_id=1, source_target_pairs={{0,1},{1,2},{2,3},{3,4},{4,5},{5,6},{6,7},{8,9},{9,10},{10,11},{11... | collective-permute-start | bytes 393224 | tf_op jit(solution)/shard_map/ppermute | solution.py:107
  117.7 74.7 %collective-permute-start.5 = (f32[8,32,128]{2,1,0:T(8,128)S(1)}, f32[8,32,128]{2,1,0:T(8,128)S(1)}, u32[]{:S(2)}, u32[]{:S(2)}) collective-permute-start(f32[8,32,128]{2,1,0:T(8,128)S(1)} %get-tuple-element.11), channel_id=1, source_target_pairs={{1,0},{2,1},{3,2},{4,3},{5,4},{6,5},{7,6},{9,8},{10,9},{11,10},{12... | collective-permute-start | bytes 393224 | tf_op jit(solution)/shard_map/ppermute | solution.py:107
  155.7 20.0 %copy-start.1 = (f32[96,48,384]{2,1,0:T(8,128)S(1)}, f32[96,48,384]{2,1,0:T(8,128)}, u32[]{:S(2)}) copy-start(f32[96,48,384]{2,1,0:T(8,128)} %copy-done) | copy-start | bytes 21233668
  157.7 15.7 %collective-permute-start.2 = (f32[98,2,384]{2,1,0:T(2,128)S(1)}, f32[98,2,384]{2,1,0:T(2,128)S(1)}, u32[]{:S(2)}, u32[]{:S(2)}) collective-permute-start(f32[98,2,384]{2,1,0:T(2,128)S(1)} %get-tuple-element.7), channel_id=1, source_target_pairs={{0,1},{1,2},{2,3},{3,4},{4,5},{5,6},{6,7},{7,0},{8,9},{9,10},{10,1... | collective-permute-start | bytes 903176 | tf_op jit(solution)/shard_map/ppermute | solution.py:114
  160.4 15.3 %collective-permute-start.3 = (f32[98,2,384]{2,1,0:T(2,128)S(1)}, f32[98,2,384]{2,1,0:T(2,128)S(1)}, u32[]{:S(2)}, u32[]{:S(2)}) collective-permute-start(f32[98,2,384]{2,1,0:T(2,128)S(1)} %get-tuple-element.8), channel_id=1, source_target_pairs={{1,0},{2,1},{3,2},{4,3},{5,4},{6,5},{7,6},{0,7},{9,8},{10,9},{11,1... | collective-permute-start | bytes 903176 | tf_op jit(solution)/shard_map/ppermute | solution.py:117
  179.4 11.7 %all-to-all-start = ((f32[8,1,1200]{2,1,0:T(1,128)}), f32[8,1,1200]{2,1,0:T(1,128)S(1)}, u32[]{:S(2)}, u32[]{:S(2)}) async-start(f32[8,1,1200]{2,1,0:T(1,128)} %all_to_all.11), calls=%async_computation | async-start | bytes 81920 | tf_op jit(solution)/shard_map/all_to_all | solution.py:667
  192.4 0.7 copy-start.3
  193.1 0.7 copy-start.4

commit v2 on v1

--- a/solution.py
+++ b/solution.py
@@ -70,6 +70,7 @@
     return table
 
 
+PATCH = REG + 2
 PATCH_X = REG + 2
 PATCH_Y = REG + 4
 PATCH_Z = REG + 2
@@ -101,23 +102,6 @@
     return x_table.astype(np.float32), table.astype(np.float32)
 
 
-def from_behind(value, axis, steps):
-    count = lax.axis_size(axis)
-    initial, last = (max(0, -steps), min(count, count - steps))
-    return lax.ppermute(value, axis, [(source, source + steps) for source in range(initial, last)])
-
-
-def extended(block, axis, dim, width):
-    count = lax.axis_size(axis)
-    forward = [(i, (i + 1) % count) for i in range(count)]
-    backward = [(target, source) for source, target in forward]
-    low = lax.ppermute(
-        lax.slice_in_dim(block, block.shape[dim] - width, None, axis=dim), axis, forward
-    )
-    high = lax.ppermute(lax.slice_in_dim(block, 0, width, axis=dim), axis, backward)
-    return jnp.concatenate([low, block, high], axis=dim)
-
-
 def decay(delta):
     return 1.0 / (1.0 + 0.5 * delta + jnp.sqrt(delta + 0.25 * delta * delta))
 
@@ -143,7 +127,11 @@
     basis_ref,
     mix_ref,
     angle_ref,
+    density_ref,
     out_ref,
+    edge_ref,
+    low_ref,
+    high_ref,
     held,
     lines,
     sent,
@@ -164,6 +152,8 @@
     send_back,
     recv_back,
     self_sem,
+    send_face,
+    recv_face,
 ):
     count_first, count_second, owners = sizes
     devices = count_first * count_second
@@ -211,6 +201,10 @@
         block = basis_ref[i * rows : (i + 1) * rows, :]
         table[i, :rows, :wave] = block
         table[i, rows : 2 * rows, wave:] = block
+        for place, row in enumerate((rows * (i + 1) % wave, (rows * i - 1) % wave)):
+            line = basis_ref[row : row + 1, :]
+            table[i, 2 * rows + 2 + place : 2 * rows + 3 + place, :wave] = line
+            table[i, 2 * rows + 4 + place : 2 * rows + 5 + place, wave:] = line
 
     def row_of(ref, i):
         return tuple(ref[i, 8 * g : 8 * g + 8, :] for g in range(groups))
@@ -255,8 +249,23 @@
         return split(up * norm), split(down * norm)
 
     pl.semaphore_wait(barrier, devices - 1)
+    face = low_ref.shape[2]
+    inner = density_ref.shape[2]
+    faces = [
+        pltpu.make_async_remote_copy(
+            src_ref=density_ref.at[:, :, pl.ds(start, face)],
+            dst_ref=target,
+            send_sem=send_face.at[n],
+            recv_sem=recv_face.at[n],
+            device_id=(place_first, lax.rem(place_second + step, count_second)),
+            device_id_type=mesh,
+        )
+        for n, (start, target, step) in enumerate(
+            ((inner - face, low_ref, 1), (0, high_ref, count_second - 1))
+        )
+    ]
     first = shares(mom_one, send_one, recv_one)
-    for copy in first:
+    for copy in first + faces:
         copy.start()
     lines[2 * rows :, :] = jnp.zeros((width - 2 * rows, wave), F32)
     lines[2 * rows : 2 * rows + 1, :] = jnp.sum(vec_ref[2] * whole, axis=0, keepdims=True)
@@ -415,6 +424,9 @@
 
     over(owners, lambda o: back_from(o).wait_recv())
     lines[...] = back[...].T
+    for n, (start, halo) in enumerate(((0, 2 * rows + 2), (rows, 2 * rows + 4))):
+        edge_ref[n, :rows, :] = lines[start : start + rows, :]
+        edge_ref[n, rows : rows + 2, :] = lines[halo : halo + 2, :]
     mean_term = vec_ref[2] * lines[2 * rows : 2 * rows + 1, :]
     weight[2] = mean_term
 
@@ -472,20 +484,175 @@
             out_ref[i, window, :] = (out_ref[i, window, :] + down[g]) * weight[1, window, :]
         return tuple(down[g] + f[g] for g in range(groups))
 
-    lax.fori_loop(0, rows, up_last, carry_up)
-    lax.fori_loop(0, rows, down_last, carry_down)
+    up = lax.fori_loop(0, rows, up_last, carry_up)
+    down = lax.fori_loop(0, rows, down_last, carry_down)
+    for g in range(groups):
+        window = slice(8 * g, 8 * g + 8)
+        scale = weight[1, window, :]
+        out_ref[rows, window, :] = (r[g] * up[g] + carry_down[g]) * scale
+        out_ref[rows + 1, window, :] = (carry_up[g] + r[g] * down[g]) * scale
+    for copy in faces:
+        copy.wait()
+
+
+def halves(value):
+    high = value.astype(jnp.bfloat16)
+    return high, (value - high.astype(F32)).astype(jnp.bfloat16)
+
+
+def grid_values_kernel(
+    step, anchor_ref, u_ref, edge_ref, strip_ref, wave_ref, out_ref, patch_ref, ext, cut, sems
+):
+    planes, strip, wave = u_ref.shape
+    rows = planes - 2
+    tall = ext.shape[1]
+    tiles = tall // 8
+    chunks = planes // step
+    tail = rows - (chunks - 1) * step
+    second = strip_ref.shape[0]
+    place_first = lax.axis_index("px")
+    place_second = lax.axis_index("py")
+    count = lax.axis_size("py")
+    sub = lax.broadcasted_iota(jnp.int32, (8, wave), 0)
+
+    def out_copy(c, size):
+        start = c * step
+        return pltpu.make_async_copy(
+            ext.at[pl.ds(start, size), :strip, :], out_ref.at[pl.ds(start, size)], sems.at[c]
+        )
+
+    def chunk(c, carry):
+        values = []
+        for i in range(step):
+            k = c * step + i
+            high, low = halves(u_ref[k])
+            stack = jnp.concatenate([high, high, low], axis=0)
+            value = jnp.dot(strip_ref[...], stack, preferred_element_type=F32)
+            s, t = edge_ref[0, pl.ds(k, 1), :], edge_ref[1, pl.ds(k, 1), :]
+            halo = jnp.where(sub == 0, 0.5 * (s - t), jnp.where(sub == 7, 0.5 * (s + t), 0.0))
+            values += [value[:strip], value[strip:] + halo]
+        high, low = halves(jnp.concatenate(values, axis=0))
+        wide = jnp.concatenate([high, low, high], axis=1)
+        result = jnp.dot(wide, wave_ref[...], preferred_element_type=F32)
+        ext[pl.ds(c * step, step)] = result.reshape(step, tall, wave)
+
+        @pl.when(c < chunks - 1)
+        def _():
+            out_copy(c, step).start()
+
+        return carry
+
+    lax.fori_loop(0, chunks, chunk, 0)
+    out_copy(chunks - 1, tail).start()
+    lane = lax.broadcasted_iota(jnp.int32, cut.shape[::2], 1)
+    cut[...] = jnp.zeros_like(cut)
+
+    def patch(t, carry):
+        slot = (place_first * count + t) * count + lax.rem(place_second - t + count, count)
+        x = jnp.clip(anchor_ref[0, slot] - place_first * rows, 0, rows - REG)
+        y = jnp.clip(anchor_ref[1, slot] - place_second * strip, 0, strip - REG) // 8
+        shift = lax.rem(wave + 1 - jnp.clip(anchor_ref[2, slot], 0, wave - REG), wave)
+        for i in range(REG + 2):
+            row = x - 1 + i
+            row = jnp.where(row < 0, rows + 1, row)
+            for d in range(3):
+                tile = lax.rem(y + d - 1 + tiles, tiles)
+                value = ext[row, pl.ds(pl.multiple_of(tile * 8, 8), 8), :]
+                cut[i, 8 * d : 8 * d + 8, :] = pltpu.roll(value, shift, 1)[:, :128]
+        total = jnp.zeros(lane.shape, F32)
+        for b in range(PATCH):
+            line = jnp.where(lane < PATCH, cut[:, 7 + b, :], 0.0)
+            total = total + (pltpu.roll(line, PATCH * b, 1) if b else line)
+        patch_ref[t + 1] = total
+        return carry
+
+    lax.fori_loop(0, count, patch, 0)
+    patch_ref[0] = patch_ref[count]
+    patch_ref[count + 1] = patch_ref[1]
+
+    def finish(c, carry):
+        out_copy(c, step).wait()
+        return carry
+
+    lax.fori_loop(0, chunks - 1, finish, 0)
+    out_copy(chunks - 1, tail).wait()
+
+
+def patch_exchange_kernel(patch_ref, out_ref, send_sems, recv_sems, own_sem):
+    count = out_ref.shape[0]
+    place_first = lax.axis_index("px")
+    place_second = lax.axis_index("py")
+    barrier = pltpu.get_barrier_semaphore()
+    mesh = pl.DeviceIdType.MESH
+    for d in range(1, count):
+        pl.semaphore_signal(
+            barrier,
+            inc=1,
+            device_id=(place_first, lax.rem(place_second + d, count)),
+            device_id_type=mesh,
+        )
+    own = pltpu.make_async_copy(
+        patch_ref.at[pl.ds(place_second, 3)], out_ref.at[0], own_sem
+    )
+    own.start()
+    pl.semaphore_wait(barrier, count - 1)
+    copies = []
+    for d in range(1, count):
+        target = lax.rem(place_second + d, count)
+        copies.append(
+            pltpu.make_async_remote_copy(
+                src_ref=patch_ref.at[pl.ds(target, 3)],
+                dst_ref=out_ref.at[count - d],
+                send_sem=send_sems.at[d],
+                recv_sem=recv_sems.at[d],
+                device_id=(place_first, target),
+                device_id_type=mesh,
+            )
+        )
+    for copy in copies:
+        copy.start()
+    own.wait()
+    for copy in copies:
+        copy.wait()
 
 
 def subgrid_kernel(
-    flag_ref, patch_ref, xt_ref, yz_ref, mid_ref, low_ref, high_ref, vel_ref, pot_ref, kick_ref
+    count_ref,
+    near_ref,
+    own_ref,
+    under_ref,
+    over_ref,
+    xt_ref,
+    yz_ref,
+    mid_ref,
+    low_ref,
+    high_ref,
+    vel_ref,
+    pot_ref,
+    kick_ref,
 ):
-    slot = pl.program_id(0)
-    live = flag_ref[0, slot] > 0
-    has_below = flag_ref[1, slot] > 0
-    has_above = flag_ref[2, slot] > 0
-    back_below = flag_ref[3, slot] > 0
-    back_above = flag_ref[4, slot] > 0
-    planes = jnp.dot(patch_ref[0], yz_ref[...], precision=HIGHEST, preferred_element_type=F32)
+    device = lax.axis_index("px") * lax.axis_size("py") + lax.axis_index("py")
+    place = pl.program_id(0)
+    slot = device * pl.num_programs(0) + place
+    below = near_ref[0, slot]
+    above = near_ref[1, slot]
+    live = place < count_ref[device]
+    has_below = below >= 0
+    has_above = above >= 0
+    back_below = near_ref[1, jnp.maximum(below, 0)] >= 0
+    back_above = near_ref[0, jnp.maximum(above, 0)] >= 0
+    column = lax.broadcasted_iota(jnp.int32, (16, 128), 1)
+    patch = jnp.where(
+        column < PATCH,
+        pltpu.roll(under_ref[0, 0], 128 - (REG - 1) * PATCH, 1),
+        jnp.where(
+            column < (PATCH + 1) * PATCH,
+            pltpu.roll(own_ref[0, 0], PATCH, 1),
+            pltpu.roll(over_ref[0, 0], (PATCH - 1) * PATCH, 1),
+        ),
+    )
+    patch = jnp.where(column < (PATCH + 2) * PATCH, patch, 0.0)
+    planes = jnp.dot(patch, yz_ref[...], precision=HIGHEST, preferred_element_type=F32)
     coarse = jnp.dot(xt_ref[...], planes, precision=HIGHEST, preferred_element_type=F32)
     start = coarse[:CELLS, :WIDE]
     x_low = coarse[CELLS : CELLS + 1, :WIDE]
@@ -539,7 +706,7 @@
         kick_ref[q, 0] = jnp.where(live, vel_ref[q, 0] - slope, 0.0)
 
 
-def poisson(root_density):
+def poisson(root_density, density, slot_anchor):
     count_first = lax.axis_size("px")
     count_second = lax.axis_size("py")
     devices = count_first * count_second
@@ -547,7 +714,7 @@
     rows, strip, wave = root_density.shape
     chunk = next(q for q in range(8, wave + 1, 8) if wave % q == 0 and wave // q <= devices)
     owners = wave // chunk
-    width = -(-(2 * rows + 2) // 128) * 128
+    width = -(-(2 * rows + 6) // 128) * 128
     basis = fourier_basis(wave)
     strip_table, strip_eig = strip_basis(strip)
     eig = 4.0 * np.sin(np.pi / wave * np.arange(wave)) ** 2
@@ -573,11 +740,19 @@
     f = jnp.einsum("xyc,by->xbc", f, y_basis, precision=HIGH)
     moment = pltpu.VMEM((count_first, 2, strip, wave), F32)
     dma = pltpu.SemaphoreType.DMA
-    u = pl.pallas_call(
+    face = jax.ShapeDtypeStruct(density.shape[:2] + (EDGE * CELLS,), F32)
+    vmem = pl.BlockSpec(memory_space=pltpu.VMEM)
+    hbm = pl.BlockSpec(memory_space=pl.ANY)
+    u, edges, low_density, high_density = pl.pallas_call(
         lambda *refs: grid_kernel((count_first, count_second, owners), *refs),
-        in_specs=[pl.BlockSpec(memory_space=pltpu.VMEM)] * 8,
-        out_specs=pl.BlockSpec(memory_space=pltpu.VMEM),
-        out_shape=jax.ShapeDtypeStruct((rows, strip, wave), F32),
+        in_specs=[vmem] * 8 + [hbm],
+        out_specs=[vmem, vmem, hbm, hbm],
+        out_shape=[
+            jax.ShapeDtypeStruct((rows + 2, strip, wave), F32),
+            jax.ShapeDtypeStruct((2, rows + 2, wave), F32),
+            face,
+            face,
+        ],
         scratch_shapes=[
             pltpu.VMEM((rows, strip, wave), F32),
             pltpu.VMEM((width, wave), F32),
@@ -599,6 +774,8 @@
             dma((devices,)),
             dma((owners,)),
             dma((2,)),
+            dma((2,)),
+            dma((2,)),
         ],
         compiler_params=pltpu.CompilerParams(
             collective_id=1, has_side_effects=True, vmem_limit_bytes=60 * 1024 * 1024
@@ -612,75 +789,69 @@
         jnp.asarray(basis.T, F32),
         jnp.asarray(mixes, F32),
         jnp.asarray(angles, F32),
-    )
-    u = jnp.einsum("xbc,by->xyc", u, y_basis, precision=HIGH)
-    return jnp.einsum("xyc,cz->xyz", u, z_basis, precision=HIGH)
+        density,
+    )
+    tall = strip + 8
+    step = max(n for n in range(1, 15) if (rows + 2) % n == 0)
+    extended = np.zeros((tall, strip))
+    extended[:strip] = strip_table.T
+    extended[strip] = -strip_table[:, 0]
+    extended[-1] = -strip_table[:, -1]
+    high, low = halves(jnp.asarray(extended, F32))
+    strip_wide = jnp.concatenate([high, low, high], axis=1)
+    high, low = halves(z_basis)
+    wave_tall = jnp.concatenate([high, high, low], axis=0)
+    chunks = (rows + 2) // step
+    coarse, patches = pl.pallas_call(
+        lambda *refs: grid_values_kernel(step, *refs),
+        in_specs=[pl.BlockSpec(memory_space=pltpu.SMEM)] + [vmem] * 4,
+        out_specs=[hbm, vmem],
+        out_shape=[
+            jax.ShapeDtypeStruct((rows, strip, wave), F32),
+            jax.ShapeDtypeStruct((count_second + 2, 16, 128), F32),
+        ],
+        scratch_shapes=[
+            pltpu.VMEM((rows + 2, tall, wave), F32),
+            pltpu.VMEM((16, 24, 128), F32),
+            dma((chunks,)),
+        ],
+        compiler_params=pltpu.CompilerParams(vmem_limit_bytes=60 * 1024 * 1024),
+    )(slot_anchor, u, edges, strip_wide, wave_tall)
+    arrived = pl.pallas_call(
+        patch_exchange_kernel,
+        in_specs=[vmem],
+        out_specs=vmem,
+        out_shape=jax.ShapeDtypeStruct((count_second, 3, 16, 128), F32),
+        scratch_shapes=[dma((count_second,)), dma((count_second,)), dma(())],
+        compiler_params=pltpu.CompilerParams(collective_id=2, has_side_effects=True),
+    )(patches)
+    return coarse, arrived, low_density, high_density
 
 
 def local(root_density, subgrid_density, velocity, slot_anchor, slot_count, neighbour):
-    first_rows, second_rows = root_density.shape[:2]
-    size_second = lax.axis_size("py")
-    place_first = lax.axis_index("px")
-    place_second = lax.axis_index("py")
-    device = place_first * size_second + place_second
     per_device = subgrid_density.shape[0]
     side = EDGE * CELLS
     inner = CELLS * CELLS
-    positions = jnp.arange(per_device, dtype=jnp.int32)
-
-    def early(density, anchors, counts, near):
-        low_density = from_behind(density[:, :, inner - side :], "py", 1)
-        high_density = from_behind(density[:, :, :side], "py", -1)
-        owner = place_first * size_second + jnp.arange(size_second, dtype=jnp.int32)
-        wanted = (place_second - jnp.arange(size_second, dtype=jnp.int32)) % size_second
-        anchor = anchors[:, owner * per_device + wanted]
-        x = jnp.clip(anchor[0] - place_first * first_rows, 0, first_rows - REG)
-        y = jnp.clip(anchor[1] - place_second * second_rows, 0, second_rows - REG)
-        columns = (anchor[2][:, None] - 1 + jnp.arange(PATCH_Z, dtype=jnp.int32)) % NR
-        pick = (jnp.arange(NR, dtype=jnp.int32)[None, :, None] == columns[:, None, :]).astype(F32)
-        slots = device * per_device + positions
-        below, above = near[0][slots], near[1][slots]
-        flags = jnp.stack(
-            [
-                positions < counts[device],
-                below >= 0,
-                above >= 0,
-                near[1][jnp.maximum(below, 0)] >= 0,
-                near[0][jnp.maximum(above, 0)] >= 0,
-            ]
-        ).astype(jnp.int32)
-        return low_density, high_density, x, y, pick, flags
-
-    low_density, high_density, x, y, pick, flags = early(
-        subgrid_density, slot_anchor, slot_count, neighbour
-    )
-    coarse_potential = poisson(root_density)
-    padded = extended(extended(coarse_potential, "px", 0, 1), "py", 1, 2)
-    cuts = jnp.stack(
-        [
-            lax.dynamic_slice(padded, (x[t], y[t], 0), (PATCH_X, PATCH_Y, NR))
-            for t in range(size_second)
-        ]
-    )
-    patches = jnp.einsum("txyn,tnz->txyz", cuts, pick, precision=HIGHEST)
-    patches = patches.reshape(size_second, -1)
-    arrived = lax.all_to_all(
-        patches, "py", split_axis=0, concat_axis=0, tiled=True
-    )
-    patch = arrived[(place_second + positions) % size_second]
-    patch = patch.reshape(per_device, PATCH_X, PATCH_Y * PATCH_Z)
-    patch = jnp.pad(
-        patch, ((0, 0), (0, 16 - PATCH_X), (0, 128 - PATCH_Y * PATCH_Z))
+    coarse_potential, patches, low_density, high_density = poisson(
+        root_density, subgrid_density, slot_anchor
     )
     x_table, yz_table = patch_tables()
+    count = lax.axis_size("py")
+    smem = pl.BlockSpec(memory_space=pltpu.SMEM)
     slot_spec = lambda width: pl.BlockSpec((1, CELLS, width), lambda s: (s, 0, 0))
     vel_spec = pl.BlockSpec((3, 1, CELLS, inner), lambda s: (0, s, 0, 0))
+    patch_spec = lambda step: pl.BlockSpec(
+        (1, 1, 16, 128), lambda s: (lax.rem(s + step + count, count), step + 1, 0, 0)
+    )
     potential, kicked = pl.pallas_call(
         subgrid_kernel,
         grid=(per_device,),
         in_specs=[
-            pl.BlockSpec(memory_space=pltpu.SMEM),
-            pl.BlockSpec((1, 16, 128), lambda s: (s, 0, 0)),
+            smem,
+            smem,
+            patch_spec(0),
+            patch_spec(-1),
+            patch_spec(1),
             pl.BlockSpec(x_table.shape, lambda s: (0, 0)),
             pl.BlockSpec(yz_table.shape, lambda s: (0, 0)),
             slot_spec(inner),
@@ -697,8 +868,11 @@
             dimension_semantics=("arbitrary",), vmem_limit_bytes=60 * 1024 * 1024
         ),
     )(
-        flags,
-        patch,
+        slot_count,
+        neighbour,
+        patches,
+        patches,
+        patches,
         jnp.asarray(x_table),
         jnp.asarray(yz_table),
         subgrid_density,

time: 213 us -> 135 us (0.63)
  between operations: 31.5 us -> 0.8 us
  Pallas kernels: 88.5 us -> 116 us
  matrix products: 36.5 us -> 15.1 us
  waiting for transfers between devices: 19 us -> 0 us
  starting transfers between devices: 18 us -> 0 us
  local copies, waits for them, and re-layouts: 13.8 us -> 1.49 us
  other arithmetic: 4.97 us -> 0 us
    pallas_call x1 -> x3, Pallas kernels: 18.6 us -> 46 us  [the longest x1 19.5 us: local(): pl.pallas_call(subgrid_kernel, grid=(per_device,), in_specs=[smem, smem,...]
    ppermute x6 -> x0, starting transfers between devices: 13.1 us -> none  [the longest x2 5.56 us: extended(): lax.ppermute(lax.slice_in_dim(block, block.shape[dim] - width, None, axis...]
    dot_general x3 -> x0, matrix products: 12.9 us -> none  [the longest x1 6.58 us: poisson(): return jnp.einsum('xyc,cz->xyz', u, z_basis, precision=HIGH)]
    ppermute x6 -> x0, waiting for transfers between devices: 12.3 us -> none  [the longest x2 9.94 us: extended(): lax.ppermute(lax.slice_in_dim(block, block.shape[dim] - width, None, axis...]
    dot_general x1, matrix products: 11.8 us -> 4.89 us  [poisson(): f = jnp.einsum('xyc,by->xbc', f, y_basis, precision=HIGH)]
    all_to_all x1 -> x0, waiting for transfers between devices: 6.73 us -> none  [local(): lax.all_to_all(patches, 'py', split_axis=0, concat_axis=0, tiled=True)]
    all_to_all x1 -> x0, starting transfers between devices: 4.94 us -> none  [local(): lax.all_to_all(patches, 'py', split_axis=0, concat_axis=0, tiled=True)]
    unnamed x27 -> x2, local copies, waits for them, and re-layouts: 4.68 us -> 0.01 us
  transfers between devices with their start and end apart: 7 -> 0, of which waited for: 3 -> 0; matrix products, arithmetic and copies ran while one was open for 6% -> 0% of each run, Pallas kernels for 0% -> 0%
where the time goes in v2:
time: 135 us; the launch traced here: 134 us
  Pallas kernels  116 us (86%)
  matrix products  15.1 us (11%)
  local copies, waits for them, and re-layouts  1.49 us (1%)
    pallas_call x1, Pallas kernels, poisson(): pl.pallas_call(lambda *refs: grid_kernel((count_first, count_second, owne...  70.5 us
    pallas_call x1, Pallas kernels, local(): pl.pallas_call(subgrid_kernel, grid=(per_device,), in_specs=[smem, smem,...  19.5 us
    pallas_call x1, Pallas kernels, poisson(): pl.pallas_call(lambda *refs: grid_values_kernel(step, *refs), in_specs=[p...  16.8 us
    dot_general x1, matrix products, poisson(): f = jnp.einsum('xyz,cz->xyc', root_density, z_basis, precision=HIGH)  10.2 us
    pallas_call x1, Pallas kernels, poisson(): pl.pallas_call(patch_exchange_kernel, in_specs=[vmem], out_specs=vmem, ou...  9.68 us
    dot_general x1, matrix products, poisson(): f = jnp.einsum('xyc,by->xbc', f, y_basis, precision=HIGH)  4.89 us

profile of v2, /device:TPU:0, one launch (start us, length us, event | category | flops | bytes accessed | tf_op | source)
XLA Modules:
  0.0 133.8 jit_solution(9693437213466003259)
XLA Ops:
  0.6 0.8 dynamic_slice.3
  1.4 0.7 broadcast_in_dim_tile.4.refs_3_
  2.1 0.0 copy-start
  2.1 10.2 %fusion.5 = f32[384,96,48]{0,2,1:T(8,128)S(1)} fusion(f32[384,384,1]{1,0,2:T(8,128)} %constant.66, f32[96,48,384]{2,1,0:T(8,128)} %param.18), kind=kOutput, calls=%fused_computation.3 | convolution fusion | flops 4076863488 | bytes 14745600 | tf_op jit(solution)/shard_map/xyz,cz->xyc/dot_general | solution.py:739
  12.3 0.0 copy-done
  12.3 4.9 %fusion.2.refs_0_ = f32[96,48,384]{2,1,0:T(8,128)} fusion(f32[48,48,1]{1,0,2:T(8,128)S(1)} %copy-done, f32[384,96,48]{0,2,1:T(8,128)S(1)} %fusion.5), kind=kOutput, calls=%fused_computation.2 | convolution fusion | flops 509607936 | bytes 14164992 | tf_op jit(solution)/shard_map/xyc,by->xbc/dot_general | solution.py:740
  17.2 70.5 %shard_map.193 = (f32[98,48,384]{2,1,0:T(8,128)}, f32[2,98,384]{2,1,0:T(8,128)}, f32[8,32,128]{2,1,0:T(8,128)}, f32[8,32,128]{2,1,0:T(8,128)}) custom-call(f32[96,48,384]{2,1,0:T(8,128)} %fusion.2.refs_0_, f32[48,1]{1,0:T(8,128)} %constant.45.clone.refs_1_, f32[1,384]{1,0:T(1,128)} %constant.46.clone.refs_2_, f32[128,1]{1,0:T(8,128)} %broadcast_in_dim_tile.4.refs_3_, ...), custom_call_target="tpu_custom_call" | custom-call | tf_op jit(solution)/shard_map/pallas_call | solution.py:746
  87.7 16.8 %shard_map.194 = (f32[96,48,384]{2,1,0:T(8,128)}, f32[10,16,128]{2,1,0:T(8,128)}) custom-call(s32[3,256]{1,0:T(4,128)} %refs_0_.1, f32[98,48,384]{2,1,0:T(8,128)} %get-tuple-element.11.refs_1_, f32[2,98,384]{2,1,0:T(8,128)} %get-tuple-element.12.refs_2_, bf16[56,144]{1,0:T(8,128)(2,1)} %constant.60.refs_3_, bf16[1152,384]{1,0:T(8,128)(2,1)} %constant.65.refs_4_), custom_call_target="tpu_custom_call" | custom-call | tf_op jit(solution)/shard_map/pallas_call | solution.py:805
  104.6 9.7 %shard_map.195.own_ref.under_ref.over_ref = f32[8,3,16,128]{3,2,1,0:T(8,128)} custom-call(f32[10,16,128]{2,1,0:T(8,128)} %get-tuple-element.14.patch_ref), custom_call_target="tpu_custom_call" | custom-call | tf_op jit(solution)/shard_map/pallas_call | solution.py:820
  114.2 19.5 %shard_map.196 = (f32[8,32,1024]{2,1,0:T(8,128)}, f32[3,8,32,1024]{3,2,1,0:T(8,128)}) custom-call(s32[32]{0:T(128)} %count_ref.1, s32[2,256]{1,0:T(2,128)} %near_ref.1, f32[8,3,16,128]{3,2,1,0:T(8,128)} %shard_map.195.own_ref.under_ref.over_ref, f32[8,3,16,128]{3,2,1,0:T(8,128)} %shard_map.195.own_ref.under_ref.over_ref, ...), custom_call_target="tpu_custom_call" | custom-call | tf_op jit(solution)/shard_map/pallas_call | solution.py:846
  (1 shorter events, 0.0 us)
Async XLA Ops:
  2.1 10.2 %copy-start = (f32[48,48,1]{1,0,2:T(8,128)S(1)}, f32[48,48,1]{1,0,2:T(8,128)}, u32[]{:S(2)}) copy-start(f32[48,48,1]{1,0,2:T(8,128)} %constant.67) | copy-start | bytes 27652

commit v3 on v2

--- a/solution.py
+++ b/solution.py
@@ -117,9 +117,21 @@
     return result
 
 
+def halves(value):
+    high = value.astype(jnp.bfloat16)
+    return high, (value - high.astype(F32)).astype(jnp.bfloat16)
+
+
+def owner_shift(place_second):
+    return place_second // 2 * 2 + 2
+
+
+LANES = 128
+
+
 def grid_kernel(
     sizes,
-    f_ref,
+    f_hbm,
     eig_b_ref,
     eig_ref,
     own_ref,
@@ -128,11 +140,12 @@
     mix_ref,
     angle_ref,
     density_ref,
-    out_ref,
+    out_hbm,
     edge_ref,
     low_ref,
     high_ref,
-    held,
+    f_ref,
+    out_ref,
     lines,
     sent,
     got,
@@ -142,7 +155,10 @@
     mom_two,
     part,
     table,
+    factor,
     weight,
+    in_sem,
+    out_sem,
     send_one,
     recv_one,
     send_two,
@@ -155,17 +171,24 @@
     send_face,
     recv_face,
 ):
-    count_first, count_second, owners = sizes
+    count_first, count_second = sizes
     devices = count_first * count_second
     rows, strip, wave = f_ref.shape
+    tiles = wave // LANES
     groups = strip // 8
     half = strip // 2
-    chunk = sent.shape[0] // owners
+    middle = rows // 2
+    fold = 4
+    chunk = got.shape[1]
     width = lines.shape[0]
     mesh = pl.DeviceIdType.MESH
     place_first = lax.axis_index("px")
     place_second = lax.axis_index("py")
     me = place_first * count_second + place_second
+    own_tile = lax.rem(
+        place_first + 2 * count_second * count_first - owner_shift(place_second), count_first
+    )
+    is_owner = own_tile < tiles
     barrier = pltpu.get_barrier_semaphore()
 
     def greet(step, carry):
@@ -179,76 +202,104 @@
         return carry
 
     lax.fori_loop(1, devices, greet, 0)
-
-    def split(value):
-        return tuple(value[8 * g : 8 * g + 8] for g in range(groups))
+    lane_of = lambda t: slice(t * LANES, (t + 1) * LANES)
+    loads = [
+        pltpu.make_async_copy(
+            f_hbm.at[:, :, lane_of(t)], f_ref.at[:, :, lane_of(t)], in_sem.at[t]
+        )
+        for t in range(tiles)
+    ]
+    for copy in loads:
+        copy.start()
+
+    window = [slice(8 * g, 8 * g + 8) for g in range(groups)]
+    even_groups = [g for g in range(groups) if 8 * g < half]
+    odd_groups = [g for g in range(groups) if 8 * g + 8 > half]
+    zeros = tuple(jnp.zeros((8, LANES), F32) for _ in range(groups))
 
     r_all = decay(eig_b_ref[...] + eig_ref[...])
     scale_all = -r_all / ((1.0 - r_all) * (1.0 + r_all))
-    ratio = power(r_all, rows)
-    norm = 1.0 / (1.0 - power(ratio, count_first))
+    ratio_all = power(r_all, rows)
     weight[0] = r_all
     weight[1] = scale_all
     weight[2] = 2.0 * vec_ref[0] * scale_all
     weight[3] = -2.0 * vec_ref[1] * scale_all
-    r = split(r_all)
-    zeros = tuple(jnp.zeros((8, wave), F32) for _ in range(groups))
-    even_groups = [g for g in range(groups) if 8 * g < half]
-    odd_groups = [g for g in range(groups) if 8 * g + 8 > half]
-
-    table[...] = jnp.zeros_like(table)
-    for i in range(count_first):
-        block = basis_ref[i * rows : (i + 1) * rows, :]
-        table[i, :rows, :wave] = block
-        table[i, rows : 2 * rows, wave:] = block
-        for place, row in enumerate((rows * (i + 1) % wave, (rows * i - 1) % wave)):
-            line = basis_ref[row : row + 1, :]
-            table[i, 2 * rows + 2 + place : 2 * rows + 3 + place, :wave] = line
-            table[i, 2 * rows + 4 + place : 2 * rows + 5 + place, wave:] = line
-
-    def row_of(ref, i):
-        return tuple(ref[i, 8 * g : 8 * g + 8, :] for g in range(groups))
-
-    def up_first(i, carry):
-        up, total = carry
-        f = row_of(f_ref, i)
-        up = tuple(r[g] * up[g] + f[g] for g in range(groups))
-        return up, tuple(total[g] + f[g] for g in range(groups))
-
-    def down_first(i, down):
-        f = row_of(f_ref, rows - 1 - i)
-        return tuple(r[g] * down[g] + f[g] for g in range(groups))
-
-    up, total = lax.fori_loop(0, rows, up_first, (zeros, zeros))
-    down = lax.fori_loop(0, rows, down_first, zeros)
-    for g in range(groups):
-        mom_one[0, 0, 8 * g : 8 * g + 8, :] = up[g]
-        mom_one[0, 1, 8 * g : 8 * g + 8, :] = down[g]
-    whole = jnp.concatenate(total, axis=0)
-
-    def shares(buffer, send, recv):
+    weight[4] = ratio_all
+    weight[5] = 1.0 / (1.0 - power(ratio_all, count_first))
+
+    def weights(which, t):
+        return tuple(weight[which, window[g], lane_of(t)] for g in range(groups))
+
+    def row_of(ref, i, t):
+        return tuple(ref[i, window[g], lane_of(t)] for g in range(groups))
+
+    def step_on(r, state, f):
+        return tuple(r[g] * state[g] + f[g] for g in range(groups))
+
+    def both_ways(start, stop, body, carry):
+        def folded(n, carry):
+            for k in range(fold):
+                i = start + n * fold + k
+                carry = body(i, rows - 1 - i, carry)
+            return carry
+
+        return lax.fori_loop(0, (stop - start) // fold, folded, carry)
+
+    def store_moments(buffer, t, up, down):
+        for g in range(groups):
+            buffer[t, 0, 0, window[g], :] = up[g]
+            buffer[t, 0, 1, window[g], :] = down[g]
+
+    def shares(buffer, send, recv, t):
         return [
             pltpu.make_async_remote_copy(
-                src_ref=buffer.at[0],
-                dst_ref=buffer.at[d],
-                send_sem=send.at[d],
-                recv_sem=recv.at[d],
+                src_ref=buffer.at[t, 0],
+                dst_ref=buffer.at[t, d],
+                send_sem=send.at[t, d],
+                recv_sem=recv.at[t, d],
                 device_id=(lax.rem(place_first + d, count_first), place_second),
                 device_id_type=mesh,
             )
             for d in range(1, count_first)
         ]
 
-    def carries(buffer):
-        up = jnp.zeros((strip, wave), F32)
-        down = jnp.zeros((strip, wave), F32)
-        for d in [0] + list(range(count_first - 1, 0, -1)):
-            up = ratio * up + buffer[d, 0]
-        for d in range(count_first):
-            down = ratio * down + buffer[d, 1]
-        return split(up * norm), split(down * norm)
-
-    pl.semaphore_wait(barrier, devices - 1)
+    def carries(buffer, t):
+        ratio, norm = weights(4, t), weights(5, t)
+        up, down = [], []
+        for g in range(groups):
+            total = buffer[t, 0, 0, window[g], :]
+            for d in range(count_first - 1, 0, -1):
+                total = ratio[g] * total + buffer[t, d, 0, window[g], :]
+            up.append(total * norm[g])
+            total = buffer[t, 0, 1, window[g], :]
+            for d in range(1, count_first):
+                total = ratio[g] * total + buffer[t, d, 1, window[g], :]
+            down.append(total * norm[g])
+        return tuple(up), tuple(down)
+
+    first = []
+    for t in range(tiles):
+        r = weights(0, t)
+        loads[t].wait()
+
+        def moments(i, j, carry):
+            up, down, total = carry
+            f = row_of(f_ref, i, t)
+            up = step_on(r, up, f)
+            down = step_on(r, down, row_of(f_ref, j, t))
+            if t == 0:
+                total = tuple(total[g] + f[g] for g in range(groups))
+            return up, down, total
+
+        up, down, total = both_ways(0, rows, moments, (zeros, zeros, zeros if t == 0 else ()))
+        store_moments(mom_one, t, up, down)
+        if t == 0:
+            whole = jnp.concatenate(total, axis=0)
+            pl.semaphore_wait(barrier, devices - 1)
+        first.append(shares(mom_one, send_one, recv_one, t))
+        for copy in first[t]:
+            copy.start()
+
     face = low_ref.shape[2]
     inner = density_ref.shape[2]
     faces = [
@@ -264,57 +315,20 @@
             ((inner - face, low_ref, 1), (0, high_ref, count_second - 1))
         )
     ]
-    first = shares(mom_one, send_one, recv_one)
-    for copy in first + faces:
-        copy.start()
-    lines[2 * rows :, :] = jnp.zeros((width - 2 * rows, wave), F32)
-    lines[2 * rows : 2 * rows + 1, :] = jnp.sum(vec_ref[2] * whole, axis=0, keepdims=True)
-    lines[2 * rows + 1 : 2 * rows + 2, :] = jnp.sum(vec_ref[3] * whole, axis=0, keepdims=True)
-    for copy in first:
-        copy.wait()
-    carry_up, carry_down = carries(mom_one)
-
-    def weighed(which, members, value):
-        total = None
-        for g in members:
-            term = weight[which, 8 * g : 8 * g + 8, :] * value[g]
-            total = term if total is None else total + term
-        return total
-
-    def up_lines(i, up):
-        f = row_of(f_ref, i)
-        up = tuple(r[g] * up[g] + f[g] for g in range(groups))
-        part[0, i] = weighed(2, even_groups, up)
-        part[1, i] = weighed(3, odd_groups, up)
-        return up
-
-    def down_lines(step, down):
-        i = rows - 1 - step
-        f = row_of(f_ref, i)
-        down = tuple(r[g] * down[g] for g in range(groups))
-        part[0, i] += weighed(2, even_groups, down)
-        part[1, i] += weighed(3, odd_groups, down)
-        return tuple(down[g] + f[g] for g in range(groups))
-
-    lax.fori_loop(0, rows, up_lines, carry_up)
-    lax.fori_loop(0, rows, down_lines, carry_down)
-    lines[:rows, :] = jnp.sum(part[0], axis=1)
-    lines[rows : 2 * rows, :] = jnp.sum(part[1], axis=1)
-    sent[...] = lines[...].T
-
-    def line_copy(o):
+
+    def line_copy(t, k):
         return pltpu.make_async_remote_copy(
-            src_ref=sent.at[pl.ds(o * chunk, chunk)],
+            src_ref=sent.at[t, pl.ds(k * chunk, chunk)],
             dst_ref=got.at[me],
-            send_sem=send_line.at[o],
+            send_sem=send_line.at[t, k],
             recv_sem=recv_line.at[me],
-            device_id=(o // count_second, lax.rem(o, count_second)),
+            device_id=(lax.rem(owner_shift(k) + t, count_first), k),
             device_id_type=mesh,
         )
 
     def line_from(d):
         return pltpu.make_async_remote_copy(
-            src_ref=sent.at[pl.ds(0, chunk)],
+            src_ref=sent.at[0, pl.ds(0, chunk)],
             dst_ref=got.at[d],
             send_sem=self_sem.at[1],
             recv_sem=recv_line.at[d],
@@ -325,53 +339,102 @@
     def back_copy(d):
         return pltpu.make_async_remote_copy(
             src_ref=answer.at[d],
-            dst_ref=back.at[pl.ds(me * chunk, chunk)],
+            dst_ref=back.at[own_tile, pl.ds(place_second * chunk, chunk)],
             send_sem=send_back.at[d],
-            recv_sem=recv_back.at[me],
+            recv_sem=recv_back.at[own_tile, place_second],
             device_id=(d // count_second, lax.rem(d, count_second)),
             device_id_type=mesh,
         )
 
-    def back_from(o):
+    def back_from(t, k):
         return pltpu.make_async_remote_copy(
             src_ref=answer.at[0],
-            dst_ref=back.at[pl.ds(o * chunk, chunk)],
+            dst_ref=back.at[t, pl.ds(k * chunk, chunk)],
             send_sem=self_sem.at[1],
-            recv_sem=recv_back.at[o],
-            device_id=(o // count_second, lax.rem(o, count_second)),
+            recv_sem=recv_back.at[t, k],
+            device_id=(lax.rem(owner_shift(k) + t, count_first), k),
             device_id_type=mesh,
         )
 
-    def over(count, action):
+    def over_devices(action):
+        def body(d, carry):
+            @pl.when(d != me)
+            def _():
+                action(d)
+
+            return carry
+
+        lax.fori_loop(0, devices, body, 0)
+
+    def over_owners(t, action):
         def body(k, carry):
-            @pl.when(k != me)
+            @pl.when((k != place_second) | (own_tile != t))
             def _():
-                action(k)
+                action(t, k)
 
             return carry
 
-        lax.fori_loop(0, count, body, 0)
-
-    over(owners, lambda o: line_copy(o).start())
-
-    @pl.when(me < owners)
+        lax.fori_loop(0, count_second, body, 0)
+
+    def weighed(values, members, state):
+        total = None
+        for g in members:
+            term = values[g] * state[g]
+            total = term if total is None else total + term
+        return total
+
+    for t in range(tiles):
+        r, even, odd = weights(0, t), weights(2, t), weights(3, t)
+        for copy in first[t]:
+            copy.wait()
+        state = carries(mom_one, t)
+
+        def lines_of(add):
+            def body(i, j, carry):
+                up, down = carry
+                up = step_on(r, up, row_of(f_ref, i, t))
+                down = tuple(r[g] * down[g] for g in range(groups))
+                for n, (values, members) in enumerate(((even, even_groups), (odd, odd_groups))):
+                    one = weighed(values, members, up)
+                    two = weighed(values, members, down)
+                    part[n, i] = part[n, i] + one if add else one
+                    part[n, j] = part[n, j] + two if add else two
+                f = row_of(f_ref, j, t)
+                return up, tuple(down[g] + f[g] for g in range(groups))
+
+            return body
+
+        state = both_ways(0, middle, lines_of(False), state)
+        both_ways(middle, rows, lines_of(True), state)
+        lines[:rows, :] = jnp.sum(part[0], axis=1)
+        lines[rows : 2 * rows, :] = jnp.sum(part[1], axis=1)
+        lines[2 * rows :, :] = jnp.zeros((width - 2 * rows, LANES), F32)
+        if t == 0:
+            for n in range(2):
+                lines[2 * rows + n : 2 * rows + n + 1, :] = jnp.sum(
+                    vec_ref[2 + n] * whole, axis=0, keepdims=True
+                )
+        sent[t] = lines[...].T
+        over_owners(t, lambda t, k: line_copy(t, k).start())
+    for copy in faces:
+        copy.start()
+
+    @pl.when(is_owner)
     def _():
         own = pltpu.make_async_copy(
-            sent.at[pl.ds(me * chunk, chunk)], got.at[me], self_sem.at[0]
+            sent.at[own_tile, pl.ds(place_second * chunk, chunk)], got.at[me], self_sem.at[0]
         )
         own.start()
-        over(devices, lambda d: line_from(d).wait_recv())
-        own.wait()
-        modes = None
+        table[...] = jnp.zeros_like(table)
         for i in range(count_first):
-            piece = got[i * count_second : (i + 1) * count_second]
-            piece = piece.reshape(count_second * chunk, width)
-            term = jnp.dot(piece, table[i], precision=HIGHEST, preferred_element_type=F32)
-            modes = term if modes is None else modes + term
-        straight = jnp.dot(mix_ref[0], modes, precision=HIGHEST, preferred_element_type=F32)
-        turned = jnp.dot(mix_ref[1], modes, precision=HIGHEST, preferred_element_type=F32)
-        s, t = straight[:, :wave], straight[:, wave:]
-        s_turned, t_turned = turned[:, :wave], turned[:, wave:]
+            for n in range(2):
+                block = basis_ref[n, i * rows : (i + 1) * rows, :]
+                table[n, i, :rows, :wave] = block
+                table[n, i, rows : 2 * rows, wave:] = block
+                for place, row in enumerate((rows * (i + 1) % wave, (rows * i - 1) % wave)):
+                    line = basis_ref[n, row : row + 1, :]
+                    table[n, i, 2 * rows + 2 + place : 2 * rows + 3 + place, :wave] = line
+                    table[n, i, 2 * rows + 4 + place : 2 * rows + 5 + place, wave:] = line
         own_eig = own_ref[...]
         lam = own_eig + eig_ref[...]
         sinh = jnp.sqrt(lam + 0.25 * lam * lam)
@@ -383,8 +446,31 @@
         half_sine = angle_ref[0]
         det = half_sine * (1.0 - square) + square
         zero = flat & (half_sine <= 0.0)
-        inverse = 1.0 / jnp.where(zero, 1.0, det)
+        inverse = jnp.where(zero, 0.0, 1.0 / jnp.where(zero, 1.0, det))
         gain = angle_ref[1] * green * inverse
+        factor[0] = gain * (2.0 + 0.5 * lam)
+        factor[1] = jnp.where(zero, 2.0 / strip, gain * (0.5 * lam))
+        factor[2] = inverse
+        factor[3] = jnp.where(zero, 1.0, 0.0)
+        over_devices(lambda d: line_from(d).wait_recv())
+        own.wait()
+        dot = lambda a, b: jnp.dot(a, b, preferred_element_type=F32)
+        modes = None
+        for i in range(count_first):
+            piece = got[i * count_second : (i + 1) * count_second]
+            high, low = halves(piece.reshape(count_second * chunk, width))
+            term = dot(high, table[0, i]) + dot(high, table[1, i]) + dot(low, table[0, i])
+            modes = term if modes is None else modes + term
+
+        def mixed(which, value):
+            high, low = halves(value)
+            stack = jnp.concatenate([high, high, low], axis=0)
+            return dot(mix_ref[which], stack)
+
+        straight = mixed(0, modes)
+        turned = mixed(1, modes)
+        s, t = straight[:, :wave], straight[:, wave:]
+        s_turned, t_turned = turned[:, :wave], turned[:, wave:]
         sums = jnp.sum(got[...], axis=0)
         lane = lax.broadcasted_iota(jnp.int32, sums.shape, 1)
         sigma = jnp.sum(jnp.where(lane == 2 * rows, sums, 0.0), axis=1, keepdims=True)
@@ -396,108 +482,121 @@
         gauge = gauge * float(1.0 / (bow[0] * np.sqrt(wave * count_second)))
         tall = lambda value: jnp.concatenate([value] * count_second, axis=0)
         mean, gauge = tall(mean), tall(gauge)
-        new_s = gain * (2.0 + 0.5 * lam) * s - t_turned * inverse
-        new_t = gain * (0.5 * lam) * t - s_turned * inverse
-        new_s = jnp.where(zero, gauge, new_s)
-        new_t = jnp.where(zero, (2.0 / strip) * t, new_t)
-        solved = jnp.concatenate([new_s, new_t], axis=1)
-        solved = jnp.dot(mix_ref[2], solved, precision=HIGHEST, preferred_element_type=F32)
+        new_s = factor[0] * s - t_turned * factor[2] + factor[3] * gauge
+        new_t = factor[1] * t - s_turned * factor[2]
+        solved = mixed(2, jnp.concatenate([new_s, new_t], axis=1))
+        high, low = halves(solved)
         wide = lax.broadcasted_iota(jnp.int32, (count_second * chunk, width), 1)
+        across = lambda a, b: lax.dot_general(
+            a, b, (((1,), (1,)), ((), ())), preferred_element_type=F32
+        )
         for i in range(count_first):
-            piece = lax.dot_general(
-                solved,
-                table[i],
-                (((1,), (1,)), ((), ())),
-                precision=HIGHEST,
-                preferred_element_type=F32,
-            )
+            piece = across(high, table[0, i]) + across(high, table[1, i]) + across(low, table[0, i])
             piece = jnp.where(wide == 2 * rows, mean, piece)
             answer[i * count_second : (i + 1) * count_second] = piece.reshape(
                 count_second, chunk, width
             )
-        over(devices, lambda d: back_copy(d).start())
+        over_devices(lambda d: back_copy(d).start())
         kept = pltpu.make_async_copy(
-            answer.at[me], back.at[pl.ds(me * chunk, chunk)], self_sem.at[0]
+            answer.at[me], back.at[own_tile, pl.ds(place_second * chunk, chunk)], self_sem.at[0]
         )
         kept.start()
         kept.wait()
 
-    over(owners, lambda o: back_from(o).wait_recv())
-    lines[...] = back[...].T
-    for n, (start, halo) in enumerate(((0, 2 * rows + 2), (rows, 2 * rows + 4))):
-        edge_ref[n, :rows, :] = lines[start : start + rows, :]
-        edge_ref[n, rows : rows + 2, :] = lines[halo : halo + 2, :]
-    mean_term = vec_ref[2] * lines[2 * rows : 2 * rows + 1, :]
-    weight[2] = mean_term
-
-    def up_second(i, up):
-        f = row_of(f_ref, i)
-        line_s = lines[pl.ds(i, 1), :]
-        line_t = lines[pl.ds(rows + i, 1), :]
-        fresh = []
+    second = []
+    for t in range(tiles):
+        over_owners(t, lambda t, k: back_from(t, k).wait_recv())
+        lines[...] = back[t].T
+        for n, (start, halo) in enumerate(((0, 2 * rows + 2), (rows, 2 * rows + 4))):
+            edge_ref[n, :rows, lane_of(t)] = lines[start : start + rows, :]
+            edge_ref[n, rows : rows + 2, lane_of(t)] = lines[halo : halo + 2, :]
+        r = weights(0, t)
+        if t == 0:
+            mean_term = vec_ref[2] * lines[2 * rows : 2 * rows + 1, :]
+            mean_term = tuple(mean_term[window[g]] for g in range(groups))
+        wide_vec = [
+            jnp.broadcast_to(vec_ref[n], (strip, LANES)) for n in range(2)
+        ]
+
+        def fresh(i):
+            f = list(row_of(f_ref, i, t))
+            line_s = lines[pl.ds(i, 1), :]
+            line_t = lines[pl.ds(rows + i, 1), :]
+            for g in range(groups):
+                if t == 0:
+                    f[g] = f[g] - mean_term[g]
+                if g in even_groups:
+                    f[g] = f[g] - wide_vec[0][window[g]] * line_s
+                if g in odd_groups:
+                    f[g] = f[g] - wide_vec[1][window[g]] * line_t
+                f_ref[i, window[g], lane_of(t)] = f[g]
+            return tuple(f)
+
+        def renewed(make):
+            def body(i, j, carry):
+                up, down = carry
+                one = fresh(i) if make else row_of(f_ref, i, t)
+                two = fresh(j) if make else row_of(f_ref, j, t)
+                return step_on(r, up, one), step_on(r, down, two)
+
+            return body
+
+        state = both_ways(0, middle, renewed(True), (zeros, zeros))
+        up, down = both_ways(middle, rows, renewed(False), state)
+        store_moments(mom_two, t, up, down)
+        second.append(shares(mom_two, send_two, recv_two, t))
+        for copy in second[t]:
+            copy.start()
+
+    stores = []
+    for t in range(tiles):
+        r, scale = weights(0, t), weights(1, t)
+        for copy in second[t]:
+            copy.wait()
+        carry_up, carry_down = carries(mom_two, t)
+
+        def put(i, value, add):
+            for g in range(groups):
+                if add:
+                    out_ref[i, window[g], lane_of(t)] = (
+                        out_ref[i, window[g], lane_of(t)] + value[g]
+                    ) * scale[g]
+                else:
+                    out_ref[i, window[g], lane_of(t)] = value[g]
+
+        def last(add):
+            def body(i, j, carry):
+                up, down = carry
+                up = step_on(r, up, row_of(f_ref, i, t))
+                down = tuple(r[g] * down[g] for g in range(groups))
+                put(i, up, add)
+                put(j, down, add)
+                f = row_of(f_ref, j, t)
+                return up, tuple(down[g] + f[g] for g in range(groups))
+
+            return body
+
+        state = both_ways(0, middle, last(False), (carry_up, carry_down))
+        up, down = both_ways(middle, rows, last(True), state)
         for g in range(groups):
-            window = slice(8 * g, 8 * g + 8)
-            value = f[g] - weight[2, window, :]
-            if g in even_groups:
-                value = value - vec_ref[0, window, :] * line_s
-            if g in odd_groups:
-                value = value - vec_ref[1, window, :] * line_t
-            held[i, window, :] = value
-            fresh.append(value)
-        return tuple(r[g] * up[g] + fresh[g] for g in range(groups))
-
-    def down_second(i, down):
-        f = row_of(held, rows - 1 - i)
-        return tuple(r[g] * down[g] + f[g] for g in range(groups))
-
-    up = lax.fori_loop(0, rows, up_second, zeros)
-    down = lax.fori_loop(0, rows, down_second, zeros)
-    for g in range(groups):
-        mom_two[0, 0, 8 * g : 8 * g + 8, :] = up[g]
-        mom_two[0, 1, 8 * g : 8 * g + 8, :] = down[g]
-    second = shares(mom_two, send_two, recv_two)
-    for copy in second:
-        copy.start()
-    over(owners, lambda o: line_copy(o).wait_send())
-
-    @pl.when(me < owners)
+            out_ref[rows, window[g], lane_of(t)] = (r[g] * up[g] + carry_down[g]) * scale[g]
+            out_ref[rows + 1, window[g], lane_of(t)] = (carry_up[g] + r[g] * down[g]) * scale[g]
+        stores.append(
+            pltpu.make_async_copy(
+                out_ref.at[:, :, lane_of(t)], out_hbm.at[:, :, lane_of(t)], out_sem.at[t]
+            )
+        )
+        stores[t].start()
+
+    for t in range(tiles):
+        over_owners(t, lambda t, k: line_copy(t, k).wait_send())
+
+    @pl.when(is_owner)
     def _():
-        over(devices, lambda d: back_copy(d).wait_send())
-
-    for copy in second:
+        over_devices(lambda d: back_copy(d).wait_send())
+
+    for copy in faces + stores:
         copy.wait()
-    carry_up, carry_down = carries(mom_two)
-
-    def up_last(i, up):
-        f = row_of(held, i)
-        up = tuple(r[g] * up[g] + f[g] for g in range(groups))
-        for g in range(groups):
-            out_ref[i, 8 * g : 8 * g + 8, :] = up[g]
-        return up
-
-    def down_last(step, down):
-        i = rows - 1 - step
-        f = row_of(held, i)
-        down = tuple(r[g] * down[g] for g in range(groups))
-        for g in range(groups):
-            window = slice(8 * g, 8 * g + 8)
-            out_ref[i, window, :] = (out_ref[i, window, :] + down[g]) * weight[1, window, :]
-        return tuple(down[g] + f[g] for g in range(groups))
-
-    up = lax.fori_loop(0, rows, up_last, carry_up)
-    down = lax.fori_loop(0, rows, down_last, carry_down)
-    for g in range(groups):
-        window = slice(8 * g, 8 * g + 8)
-        scale = weight[1, window, :]
-        out_ref[rows, window, :] = (r[g] * up[g] + carry_down[g]) * scale
-        out_ref[rows + 1, window, :] = (carry_up[g] + r[g] * down[g]) * scale
-    for copy in faces:
-        copy.wait()
-
-
-def halves(value):
-    high = value.astype(jnp.bfloat16)
-    return high, (value - high.astype(F32)).astype(jnp.bfloat16)
 
 
 def grid_values_kernel(
@@ -710,10 +809,10 @@
     count_first = lax.axis_size("px")
     count_second = lax.axis_size("py")
     devices = count_first * count_second
-    device = lax.axis_index("px") * count_second + lax.axis_index("py")
+    place_second = lax.axis_index("py")
     rows, strip, wave = root_density.shape
-    chunk = next(q for q in range(8, wave + 1, 8) if wave % q == 0 and wave // q <= devices)
-    owners = wave // chunk
+    tiles = wave // LANES
+    chunk = LANES // count_second
     width = -(-(2 * rows + 6) // 128) * 128
     basis = fourier_basis(wave)
     strip_table, strip_eig = strip_basis(strip)
@@ -731,22 +830,26 @@
             strip_table @ bow,
         ]
     )[:, :, None]
-    own = lax.rem(device, owners) * chunk
+    own_tile = lax.rem(
+        lax.axis_index("px") + 2 * devices - owner_shift(place_second), count_first
+    )
+    mix_high, mix_low = halves(jnp.asarray(mixes, F32))
+    own = jnp.minimum(own_tile, tiles - 1) * LANES + place_second * chunk
     own_eig = lax.dynamic_slice_in_dim(jnp.asarray(eig, F32), own, chunk)
     own_eig = jnp.tile(own_eig, count_second)[:, None]
     z_basis = jnp.asarray(basis, F32)
     y_basis = jnp.asarray(strip_table, F32)
     f = jnp.einsum("xyz,cz->xyc", root_density, z_basis, precision=HIGH)
     f = jnp.einsum("xyc,by->xbc", f, y_basis, precision=HIGH)
-    moment = pltpu.VMEM((count_first, 2, strip, wave), F32)
+    moment = pltpu.VMEM((tiles, count_first, 2, strip, LANES), F32)
     dma = pltpu.SemaphoreType.DMA
     face = jax.ShapeDtypeStruct(density.shape[:2] + (EDGE * CELLS,), F32)
     vmem = pl.BlockSpec(memory_space=pltpu.VMEM)
     hbm = pl.BlockSpec(memory_space=pl.ANY)
     u, edges, low_density, high_density = pl.pallas_call(
-        lambda *refs: grid_kernel((count_first, count_second, owners), *refs),
-        in_specs=[vmem] * 8 + [hbm],
-        out_specs=[vmem, vmem, hbm, hbm],
+        lambda *refs: grid_kernel((count_first, count_second), *refs),
+        in_specs=[hbm] + [vmem] * 7 + [hbm],
+        out_specs=[hbm, vmem, hbm, hbm],
         out_shape=[
             jax.ShapeDtypeStruct((rows + 2, strip, wave), F32),
             jax.ShapeDtypeStruct((2, rows + 2, wave), F32),
@@ -755,24 +858,28 @@
         ],
         scratch_shapes=[
             pltpu.VMEM((rows, strip, wave), F32),
-            pltpu.VMEM((width, wave), F32),
-            pltpu.VMEM((wave, width), F32),
+            pltpu.VMEM((rows + 2, strip, wave), F32),
+            pltpu.VMEM((width, LANES), F32),
+            pltpu.VMEM((tiles, LANES, width), F32),
             pltpu.VMEM((devices, chunk, width), F32),
             pltpu.VMEM((devices, chunk, width), F32),
-            pltpu.VMEM((wave, width), F32),
+            pltpu.VMEM((tiles, LANES, width), F32),
             moment,
             moment,
-            pltpu.VMEM((2, rows, 8, wave), F32),
-            pltpu.VMEM((count_first, width, 2 * wave), F32),
-            pltpu.VMEM((4, strip, wave), F32),
-            dma((count_first,)),
-            dma((count_first,)),
-            dma((count_first,)),
-            dma((count_first,)),
-            dma((owners,)),
+            pltpu.VMEM((2, rows, 8, LANES), F32),
+            pltpu.VMEM((2, count_first, width, 2 * wave), jnp.bfloat16),
+            pltpu.VMEM((4, count_second * chunk, wave), F32),
+            pltpu.VMEM((6, strip, wave), F32),
+            dma((tiles,)),
+            dma((tiles,)),
+            dma((tiles, count_first)),
+            dma((tiles, count_first)),
+            dma((tiles, count_first)),
+            dma((tiles, count_first)),
+            dma((tiles, count_second)),
             dma((devices,)),
             dma((devices,)),
-            dma((owners,)),
+            dma((tiles, count_second)),
             dma((2,)),
             dma((2,)),
             dma((2,)),
@@ -786,8 +893,8 @@
         jnp.asarray(eig[None, :], F32),
         own_eig,
         jnp.asarray(vectors, F32),
-        jnp.asarray(basis.T, F32),
-        jnp.asarray(mixes, F32),
+        jnp.stack(halves(jnp.asarray(basis.T, F32))),
+        jnp.concatenate([mix_high, mix_low, mix_high], axis=2),
         jnp.asarray(angles, F32),
         density,
     )

time: 135 us -> 113 us (0.84)
  Pallas kernels: 116 us -> 95.5 us
    pallas_call x1, Pallas kernels: 70.5 us -> 47.6 us  [poisson(): pl.pallas_call(lambda *refs: grid_kernel((count_first, count_second), *re...]
    pallas_call x1, Pallas kernels: 9.68 us -> 11.7 us  [poisson(): pl.pallas_call(patch_exchange_kernel, in_specs=[vmem], out_specs=vmem, ou...]
where the time goes in v3:
time: 113 us
  Pallas kernels  95.5 us (85%)
  matrix products  15.1 us (13%)
  local copies, waits for them, and re-layouts  1.49 us (1%)
    pallas_call x1, Pallas kernels, poisson(): pl.pallas_call(lambda *refs: grid_kernel((count_first, count_second), *re...  47.6 us
    pallas_call x1, Pallas kernels, local(): pl.pallas_call(subgrid_kernel, grid=(per_device,), in_specs=[smem, smem,...  19.5 us
    pallas_call x1, Pallas kernels, poisson(): pl.pallas_call(lambda *refs: grid_values_kernel(step, *refs), in_specs=[p...  16.8 us
    pallas_call x1, Pallas kernels, poisson(): pl.pallas_call(patch_exchange_kernel, in_specs=[vmem], out_specs=vmem, ou...  11.7 us
    dot_general x1, matrix products, poisson(): f = jnp.einsum('xyz,cz->xyc', root_density, z_basis, precision=HIGH)  10.2 us
    dot_general x1, matrix products, poisson(): f = jnp.einsum('xyc,by->xbc', f, y_basis, precision=HIGH)  4.89 us

profile of v3, /device:TPU:0, one launch (start us, length us, event | category | flops | bytes accessed | tf_op | source)
XLA Modules:
  0.0 112.9 jit_solution(4752059124468244753)
XLA Ops:
  0.7 0.8 dynamic_slice.3
  1.4 0.7 broadcast_in_dim_tile.4.refs_3_
  2.1 0.0 copy-start
  2.1 10.2 %fusion.5 = f32[384,96,48]{0,2,1:T(8,128)S(1)} fusion(f32[384,384,1]{1,0,2:T(8,128)} %constant.96, f32[96,48,384]{2,1,0:T(8,128)} %param.18), kind=kOutput, calls=%fused_computation.3 | convolution fusion | flops 4076863488 | bytes 14745600 | tf_op jit(solution)/shard_map/xyz,cz->xyc/dot_general | solution.py:842
  12.3 0.0 copy-done
  12.4 4.9 %fusion.2.refs_0_ = f32[96,48,384]{2,1,0:T(8,128)} fusion(f32[48,48,1]{1,0,2:T(8,128)S(1)} %copy-done, f32[384,96,48]{0,2,1:T(8,128)S(1)} %fusion.5), kind=kOutput, calls=%fused_computation.2 | convolution fusion | flops 509607936 | bytes 14164992 | tf_op jit(solution)/shard_map/xyc,by->xbc/dot_general | solution.py:843
  17.2 47.6 %shard_map.193 = (f32[98,48,384]{2,1,0:T(8,128)}, f32[2,98,384]{2,1,0:T(8,128)}, f32[8,32,128]{2,1,0:T(8,128)}, f32[8,32,128]{2,1,0:T(8,128)}) custom-call(f32[96,48,384]{2,1,0:T(8,128)} %fusion.2.refs_0_, f32[48,1]{1,0:T(8,128)} %constant.64.clone.refs_1_, f32[1,384]{1,0:T(1,128)} %constant.65.clone.refs_2_, f32[128,1]{1,0:T(8,128)} %broadcast_in_dim_tile.4.refs_3_, ...), custom_call_target="tpu_custom_call" | custom-call | tf_op jit(solution)/shard_map/pallas_call | solution.py:849
  64.9 16.8 %shard_map.194 = (f32[96,48,384]{2,1,0:T(8,128)}, f32[10,16,128]{2,1,0:T(8,128)}) custom-call(s32[3,256]{1,0:T(4,128)} %refs_0_.1, f32[98,48,384]{2,1,0:T(8,128)} %get-tuple-element.11.refs_1_, f32[2,98,384]{2,1,0:T(8,128)} %get-tuple-element.12.refs_2_, bf16[56,144]{1,0:T(8,128)(2,1)} %constant.90.refs_3_, bf16[1152,384]{1,0:T(8,128)(2,1)} %constant.95.refs_4_), custom_call_target="tpu_custom_call" | custom-call | tf_op jit(solution)/shard_map/pallas_call | solution.py:912
  81.6 11.7 %shard_map.195.own_ref.under_ref.over_ref = f32[8,3,16,128]{3,2,1,0:T(8,128)} custom-call(f32[10,16,128]{2,1,0:T(8,128)} %get-tuple-element.14.patch_ref), custom_call_target="tpu_custom_call" | custom-call | tf_op jit(solution)/shard_map/pallas_call | solution.py:927
  93.3 19.5 %shard_map.196 = (f32[8,32,1024]{2,1,0:T(8,128)}, f32[3,8,32,1024]{3,2,1,0:T(8,128)}) custom-call(s32[32]{0:T(128)} %count_ref.1, s32[2,256]{1,0:T(2,128)} %near_ref.1, f32[8,3,16,128]{3,2,1,0:T(8,128)} %shard_map.195.own_ref.under_ref.over_ref, f32[8,3,16,128]{3,2,1,0:T(8,128)} %shard_map.195.own_ref.under_ref.over_ref, ...), custom_call_target="tpu_custom_call" | custom-call | tf_op jit(solution)/shard_map/pallas_call | solution.py:953
  (1 shorter events, 0.0 us)
Async XLA Ops:
  2.1 10.2 %copy-start = (f32[48,48,1]{1,0,2:T(8,128)S(1)}, f32[48,48,1]{1,0,2:T(8,128)}, u32[]{:S(2)}) copy-start(f32[48,48,1]{1,0,2:T(8,128)} %constant.97) | copy-start | bytes 27652

commit v4 on v3

--- a/solution.py
+++ b/solution.py
@@ -120,6 +120,13 @@
 def halves(value):
     high = value.astype(jnp.bfloat16)
     return high, (value - high.astype(F32)).astype(jnp.bfloat16)
+
+
+def thirds(value):
+    high = value.astype(jnp.bfloat16)
+    rest = value - high.astype(F32)
+    middle = rest.astype(jnp.bfloat16)
+    return high, middle, (rest - middle.astype(F32)).astype(jnp.bfloat16)
 
 
 def owner_shift(place_second):
@@ -435,7 +442,8 @@
                     line = basis_ref[n, row : row + 1, :]
                     table[n, i, 2 * rows + 2 + place : 2 * rows + 3 + place, :wave] = line
                     table[n, i, 2 * rows + 4 + place : 2 * rows + 5 + place, wave:] = line
-        own_eig = own_ref[...]
+        start = own_tile * LANES + place_second * chunk
+        own_eig = jnp.concatenate([own_ref[pl.ds(start, chunk), :]] * count_second, axis=0)
         lam = own_eig + eig_ref[...]
         sinh = jnp.sqrt(lam + 0.25 * lam * lam)
         flat = lam <= 0.0
@@ -718,9 +726,7 @@
 def subgrid_kernel(
     count_ref,
     near_ref,
-    own_ref,
-    under_ref,
-    over_ref,
+    patch_ref,
     xt_ref,
     yz_ref,
     mid_ref,
@@ -729,6 +735,7 @@
     vel_ref,
     pot_ref,
     kick_ref,
+    plane_ref,
 ):
     device = lax.axis_index("px") * lax.axis_size("py") + lax.axis_index("py")
     place = pl.program_id(0)
@@ -740,19 +747,28 @@
     has_above = above >= 0
     back_below = near_ref[1, jnp.maximum(below, 0)] >= 0
     back_above = near_ref[0, jnp.maximum(above, 0)] >= 0
-    column = lax.broadcasted_iota(jnp.int32, (16, 128), 1)
-    patch = jnp.where(
-        column < PATCH,
-        pltpu.roll(under_ref[0, 0], 128 - (REG - 1) * PATCH, 1),
-        jnp.where(
-            column < (PATCH + 1) * PATCH,
-            pltpu.roll(own_ref[0, 0], PATCH, 1),
-            pltpu.roll(over_ref[0, 0], (PATCH - 1) * PATCH, 1),
-        ),
-    )
-    patch = jnp.where(column < (PATCH + 2) * PATCH, patch, 0.0)
-    planes = jnp.dot(patch, yz_ref[...], precision=HIGHEST, preferred_element_type=F32)
-    coarse = jnp.dot(xt_ref[...], planes, precision=HIGHEST, preferred_element_type=F32)
+
+    @pl.when(place == 0)
+    def _():
+        column = lax.broadcasted_iota(jnp.int32, (16, LANES), 1)
+        count = patch_ref.shape[0]
+        stack = []
+        for s in range(count):
+            own = pltpu.roll(patch_ref[s, 1], PATCH, 1)
+            under = pltpu.roll(patch_ref[(s - 1) % count, 0], LANES - (REG - 1) * PATCH, 1)
+            over = pltpu.roll(patch_ref[(s + 1) % count, 2], (PATCH - 1) * PATCH, 1)
+            patch = jnp.where(
+                column < PATCH, under, jnp.where(column < (PATCH + 1) * PATCH, own, over)
+            )
+            stack.append(jnp.where(column < (PATCH + 2) * PATCH, patch, 0.0))
+        total = None
+        for piece in thirds(jnp.concatenate(stack, axis=0)):
+            term = jnp.dot(piece, yz_ref[...], preferred_element_type=F32)
+            total = term if total is None else total + term
+        plane_ref[...] = total.reshape(plane_ref.shape)
+
+    pieces = jnp.concatenate(thirds(plane_ref[place]), axis=0)
+    coarse = jnp.dot(xt_ref[...], pieces, preferred_element_type=F32)
     start = coarse[:CELLS, :WIDE]
     x_low = coarse[CELLS : CELLS + 1, :WIDE]
     x_high = coarse[CELLS + 1 : CELLS + 2, :WIDE]
@@ -797,7 +813,7 @@
     for _ in range(SWEEPS):
         first, second, last = beside(v)
         total = first[1] + first[0] + second[1] + second[0] + last[1] + last[0]
-        new = (1.0 - RELAXATION) * v + RELAXATION * (total - rho) / 6.0
+        new = (total + (v - rho)) * (RELAXATION / 6.0)
         v = jnp.where(fixed, v, new)
     pot_ref[0] = jnp.where(live, v[:, side:end], 0.0)
     for q, (below, above) in enumerate(beside(v)):
@@ -809,7 +825,6 @@
     count_first = lax.axis_size("px")
     count_second = lax.axis_size("py")
     devices = count_first * count_second
-    place_second = lax.axis_index("py")
     rows, strip, wave = root_density.shape
     tiles = wave // LANES
     chunk = LANES // count_second
@@ -830,13 +845,7 @@
             strip_table @ bow,
         ]
     )[:, :, None]
-    own_tile = lax.rem(
-        lax.axis_index("px") + 2 * devices - owner_shift(place_second), count_first
-    )
     mix_high, mix_low = halves(jnp.asarray(mixes, F32))
-    own = jnp.minimum(own_tile, tiles - 1) * LANES + place_second * chunk
-    own_eig = lax.dynamic_slice_in_dim(jnp.asarray(eig, F32), own, chunk)
-    own_eig = jnp.tile(own_eig, count_second)[:, None]
     z_basis = jnp.asarray(basis, F32)
     y_basis = jnp.asarray(strip_table, F32)
     f = jnp.einsum("xyz,cz->xyc", root_density, z_basis, precision=HIGH)
@@ -891,7 +900,7 @@
         f,
         jnp.asarray(strip_eig[:, None], F32),
         jnp.asarray(eig[None, :], F32),
-        own_eig,
+        jnp.asarray(eig[:, None], F32),
         jnp.asarray(vectors, F32),
         jnp.stack(halves(jnp.asarray(basis.T, F32))),
         jnp.concatenate([mix_high, mix_low, mix_high], axis=2),
@@ -943,22 +952,18 @@
         root_density, subgrid_density, slot_anchor
     )
     x_table, yz_table = patch_tables()
-    count = lax.axis_size("py")
     smem = pl.BlockSpec(memory_space=pltpu.SMEM)
     slot_spec = lambda width: pl.BlockSpec((1, CELLS, width), lambda s: (s, 0, 0))
     vel_spec = pl.BlockSpec((3, 1, CELLS, inner), lambda s: (0, s, 0, 0))
-    patch_spec = lambda step: pl.BlockSpec(
-        (1, 1, 16, 128), lambda s: (lax.rem(s + step + count, count), step + 1, 0, 0)
-    )
+    x_table = jnp.asarray(np.tile(x_table, (1, 3)), jnp.bfloat16)
+    yz_table = jnp.asarray(yz_table, jnp.bfloat16)
     potential, kicked = pl.pallas_call(
         subgrid_kernel,
         grid=(per_device,),
         in_specs=[
             smem,
             smem,
-            patch_spec(0),
-            patch_spec(-1),
-            patch_spec(1),
+            pl.BlockSpec(patches.shape, lambda s: (0, 0, 0, 0)),
             pl.BlockSpec(x_table.shape, lambda s: (0, 0)),
             pl.BlockSpec(yz_table.shape, lambda s: (0, 0)),
             slot_spec(inner),
@@ -971,6 +976,7 @@
             jax.ShapeDtypeStruct(subgrid_density.shape, F32),
             jax.ShapeDtypeStruct(velocity.shape, F32),
         ],
+        scratch_shapes=[pltpu.VMEM((per_device, 16, 3 * WIDE), F32)],
         compiler_params=pltpu.CompilerParams(
             dimension_semantics=("arbitrary",), vmem_limit_bytes=60 * 1024 * 1024
         ),
@@ -978,10 +984,8 @@
         slot_count,
         neighbour,
         patches,
-        patches,
-        patches,
-        jnp.asarray(x_table),
-        jnp.asarray(yz_table),
+        x_table,
+        yz_table,
         subgrid_density,
         low_density,
         high_density,

time: 113 us -> 107 us (0.947)
  Pallas kernels: 95.5 us -> 91.1 us
  local copies, waits for them, and re-layouts: 1.49 us -> 0.01 us
    pallas_call x1, Pallas kernels: 19.5 us -> 14.9 us  [local(): pl.pallas_call(subgrid_kernel, grid=(per_device,), in_specs=[smem, smem,...]
where the time goes in v4:
time: 107 us
  Pallas kernels  91.1 us (85%)
  matrix products  15.1 us (14%)
    pallas_call x1, Pallas kernels, poisson(): pl.pallas_call(lambda *refs: grid_kernel((count_first, count_second), *re...  47.7 us
    pallas_call x1, Pallas kernels, poisson(): pl.pallas_call(lambda *refs: grid_values_kernel(step, *refs), in_specs=[p...  16.8 us
    pallas_call x1, Pallas kernels, local(): pl.pallas_call(subgrid_kernel, grid=(per_device,), in_specs=[smem, smem,...  14.9 us
    pallas_call x1, Pallas kernels, poisson(): pl.pallas_call(patch_exchange_kernel, in_specs=[vmem], out_specs=vmem, ou...  11.7 us
    dot_general x1, matrix products, poisson(): f = jnp.einsum('xyz,cz->xyc', root_density, z_basis, precision=HIGH)  10.2 us
    dot_general x1, matrix products, poisson(): f = jnp.einsum('xyc,by->xbc', f, y_basis, precision=HIGH)  4.89 us

profile of v4, /device:TPU:0, one launch (start us, length us, event | category | flops | bytes accessed | tf_op | source)
XLA Modules:
  0.0 106.8 jit_solution(8169995054252866913)
XLA Ops:
  0.6 0.0 copy-start
  0.6 10.2 %fusion.5 = f32[384,96,48]{0,2,1:T(8,128)S(1)} fusion(f32[384,384,1]{1,0,2:T(8,128)} %constant.60, f32[96,48,384]{2,1,0:T(8,128)} %param.18), kind=kOutput, calls=%fused_computation.3 | convolution fusion | flops 4076863488 | bytes 14745600 | tf_op jit(solution)/shard_map/xyz,cz->xyc/dot_general | solution.py:851
  10.8 0.0 copy-done
  10.9 4.9 %fusion.2.refs_0_ = f32[96,48,384]{2,1,0:T(8,128)} fusion(f32[48,48,1]{1,0,2:T(8,128)S(1)} %copy-done, f32[384,96,48]{0,2,1:T(8,128)S(1)} %fusion.5), kind=kOutput, calls=%fused_computation.2 | convolution fusion | flops 509607936 | bytes 14164992 | tf_op jit(solution)/shard_map/xyc,by->xbc/dot_general | solution.py:852
  15.7 47.7 %shard_map.193 = (f32[98,48,384]{2,1,0:T(8,128)}, f32[2,98,384]{2,1,0:T(8,128)}, f32[8,32,128]{2,1,0:T(8,128)}, f32[8,32,128]{2,1,0:T(8,128)}) custom-call(f32[96,48,384]{2,1,0:T(8,128)} %fusion.2.refs_0_, f32[48,1]{1,0:T(8,128)} %constant.27.clone.refs_1_, f32[1,384]{1,0:T(1,128)} %constant.28.clone.refs_2_, f32[384,1]{1,0:T(8,128)} %constant.29.clone.refs_3_, ...), custom_call_target="tpu_custom_call" | custom-call | tf_op jit(solution)/shard_map/pallas_call | solution.py:858
  63.4 16.8 %shard_map.194 = (f32[96,48,384]{2,1,0:T(8,128)}, f32[10,16,128]{2,1,0:T(8,128)}) custom-call(s32[3,256]{1,0:T(4,128)} %refs_0_.1, f32[98,48,384]{2,1,0:T(8,128)} %get-tuple-element.11.refs_1_, f32[2,98,384]{2,1,0:T(8,128)} %get-tuple-element.12.refs_2_, bf16[56,144]{1,0:T(8,128)(2,1)} %constant.54.refs_3_, bf16[1152,384]{1,0:T(8,128)(2,1)} %constant.59.refs_4_), custom_call_target="tpu_custom_call" | custom-call | tf_op jit(solution)/shard_map/pallas_call | solution.py:921
  80.2 11.7 %shard_map.195.patch_ref = f32[8,3,16,128]{3,2,1,0:T(8,128)} custom-call(f32[10,16,128]{2,1,0:T(8,128)} %get-tuple-element.14.patch_ref), custom_call_target="tpu_custom_call" | custom-call | tf_op jit(solution)/shard_map/pallas_call | solution.py:936
  92.0 14.9 %shard_map.196 = (f32[8,32,1024]{2,1,0:T(8,128)}, f32[3,8,32,1024]{3,2,1,0:T(8,128)}) custom-call(s32[32]{0:T(128)} %count_ref.1, s32[2,256]{1,0:T(2,128)} %near_ref.1, f32[8,3,16,128]{3,2,1,0:T(8,128)} %shard_map.195.patch_ref, bf16[40,48]{1,0:T(8,128)(2,1)} %constant.34.clone.xt_ref, bf16[128,3840]{1,0:T(8,128)(2,1)} %constant.35.clone.yz_ref, ...), custom_call_target="tpu_custom_call" | custom-call | tf_op jit(solution)/shard_map/pallas_call | solution.py:960
Async XLA Ops:
  0.6 10.2 %copy-start = (f32[48,48,1]{1,0,2:T(8,128)S(1)}, f32[48,48,1]{1,0,2:T(8,128)}, u32[]{:S(2)}) copy-start(f32[48,48,1]{1,0,2:T(8,128)} %constant.61) | copy-start | bytes 27652

commit v5 on v4

--- a/solution.py
+++ b/solution.py
@@ -134,11 +134,13 @@
 
 
 LANES = 128
+BLOCK = 16
 
 
 def grid_kernel(
     sizes,
-    f_hbm,
+    anchor_ref,
+    root_hbm,
     eig_b_ref,
     eig_ref,
     own_ref,
@@ -146,13 +148,21 @@
     basis_ref,
     mix_ref,
     angle_ref,
+    strip_ref,
+    unstrip_ref,
+    wave_ref,
     density_ref,
     out_hbm,
-    edge_ref,
+    arrived_ref,
     low_ref,
     high_ref,
+    edge_ref,
     f_ref,
     out_ref,
+    pair,
+    forward,
+    patches,
+    cut,
     lines,
     sent,
     got,
@@ -177,6 +187,8 @@
     self_sem,
     send_face,
     recv_face,
+    send_patch,
+    recv_patch,
 ):
     count_first, count_second = sizes
     devices = count_first * count_second
@@ -210,14 +222,27 @@
 
     lax.fori_loop(1, devices, greet, 0)
     lane_of = lambda t: slice(t * LANES, (t + 1) * LANES)
-    loads = [
-        pltpu.make_async_copy(
-            f_hbm.at[:, :, lane_of(t)], f_ref.at[:, :, lane_of(t)], in_sem.at[t]
-        )
-        for t in range(tiles)
-    ]
-    for copy in loads:
-        copy.start()
+
+    def load(n):
+        piece = pl.ds(n * BLOCK, BLOCK)
+        return pltpu.make_async_copy(root_hbm.at[piece], f_ref.at[piece], in_sem.at[n])
+
+    def store(n):
+        return pltpu.make_async_copy(
+            out_ref.at[pl.ds(n * BLOCK + 1, BLOCK)],
+            out_hbm.at[pl.ds(n * BLOCK, BLOCK)],
+            out_sem.at[n],
+        )
+
+    blocks = rows // BLOCK
+    for n in range(blocks):
+        load(n).start()
+    dot = lambda a, b: jnp.dot(a, b, preferred_element_type=F32)
+    forward[...] = jnp.zeros_like(forward)
+    for t in range(tiles):
+        forward[t, :wave, :LANES] = basis_ref[0, :, lane_of(t)]
+        forward[t, wave:, :LANES] = basis_ref[0, :, lane_of(t)]
+        forward[t, :wave, LANES:] = basis_ref[1, :, lane_of(t)]
 
     window = [slice(8 * g, 8 * g + 8) for g in range(groups)]
     even_groups = [g for g in range(groups) if 8 * g < half]
@@ -287,7 +312,26 @@
     first = []
     for t in range(tiles):
         r = weights(0, t)
-        loads[t].wait()
+
+        def transform(n, carry):
+            piece = pl.ds(n * BLOCK, BLOCK)
+            if t == 0:
+                load(n).wait()
+                high, low = halves(f_ref[piece].reshape(BLOCK * strip, wave))
+                pair[n, :, :wave] = high
+                pair[n, :, wave:] = low
+            both = dot(pair[n], forward[t])
+            value = both[:, :LANES] + both[:, LANES:]
+            for m in range(0, BLOCK, 2):
+                sides = [value[(m + q) * strip : (m + q + 1) * strip] for q in range(2)]
+                high, low = halves(jnp.concatenate(sides, axis=1))
+                stack = jnp.concatenate([high, high, low], axis=0)
+                result = dot(strip_ref[...], stack)
+                for q in range(2):
+                    f_ref[n * BLOCK + m + q, :, lane_of(t)] = result[:, lane_of(q)]
+            return carry
+
+        lax.fori_loop(0, blocks, transform, 0)
 
         def moments(i, j, carry):
             up, down, total = carry
@@ -462,7 +506,6 @@
         factor[3] = jnp.where(zero, 1.0, 0.0)
         over_devices(lambda d: line_from(d).wait_recv())
         own.wait()
-        dot = lambda a, b: jnp.dot(a, b, preferred_element_type=F32)
         modes = None
         for i in range(count_first):
             piece = got[i * count_second : (i + 1) * count_second]
@@ -512,12 +555,17 @@
         kept.wait()
 
     second = []
+    edge_ref[...] = jnp.zeros_like(edge_ref)
     for t in range(tiles):
         over_owners(t, lambda t, k: back_from(t, k).wait_recv())
         lines[...] = back[t].T
-        for n, (start, halo) in enumerate(((0, 2 * rows + 2), (rows, 2 * rows + 4))):
-            edge_ref[n, :rows, lane_of(t)] = lines[start : start + rows, :]
-            edge_ref[n, rows : rows + 2, lane_of(t)] = lines[halo : halo + 2, :]
+        after = 2 * rows + 2
+        for place, sign in ((0, -1.0), (7, 1.0)):
+            mixed_lines = 0.5 * (lines[:rows, :] + sign * lines[rows : 2 * rows, :])
+            edge_ref[1 : rows + 1, place, lane_of(t)] = mixed_lines
+            ends = 0.5 * (lines[after : after + 2, :] + sign * lines[after + 2 : after + 4, :])
+            edge_ref[rows + 1, place : place + 1, lane_of(t)] = ends[0:1]
+            edge_ref[0, place : place + 1, lane_of(t)] = ends[1:2]
         r = weights(0, t)
         if t == 0:
             mean_term = vec_ref[2] * lines[2 * rows : 2 * rows + 1, :]
@@ -556,7 +604,6 @@
         for copy in second[t]:
             copy.start()
 
-    stores = []
     for t in range(tiles):
         r, scale = weights(0, t), weights(1, t)
         for copy in second[t]:
@@ -566,11 +613,11 @@
         def put(i, value, add):
             for g in range(groups):
                 if add:
-                    out_ref[i, window[g], lane_of(t)] = (
-                        out_ref[i, window[g], lane_of(t)] + value[g]
+                    out_ref[i + 1, window[g], lane_of(t)] = (
+                        out_ref[i + 1, window[g], lane_of(t)] + value[g]
                     ) * scale[g]
                 else:
-                    out_ref[i, window[g], lane_of(t)] = value[g]
+                    out_ref[i + 1, window[g], lane_of(t)] = value[g]
 
         def last(add):
             def body(i, j, carry):
@@ -587,140 +634,109 @@
         state = both_ways(0, middle, last(False), (carry_up, carry_down))
         up, down = both_ways(middle, rows, last(True), state)
         for g in range(groups):
-            out_ref[rows, window[g], lane_of(t)] = (r[g] * up[g] + carry_down[g]) * scale[g]
-            out_ref[rows + 1, window[g], lane_of(t)] = (carry_up[g] + r[g] * down[g]) * scale[g]
-        stores.append(
-            pltpu.make_async_copy(
-                out_ref.at[:, :, lane_of(t)], out_hbm.at[:, :, lane_of(t)], out_sem.at[t]
-            )
-        )
-        stores[t].start()
-
-    for t in range(tiles):
-        over_owners(t, lambda t, k: line_copy(t, k).wait_send())
-
-    @pl.when(is_owner)
-    def _():
-        over_devices(lambda d: back_copy(d).wait_send())
-
-    for copy in faces + stores:
-        copy.wait()
-
-
-def grid_values_kernel(
-    step, anchor_ref, u_ref, edge_ref, strip_ref, wave_ref, out_ref, patch_ref, ext, cut, sems
-):
-    planes, strip, wave = u_ref.shape
-    rows = planes - 2
-    tall = ext.shape[1]
-    tiles = tall // 8
-    chunks = planes // step
-    tail = rows - (chunks - 1) * step
-    second = strip_ref.shape[0]
-    place_first = lax.axis_index("px")
-    place_second = lax.axis_index("py")
-    count = lax.axis_size("py")
-    sub = lax.broadcasted_iota(jnp.int32, (8, wave), 0)
-
-    def out_copy(c, size):
-        start = c * step
-        return pltpu.make_async_copy(
-            ext.at[pl.ds(start, size), :strip, :], out_ref.at[pl.ds(start, size)], sems.at[c]
-        )
-
-    def chunk(c, carry):
-        values = []
-        for i in range(step):
-            k = c * step + i
-            high, low = halves(u_ref[k])
-            stack = jnp.concatenate([high, high, low], axis=0)
-            value = jnp.dot(strip_ref[...], stack, preferred_element_type=F32)
-            s, t = edge_ref[0, pl.ds(k, 1), :], edge_ref[1, pl.ds(k, 1), :]
-            halo = jnp.where(sub == 0, 0.5 * (s - t), jnp.where(sub == 7, 0.5 * (s + t), 0.0))
-            values += [value[:strip], value[strip:] + halo]
-        high, low = halves(jnp.concatenate(values, axis=0))
-        wide = jnp.concatenate([high, low, high], axis=1)
-        result = jnp.dot(wide, wave_ref[...], preferred_element_type=F32)
-        ext[pl.ds(c * step, step)] = result.reshape(step, tall, wave)
-
-        @pl.when(c < chunks - 1)
-        def _():
-            out_copy(c, step).start()
-
-        return carry
-
-    lax.fori_loop(0, chunks, chunk, 0)
-    out_copy(chunks - 1, tail).start()
-    lane = lax.broadcasted_iota(jnp.int32, cut.shape[::2], 1)
+            out_ref[rows + 1, window[g], lane_of(t)] = (r[g] * up[g] + carry_down[g]) * scale[g]
+            out_ref[0, window[g], lane_of(t)] = (carry_up[g] + r[g] * down[g]) * scale[g]
+
+    tall = strip + 8
+    tall_row = lax.broadcasted_iota(jnp.int32, (24, tall), 0)
+    tall_column = lax.broadcasted_iota(jnp.int32, (24, tall), 1)
+    cell = lax.broadcasted_iota(jnp.int32, (wave, LANES), 0)
+    spot = lax.broadcasted_iota(jnp.int32, (wave, LANES), 1)
+    lane = lax.broadcasted_iota(jnp.int32, (16, LANES), 1)
     cut[...] = jnp.zeros_like(cut)
 
     def patch(t, carry):
-        slot = (place_first * count + t) * count + lax.rem(place_second - t + count, count)
+        slot = (place_first * count_second + t) * count_second + lax.rem(
+            place_second - t + count_second, count_second
+        )
         x = jnp.clip(anchor_ref[0, slot] - place_first * rows, 0, rows - REG)
         y = jnp.clip(anchor_ref[1, slot] - place_second * strip, 0, strip - REG) // 8
-        shift = lax.rem(wave + 1 - jnp.clip(anchor_ref[2, slot], 0, wave - REG), wave)
-        for i in range(REG + 2):
-            row = x - 1 + i
-            row = jnp.where(row < 0, rows + 1, row)
-            for d in range(3):
-                tile = lax.rem(y + d - 1 + tiles, tiles)
-                value = ext[row, pl.ds(pl.multiple_of(tile * 8, 8), 8), :]
-                cut[i, 8 * d : 8 * d + 8, :] = pltpu.roll(value, shift, 1)[:, :128]
+        origin = jnp.clip(anchor_ref[2, slot], 0, wave - REG) - 1 + spot
+        origin = jnp.where(origin < 0, origin + wave, origin)
+        origin = jnp.where(origin >= wave, origin - wave, origin)
+        select = jnp.where(cell == origin, 1.0, 0.0).astype(jnp.bfloat16)
+        wave_high = dot(wave_ref[0], select).astype(jnp.bfloat16)
+        wave_low = dot(wave_ref[1], select).astype(jnp.bfloat16)
+        table_top = jnp.concatenate([wave_high, wave_low], axis=1)
+        table_low = jnp.concatenate([wave_high, jnp.zeros_like(wave_low)], axis=1)
+        wanted = tall_row + 8 * y - 8
+        wanted = jnp.where(wanted < 0, wanted + tall, wanted)
+        pick = jnp.where(tall_column == wanted, 1.0, 0.0).astype(jnp.bfloat16)
+        mix = dot(pick, unstrip_ref[...]).astype(jnp.bfloat16)
+        halo_row = jnp.where(wanted[:, :1] >= strip, 1.0, 0.0)
+        values = []
+        for i in range(PATCH):
+            high, low = halves(out_ref[x + i])
+            value = dot(mix, jnp.concatenate([high, high, low], axis=0))
+            halo = jnp.concatenate([edge_ref[x + i]] * 3, axis=0)
+            values.append(value + halo * halo_row)
+        high, low = halves(jnp.concatenate(values, axis=0))
+        both = dot(high, table_top) + dot(low, table_low)
+        both = both[:, :LANES] + both[:, LANES:]
+        for i in range(PATCH):
+            cut[i] = both[24 * i : 24 * i + 24]
         total = jnp.zeros(lane.shape, F32)
         for b in range(PATCH):
             line = jnp.where(lane < PATCH, cut[:, 7 + b, :], 0.0)
             total = total + (pltpu.roll(line, PATCH * b, 1) if b else line)
-        patch_ref[t + 1] = total
+        patches[t + 1] = total
         return carry
 
-    lax.fori_loop(0, count, patch, 0)
-    patch_ref[0] = patch_ref[count]
-    patch_ref[count + 1] = patch_ref[1]
-
-    def finish(c, carry):
-        out_copy(c, step).wait()
-        return carry
-
-    lax.fori_loop(0, chunks - 1, finish, 0)
-    out_copy(chunks - 1, tail).wait()
-
-
-def patch_exchange_kernel(patch_ref, out_ref, send_sems, recv_sems, own_sem):
-    count = out_ref.shape[0]
-    place_first = lax.axis_index("px")
-    place_second = lax.axis_index("py")
-    barrier = pltpu.get_barrier_semaphore()
-    mesh = pl.DeviceIdType.MESH
-    for d in range(1, count):
-        pl.semaphore_signal(
-            barrier,
-            inc=1,
-            device_id=(place_first, lax.rem(place_second + d, count)),
-            device_id_type=mesh,
-        )
+    lax.fori_loop(0, count_second, patch, 0)
+    patches[0] = patches[count_second]
+    patches[count_second + 1] = patches[1]
     own = pltpu.make_async_copy(
-        patch_ref.at[pl.ds(place_second, 3)], out_ref.at[0], own_sem
+        patches.at[pl.ds(place_second, 3)], arrived_ref.at[0], self_sem.at[0]
     )
     own.start()
-    pl.semaphore_wait(barrier, count - 1)
-    copies = []
-    for d in range(1, count):
-        target = lax.rem(place_second + d, count)
-        copies.append(
+    moves = []
+    for d in range(1, count_second):
+        target = lax.rem(place_second + d, count_second)
+        moves.append(
             pltpu.make_async_remote_copy(
-                src_ref=patch_ref.at[pl.ds(target, 3)],
-                dst_ref=out_ref.at[count - d],
-                send_sem=send_sems.at[d],
-                recv_sem=recv_sems.at[d],
+                src_ref=patches.at[pl.ds(target, 3)],
+                dst_ref=arrived_ref.at[count_second - d],
+                send_sem=send_patch.at[d],
+                recv_sem=recv_patch.at[d],
                 device_id=(place_first, target),
                 device_id_type=mesh,
             )
         )
-    for copy in copies:
+    for copy in moves:
         copy.start()
-    own.wait()
-    for copy in copies:
+    unstrip = unstrip_ref[:strip, :]
+
+    def restore(n, carry):
+        for m in range(BLOCK):
+            row = n * BLOCK + m + 1
+            high, low = halves(out_ref[row])
+            out_ref[row] = dot(unstrip, jnp.concatenate([high, high, low], axis=0))
+        store(n).start()
+        return carry
+
+    lax.fori_loop(0, blocks, restore, 0)
+    for t in range(tiles):
+        over_owners(t, lambda t, k: line_copy(t, k).wait_send())
+
+    @pl.when(is_owner)
+    def _():
+        over_devices(lambda d: back_copy(d).wait_send())
+
+    for copy in faces + moves + [own]:
         copy.wait()
+    for n in range(blocks):
+        store(n).wait()
+
+
+def grid_values_kernel(u_ref, wave_ref, out_ref):
+    planes, strip, wave = u_ref.shape
+    high, low = halves(u_ref[...].reshape(planes * strip, wave))
+    pair = jnp.concatenate([high, low], axis=1)
+    for t in range(wave // LANES):
+        lanes = slice(t * LANES, (t + 1) * LANES)
+        both = jnp.dot(pair, wave_ref[t], preferred_element_type=F32)
+        value = both[:, :LANES] + both[:, LANES:]
+        out_ref[:, :, lanes] = value.reshape(planes, strip, LANES)
 
 
 def subgrid_kernel(
@@ -846,28 +862,38 @@
         ]
     )[:, :, None]
     mix_high, mix_low = halves(jnp.asarray(mixes, F32))
-    z_basis = jnp.asarray(basis, F32)
-    y_basis = jnp.asarray(strip_table, F32)
-    f = jnp.einsum("xyz,cz->xyc", root_density, z_basis, precision=HIGH)
-    f = jnp.einsum("xyc,by->xbc", f, y_basis, precision=HIGH)
+    wave_halves = jnp.stack(halves(jnp.asarray(basis, F32)))
+    high, low = halves(jnp.asarray(strip_table, F32))
+    strip_wide = jnp.concatenate([high, low, high], axis=1)
+    extended = np.zeros((strip + 8, strip))
+    extended[:strip] = strip_table.T
+    extended[strip] = -strip_table[:, 0]
+    extended[-1] = -strip_table[:, -1]
+    high, low = halves(jnp.asarray(extended, F32))
+    unstrip_wide = jnp.concatenate([high, low, high], axis=1)
     moment = pltpu.VMEM((tiles, count_first, 2, strip, LANES), F32)
     dma = pltpu.SemaphoreType.DMA
     face = jax.ShapeDtypeStruct(density.shape[:2] + (EDGE * CELLS,), F32)
     vmem = pl.BlockSpec(memory_space=pltpu.VMEM)
     hbm = pl.BlockSpec(memory_space=pl.ANY)
-    u, edges, low_density, high_density = pl.pallas_call(
+    uy, arrived, low_density, high_density = pl.pallas_call(
         lambda *refs: grid_kernel((count_first, count_second), *refs),
-        in_specs=[hbm] + [vmem] * 7 + [hbm],
+        in_specs=[pl.BlockSpec(memory_space=pltpu.SMEM), hbm] + [vmem] * 10 + [hbm],
         out_specs=[hbm, vmem, hbm, hbm],
         out_shape=[
-            jax.ShapeDtypeStruct((rows + 2, strip, wave), F32),
-            jax.ShapeDtypeStruct((2, rows + 2, wave), F32),
+            jax.ShapeDtypeStruct((rows, strip, wave), F32),
+            jax.ShapeDtypeStruct((count_second, 3, 16, LANES), F32),
             face,
             face,
         ],
         scratch_shapes=[
+            pltpu.VMEM((rows + 2, 8, wave), F32),
             pltpu.VMEM((rows, strip, wave), F32),
             pltpu.VMEM((rows + 2, strip, wave), F32),
+            pltpu.VMEM((rows // BLOCK, BLOCK * strip, 2 * wave), jnp.bfloat16),
+            pltpu.VMEM((tiles, 2 * wave, 2 * LANES), jnp.bfloat16),
+            pltpu.VMEM((count_second + 2, 16, LANES), F32),
+            pltpu.VMEM((16, 24, LANES), F32),
             pltpu.VMEM((width, LANES), F32),
             pltpu.VMEM((tiles, LANES, width), F32),
             pltpu.VMEM((devices, chunk, width), F32),
@@ -879,8 +905,8 @@
             pltpu.VMEM((2, count_first, width, 2 * wave), jnp.bfloat16),
             pltpu.VMEM((4, count_second * chunk, wave), F32),
             pltpu.VMEM((6, strip, wave), F32),
-            dma((tiles,)),
-            dma((tiles,)),
+            dma((rows // BLOCK,)),
+            dma((rows // BLOCK,)),
             dma((tiles, count_first)),
             dma((tiles, count_first)),
             dma((tiles, count_first)),
@@ -892,12 +918,15 @@
             dma((2,)),
             dma((2,)),
             dma((2,)),
+            dma((count_second,)),
+            dma((count_second,)),
         ],
         compiler_params=pltpu.CompilerParams(
             collective_id=1, has_side_effects=True, vmem_limit_bytes=60 * 1024 * 1024
         ),
     )(
-        f,
+        slot_anchor,
+        root_density,
         jnp.asarray(strip_eig[:, None], F32),
         jnp.asarray(eig[None, :], F32),
         jnp.asarray(eig[:, None], F32),
@@ -905,42 +934,26 @@
         jnp.stack(halves(jnp.asarray(basis.T, F32))),
         jnp.concatenate([mix_high, mix_low, mix_high], axis=2),
         jnp.asarray(angles, F32),
+        strip_wide,
+        unstrip_wide,
+        wave_halves,
         density,
     )
-    tall = strip + 8
-    step = max(n for n in range(1, 15) if (rows + 2) % n == 0)
-    extended = np.zeros((tall, strip))
-    extended[:strip] = strip_table.T
-    extended[strip] = -strip_table[:, 0]
-    extended[-1] = -strip_table[:, -1]
-    high, low = halves(jnp.asarray(extended, F32))
-    strip_wide = jnp.concatenate([high, low, high], axis=1)
-    high, low = halves(z_basis)
-    wave_tall = jnp.concatenate([high, high, low], axis=0)
-    chunks = (rows + 2) // step
-    coarse, patches = pl.pallas_call(
-        lambda *refs: grid_values_kernel(step, *refs),
-        in_specs=[pl.BlockSpec(memory_space=pltpu.SMEM)] + [vmem] * 4,
-        out_specs=[hbm, vmem],
-        out_shape=[
-            jax.ShapeDtypeStruct((rows, strip, wave), F32),
-            jax.ShapeDtypeStruct((count_second + 2, 16, 128), F32),
-        ],
-        scratch_shapes=[
-            pltpu.VMEM((rows + 2, tall, wave), F32),
-            pltpu.VMEM((16, 24, 128), F32),
-            dma((chunks,)),
-        ],
+    step = 8
+    high = wave_halves[0].reshape(wave, tiles, LANES)
+    low = wave_halves[1].reshape(wave, tiles, LANES)
+    top = jnp.concatenate([high, low], axis=2)
+    bottom = jnp.concatenate([high, jnp.zeros_like(low)], axis=2)
+    inverse = jnp.concatenate([top, bottom], axis=0).transpose(1, 0, 2)
+    block = pl.BlockSpec((step, strip, wave), lambda n: (n, 0, 0))
+    coarse = pl.pallas_call(
+        grid_values_kernel,
+        grid=(rows // step,),
+        in_specs=[block, pl.BlockSpec(inverse.shape, lambda n: (0, 0, 0))],
+        out_specs=block,
+        out_shape=jax.ShapeDtypeStruct((rows, strip, wave), F32),
         compiler_params=pltpu.CompilerParams(vmem_limit_bytes=60 * 1024 * 1024),
-    )(slot_anchor, u, edges, strip_wide, wave_tall)
-    arrived = pl.pallas_call(
-        patch_exchange_kernel,
-        in_specs=[vmem],
-        out_specs=vmem,
-        out_shape=jax.ShapeDtypeStruct((count_second, 3, 16, 128), F32),
-        scratch_shapes=[dma((count_second,)), dma((count_second,)), dma(())],
-        compiler_params=pltpu.CompilerParams(collective_id=2, has_side_effects=True),
-    )(patches)
+    )(uy, inverse)
     return coarse, arrived, low_density, high_density
 
 

time: 107 us -> 98.6 us (0.921)
  matrix products: 15.1 us -> 0 us
  Pallas kernels: 91.1 us -> 97.5 us
    pallas_call x1, Pallas kernels: 47.7 us -> 69.2 us  [poisson(): pl.pallas_call(lambda *refs: grid_kernel((count_first, count_second), *re...]
    pallas_call x2 -> x1, Pallas kernels: 28.5 us -> 13.4 us  [poisson(): pl.pallas_call(grid_values_kernel, grid=(rows // step,), in_specs=[block,...]
    dot_general x2 -> x0, matrix products: 15.1 us -> none  [the longest x1 10.2 us: poisson(): f = jnp.einsum('xyz,cz->xyc', root_density, z_basis, precision=HIGH)]
where the time goes in v5:
time: 98.6 us; the launch traced here: 98.2 us
  Pallas kernels  97.5 us (99%)
    pallas_call x1, Pallas kernels, poisson(): pl.pallas_call(lambda *refs: grid_kernel((count_first, count_second), *re...  69.2 us
    pallas_call x1, Pallas kernels, local(): pl.pallas_call(subgrid_kernel, grid=(per_device,), in_specs=[smem, smem,...  14.9 us
    pallas_call x1, Pallas kernels, poisson(): pl.pallas_call(grid_values_kernel, grid=(rows // step,), in_specs=[block,...  13.4 us

profile of v5, /device:TPU:0, one launch (start us, length us, event | category | flops | bytes accessed | tf_op | source)
XLA Modules:
  0.0 98.2 jit_solution(11428840390428504141)
XLA Ops:
  0.6 69.2 %shard_map.193 = (f32[96,48,384]{2,1,0:T(8,128)}, f32[8,3,16,128]{3,2,1,0:T(8,128)}, f32[8,32,128]{2,1,0:T(8,128)}, f32[8,32,128]{2,1,0:T(8,128)}) custom-call(s32[3,256]{1,0:T(4,128)} %refs_0_.1, f32[96,48,384]{2,1,0:T(8,128)} %refs_1_.1, f32[48,1]{1,0:T(8,128)} %constant.30.clone.refs_2_, f32[1,384]{1,0:T(1,128)} %constant.31.clone.refs_3_, ...), custom_call_target="tpu_custom_call" | custom-call | tf_op jit(solution)/shard_map/pallas_call | solution.py:879
  69.9 13.4 %shard_map.194 = f32[96,48,384]{2,1,0:T(8,128)} custom-call(f32[96,48,384]{2,1,0:T(8,128)} %get-tuple-element.9.u_ref, bf16[3,768,256]{2,1,0:T(8,128)(2,1)} %constant.76.wave_ref), custom_call_target="tpu_custom_call" | custom-call | tf_op jit(solution)/shard_map/pallas_call | solution.py:949
  83.3 14.9 %shard_map.195 = (f32[8,32,1024]{2,1,0:T(8,128)}, f32[3,8,32,1024]{3,2,1,0:T(8,128)}) custom-call(s32[32]{0:T(128)} %count_ref.1, s32[2,256]{1,0:T(2,128)} %near_ref.1, f32[8,3,16,128]{3,2,1,0:T(8,128)} %get-tuple-element.10.patch_ref, bf16[40,48]{1,0:T(8,128)(2,1)} %constant.36.clone.xt_ref, bf16[128,3840]{1,0:T(8,128)(2,1)} %constant.37.clone.yz_ref, ...), custom_call_target="tpu_custom_call" | custom-call | tf_op jit(solution)/shard_map/pallas_call | solution.py:973

commit v6 on v5

--- a/solution.py
+++ b/solution.py
@@ -15,8 +15,7 @@
 LAYERS = CELLS + 2 * EDGE
 WIDE = LAYERS * CELLS
 RELAXATION = 6.0 / 7.0
-HIGHEST = lax.Precision.HIGHEST
-HIGH = lax.Precision.HIGH
+LANES = 128
 F32 = jnp.float32
 
 
@@ -95,9 +94,16 @@
     def both(ys, zs):
         return np.einsum("jb,kc->bcjk", ys, zs).reshape(PATCH_Y * PATCH_Z, WIDE)
 
-    table = np.zeros((128, 3 * WIDE))
+    ends = both(y_edge, z_side[1:-1])
+    table = np.zeros((LANES, 2 * WIDE + 2 * LANES))
     table[: PATCH_Y * PATCH_Z] = np.concatenate(
-        [both(y_side, z_side[1:-1]), both(y_side, z_edge), both(y_edge, z_side[1:-1])], axis=1
+        [
+            both(y_side, z_side[1:-1]),
+            both(y_side, z_edge),
+            ends[:, :LANES],
+            ends[:, -LANES:],
+        ],
+        axis=1,
     )
     return x_table.astype(np.float32), table.astype(np.float32)
 
@@ -133,7 +139,6 @@
     return place_second // 2 * 2 + 2
 
 
-LANES = 128
 BLOCK = 16
 
 
@@ -728,17 +733,6 @@
         store(n).wait()
 
 
-def grid_values_kernel(u_ref, wave_ref, out_ref):
-    planes, strip, wave = u_ref.shape
-    high, low = halves(u_ref[...].reshape(planes * strip, wave))
-    pair = jnp.concatenate([high, low], axis=1)
-    for t in range(wave // LANES):
-        lanes = slice(t * LANES, (t + 1) * LANES)
-        both = jnp.dot(pair, wave_ref[t], preferred_element_type=F32)
-        value = both[:, :LANES] + both[:, LANES:]
-        out_ref[:, :, lanes] = value.reshape(planes, strip, LANES)
-
-
 def subgrid_kernel(
     count_ref,
     near_ref,
@@ -749,9 +743,16 @@
     low_ref,
     high_ref,
     vel_ref,
+    u_ref,
+    wave_ref,
     pot_ref,
     kick_ref,
+    grid_ref,
     plane_ref,
+    coarse_ref,
+    iterate,
+    steady,
+    pair,
 ):
     device = lax.axis_index("px") * lax.axis_size("py") + lax.axis_index("py")
     place = pl.program_id(0)
@@ -763,6 +764,10 @@
     has_above = above >= 0
     back_below = near_ref[1, jnp.maximum(below, 0)] >= 0
     back_above = near_ref[0, jnp.maximum(above, 0)] >= 0
+    tiles = WIDE // LANES
+    lanes = lambda g: slice(g * LANES, (g + 1) * LANES)
+    planes, strip, wave = u_ref.shape
+    dot = lambda a, b: jnp.dot(a, b, preferred_element_type=F32)
 
     @pl.when(place == 0)
     def _():
@@ -779,62 +784,109 @@
             stack.append(jnp.where(column < (PATCH + 2) * PATCH, patch, 0.0))
         total = None
         for piece in thirds(jnp.concatenate(stack, axis=0)):
-            term = jnp.dot(piece, yz_ref[...], preferred_element_type=F32)
+            term = dot(piece, yz_ref[...])
             total = term if total is None else total + term
         plane_ref[...] = total.reshape(plane_ref.shape)
 
-    pieces = jnp.concatenate(thirds(plane_ref[place]), axis=0)
-    coarse = jnp.dot(xt_ref[...], pieces, preferred_element_type=F32)
-    start = coarse[:CELLS, :WIDE]
-    x_low = coarse[CELLS : CELLS + 1, :WIDE]
-    x_high = coarse[CELLS + 1 : CELLS + 2, :WIDE]
-    z_edge = coarse[:CELLS, WIDE : 2 * WIDE]
-    y_edge = coarse[:CELLS, 2 * WIDE :]
-    shape = (CELLS, WIDE)
-    row = lax.broadcasted_iota(jnp.int32, shape, 0)
-    lane = lax.broadcasted_iota(jnp.int32, shape, 1)
-    third = lane % CELLS
-    side = EDGE * CELLS
-    end = WIDE - side
-    y_above = jnp.where(lane >= WIDE - CELLS, y_edge, pltpu.roll(start, WIDE - CELLS, 1))
-    y_below = jnp.where(lane < CELLS, y_edge, pltpu.roll(start, CELLS, 1))
-    cut_above = (lane >= WIDE - CELLS) | (
-        (lane >= side - CELLS) & (lane < side) & jnp.logical_not(back_below)
-    )
-    cut_below = (lane < CELLS) | (
-        (lane >= end) & (lane < end + CELLS) & jnp.logical_not(back_above)
-    )
-    fixed = ((lane < side) & jnp.logical_not(has_below)) | (
-        (lane >= end) & jnp.logical_not(has_above)
-    )
-    rho = jnp.concatenate([low_ref[0], mid_ref[0], high_ref[0]], axis=1) * (1.0 / (REF * REF))
-
-    def beside(v):
-        return (
-            (
-                jnp.where(row == 0, x_low, pltpu.roll(v, 1, 0)),
-                jnp.where(row == CELLS - 1, x_high, pltpu.roll(v, CELLS - 1, 0)),
-            ),
-            (
-                jnp.where(cut_below, y_below, pltpu.roll(v, CELLS, 1)),
-                jnp.where(cut_above, y_above, pltpu.roll(v, WIDE - CELLS, 1)),
-            ),
-            (
-                jnp.where(third == 0, z_edge, pltpu.roll(v, 1, 1)),
-                jnp.where(third == CELLS - 1, z_edge, pltpu.roll(v, WIDE - 1, 1)),
-            ),
-        )
-
-    v = start
-    for _ in range(SWEEPS):
-        first, second, last = beside(v)
-        total = first[1] + first[0] + second[1] + second[0] + last[1] + last[0]
-        new = (total + (v - rho)) * (RELAXATION / 6.0)
-        v = jnp.where(fixed, v, new)
-    pot_ref[0] = jnp.where(live, v[:, side:end], 0.0)
-    for q, (below, above) in enumerate(beside(v)):
-        slope = (above[:, side:end] - below[:, side:end]) * (REF / 2.0)
-        kick_ref[q, 0] = jnp.where(live, vel_ref[q, 0] - slope, 0.0)
+    coarse_ref[...] = dot(xt_ref[...], jnp.concatenate(thirds(plane_ref[place]), axis=0))
+    high, low = halves(u_ref[...].reshape(planes * strip, wave))
+    pair[:, :wave] = high
+    pair[:, wave:] = low
+
+    def restore(t):
+        both = dot(pair[...], wave_ref[t])
+        value = both[:, :LANES] + both[:, LANES:]
+        grid_ref[:, :, lanes(t)] = value.reshape(planes, strip, LANES)
+
+    lane = lax.broadcasted_iota(jnp.int32, (CELLS, LANES), 1)
+    first = lane % CELLS == 0
+    final = lane % CELLS == CELLS - 1
+    front = lane < CELLS
+    rear = lane >= LANES - CELLS
+    body = slice(8, 8 + CELLS)
+    behind = slice(7, 7 + CELLS)
+    ahead = slice(9, 9 + CELLS)
+
+    for g in range(tiles):
+        start = coarse_ref[:CELLS, lanes(g)]
+        iterate[0, g, body] = start
+        for n in range(2):
+            iterate[n, g, 7:8] = coarse_ref[CELLS : CELLS + 1, lanes(g)]
+            iterate[n, g, 8 + CELLS : 9 + CELLS] = coarse_ref[CELLS + 1 : CELLS + 2, lanes(g)]
+        if g == 0:
+            rho = low_ref[0]
+        elif g == tiles - 1:
+            rho = high_ref[0]
+        else:
+            rho = mid_ref[0, :, lanes(g - 1)]
+        steady[g] = coarse_ref[:CELLS, lanes(tiles + g)] - rho * (1.0 / (REF * REF))
+
+    def turn(value, amount):
+        return pltpu.roll(value, amount % LANES, 1)
+
+    edge_low = coarse_ref[:CELLS, lanes(2 * tiles)]
+    edge_high = coarse_ref[:CELLS, lanes(2 * tiles + 1)]
+    held_above = jnp.where(back_below, 0.0, turn(coarse_ref[:CELLS, lanes(1)], -CELLS))
+    held_below = jnp.where(back_above, 0.0, turn(coarse_ref[:CELLS, lanes(tiles - 2)], CELLS))
+
+    def second_sides(source, g):
+        value = source[g]
+        down = turn(value, CELLS)
+        up = turn(value, -CELLS)
+        if g == 0:
+            lower = edge_low
+        else:
+            lower = turn(source[g - 1], CELLS)
+            if g == tiles - 1:
+                lower = jnp.where(back_above, lower, held_below)
+        if g == tiles - 1:
+            upper = edge_high
+        else:
+            upper = turn(source[g + 1], -CELLS)
+            if g == 0:
+                upper = jnp.where(back_below, upper, held_above)
+        return jnp.where(front, lower, down), jnp.where(rear, upper, up)
+
+    for n in range(SWEEPS):
+        if n < wave // LANES:
+            restore(n)
+        now, later = n % 2, (n + 1) % 2
+        source = {}
+        for g in range(tiles):
+            for k in (g, g + 1):
+                if k < tiles and k not in source:
+                    source[k] = iterate[now, k, body]
+            value = source[g]
+            total = iterate[now, g, behind] + iterate[now, g, ahead]
+            lower, upper = second_sides(source, g)
+            total = total + (lower + upper)
+            total = total + jnp.where(first, 0.0, turn(value, 1))
+            total = total + jnp.where(final, 0.0, turn(value, -1))
+            new = (total + (value + steady[g])) * (RELAXATION / 6.0)
+            if g == 0:
+                new = jnp.where(has_below, new, value)
+            if g == tiles - 1:
+                new = jnp.where(has_above, new, value)
+            iterate[later, g, body] = new
+    for n in range(SWEEPS, wave // LANES):
+        restore(n)
+
+    now = SWEEPS % 2
+    source = {g: iterate[now, g, body] for g in range(3)}
+    for g in range(1, tiles - 1):
+        source[g + 1] = iterate[now, g + 1, body]
+        value = source[g]
+        lower, upper = second_sides(source, g)
+        edge = coarse_ref[:CELLS, lanes(tiles + g)]
+        slopes = (
+            iterate[now, g, ahead] - iterate[now, g, behind],
+            upper - lower,
+            jnp.where(final, edge, turn(value, -1)) - jnp.where(first, edge, turn(value, 1)),
+        )
+        pot_ref[0, :, lanes(g - 1)] = jnp.where(live, value, 0.0)
+        for q, slope in enumerate(slopes):
+            moved = vel_ref[q, 0, :, lanes(g - 1)] - slope * (REF / 2.0)
+            kick_ref[q, 0, :, lanes(g - 1)] = jnp.where(live, moved, 0.0)
 
 
 def poisson(root_density, density, slot_anchor):
@@ -939,29 +991,19 @@
         wave_halves,
         density,
     )
-    step = 8
     high = wave_halves[0].reshape(wave, tiles, LANES)
     low = wave_halves[1].reshape(wave, tiles, LANES)
     top = jnp.concatenate([high, low], axis=2)
     bottom = jnp.concatenate([high, jnp.zeros_like(low)], axis=2)
     inverse = jnp.concatenate([top, bottom], axis=0).transpose(1, 0, 2)
-    block = pl.BlockSpec((step, strip, wave), lambda n: (n, 0, 0))
-    coarse = pl.pallas_call(
-        grid_values_kernel,
-        grid=(rows // step,),
-        in_specs=[block, pl.BlockSpec(inverse.shape, lambda n: (0, 0, 0))],
-        out_specs=block,
-        out_shape=jax.ShapeDtypeStruct((rows, strip, wave), F32),
-        compiler_params=pltpu.CompilerParams(vmem_limit_bytes=60 * 1024 * 1024),
-    )(uy, inverse)
-    return coarse, arrived, low_density, high_density
+    return uy, inverse, arrived, low_density, high_density
 
 
 def local(root_density, subgrid_density, velocity, slot_anchor, slot_count, neighbour):
     per_device = subgrid_density.shape[0]
     side = EDGE * CELLS
     inner = CELLS * CELLS
-    coarse_potential, patches, low_density, high_density = poisson(
+    uy, inverse, patches, low_density, high_density = poisson(
         root_density, subgrid_density, slot_anchor
     )
     x_table, yz_table = patch_tables()
@@ -970,7 +1012,11 @@
     vel_spec = pl.BlockSpec((3, 1, CELLS, inner), lambda s: (0, s, 0, 0))
     x_table = jnp.asarray(np.tile(x_table, (1, 3)), jnp.bfloat16)
     yz_table = jnp.asarray(yz_table, jnp.bfloat16)
-    potential, kicked = pl.pallas_call(
+    columns = yz_table.shape[1]
+    planes, strip, wave = uy.shape
+    planes //= per_device
+    grid_spec = pl.BlockSpec((planes, strip, wave), lambda s: (s, 0, 0))
+    potential, kicked, coarse_potential = pl.pallas_call(
         subgrid_kernel,
         grid=(per_device,),
         in_specs=[
@@ -983,13 +1029,22 @@
             slot_spec(side),
             slot_spec(side),
             vel_spec,
+            grid_spec,
+            pl.BlockSpec(inverse.shape, lambda s: (0, 0, 0)),
         ],
-        out_specs=[slot_spec(inner), vel_spec],
+        out_specs=[slot_spec(inner), vel_spec, grid_spec],
         out_shape=[
             jax.ShapeDtypeStruct(subgrid_density.shape, F32),
             jax.ShapeDtypeStruct(velocity.shape, F32),
+            jax.ShapeDtypeStruct(uy.shape, F32),
         ],
-        scratch_shapes=[pltpu.VMEM((per_device, 16, 3 * WIDE), F32)],
+        scratch_shapes=[
+            pltpu.VMEM((per_device, 16, columns), F32),
+            pltpu.VMEM((CELLS + 8, columns), F32),
+            pltpu.VMEM((2, WIDE // LANES, CELLS + 16, LANES), F32),
+            pltpu.VMEM((WIDE // LANES, CELLS, LANES), F32),
+            pltpu.VMEM((planes * strip, 2 * wave), jnp.bfloat16),
+        ],
         compiler_params=pltpu.CompilerParams(
             dimension_semantics=("arbitrary",), vmem_limit_bytes=60 * 1024 * 1024
         ),
@@ -1003,6 +1058,8 @@
         low_density,
         high_density,
         velocity,
+        uy,
+        inverse,
     )
     return (coarse_potential, potential, kicked)
 

time: 98.6 us -> 85.8 us (0.87)
  Pallas kernels: 97.5 us -> 84.8 us
    pallas_call x1 -> x0, Pallas kernels: 13.4 us -> none  [poisson(): pl.pallas_call(grid_values_kernel, grid=(rows // step,), in_specs=[block,...]
where the time goes in v6:
time: 85.8 us; the launch traced here: 85.5 us
  Pallas kernels  84.8 us (99%)
    pallas_call x1, Pallas kernels, poisson(): pl.pallas_call(lambda *refs: grid_kernel((count_first, count_second), *re...  69.2 us
    pallas_call x1, Pallas kernels, local(): pl.pallas_call(subgrid_kernel, grid=(per_device,), in_specs=[smem, smem,...  15.6 us

profile of v6, /device:TPU:0, one launch (start us, length us, event | category | flops | bytes accessed | tf_op | source)
XLA Modules:
  0.0 85.5 jit_solution(10492656767704389971)
XLA Ops:
  0.6 69.2 %shard_map.193 = (f32[96,48,384]{2,1,0:T(8,128)}, f32[8,3,16,128]{3,2,1,0:T(8,128)}, f32[8,32,128]{2,1,0:T(8,128)}, f32[8,32,128]{2,1,0:T(8,128)}) custom-call(s32[3,256]{1,0:T(4,128)} %refs_0_.1, f32[96,48,384]{2,1,0:T(8,128)} %refs_1_.1, f32[48,1]{1,0:T(8,128)} %constant.30.clone.refs_2_, f32[1,384]{1,0:T(1,128)} %constant.31.clone.refs_3_, ...), custom_call_target="tpu_custom_call" | custom-call | tf_op jit(solution)/shard_map/pallas_call | solution.py:931
  69.9 15.6 %shard_map.194 = (f32[8,32,1024]{2,1,0:T(8,128)}, f32[3,8,32,1024]{3,2,1,0:T(8,128)}, f32[96,48,384]{2,1,0:T(8,128)}) custom-call(s32[32]{0:T(128)} %count_ref.1, s32[2,256]{1,0:T(2,128)} %near_ref.1, f32[8,3,16,128]{3,2,1,0:T(8,128)} %get-tuple-element.10.patch_ref, bf16[40,48]{1,0:T(8,128)(2,1)} %constant.36.clone.xt_ref, ...), custom_call_target="tpu_custom_call" | custom-call | tf_op jit(solution)/shard_map/pallas_call | solution.py:1019

commit v7 on v6

--- a/solution.py
+++ b/solution.py
@@ -139,7 +139,7 @@
     return place_second // 2 * 2 + 2
 
 
-BLOCK = 16
+BLOCKS = 6
 
 
 def grid_kernel(
@@ -168,6 +168,9 @@
     forward,
     patches,
     cut,
+    windows,
+    strip_mix,
+    halo_rows,
     lines,
     sent,
     got,
@@ -215,6 +218,23 @@
     is_owner = own_tile < tiles
     barrier = pltpu.get_barrier_semaphore()
 
+    lane_of = lambda t: slice(t * LANES, (t + 1) * LANES)
+
+    block = rows // BLOCKS
+
+    def load(n):
+        piece = pl.ds(n * block, block)
+        return pltpu.make_async_copy(root_hbm.at[piece], f_ref.at[piece], in_sem.at[n])
+
+    def store(n):
+        return pltpu.make_async_copy(
+            out_ref.at[pl.ds(n * block + 1, block)],
+            out_hbm.at[pl.ds(n * block, block)],
+            out_sem.at[n],
+        )
+
+    for n in range(BLOCKS):
+        load(n).start()
     def greet(step, carry):
         other = lax.rem(me + step, devices)
         pl.semaphore_signal(
@@ -226,22 +246,6 @@
         return carry
 
     lax.fori_loop(1, devices, greet, 0)
-    lane_of = lambda t: slice(t * LANES, (t + 1) * LANES)
-
-    def load(n):
-        piece = pl.ds(n * BLOCK, BLOCK)
-        return pltpu.make_async_copy(root_hbm.at[piece], f_ref.at[piece], in_sem.at[n])
-
-    def store(n):
-        return pltpu.make_async_copy(
-            out_ref.at[pl.ds(n * BLOCK + 1, BLOCK)],
-            out_hbm.at[pl.ds(n * BLOCK, BLOCK)],
-            out_sem.at[n],
-        )
-
-    blocks = rows // BLOCK
-    for n in range(blocks):
-        load(n).start()
     dot = lambda a, b: jnp.dot(a, b, preferred_element_type=F32)
     forward[...] = jnp.zeros_like(forward)
     for t in range(tiles):
@@ -315,28 +319,33 @@
         return tuple(up), tuple(down)
 
     first = []
-    for t in range(tiles):
+    whole = []
+
+    def open_tile(t):
         r = weights(0, t)
+        span = (2 if t == 0 else 3) * block
 
         def transform(n, carry):
-            piece = pl.ds(n * BLOCK, BLOCK)
+            piece = pl.ds(n * span, span)
+            spread = pl.ds(pl.multiple_of(n * span * strip, 8), span * strip)
             if t == 0:
-                load(n).wait()
-                high, low = halves(f_ref[piece].reshape(BLOCK * strip, wave))
-                pair[n, :, :wave] = high
-                pair[n, :, wave:] = low
-            both = dot(pair[n], forward[t])
+                for m in range(span // block):
+                    load(n * (span // block) + m).wait()
+                high, low = halves(f_ref[piece].reshape(span * strip, wave))
+                pair[spread, :wave] = high
+                pair[spread, wave:] = low
+            both = dot(pair[spread], forward[t])
             value = both[:, :LANES] + both[:, LANES:]
-            for m in range(0, BLOCK, 2):
+            for m in range(0, span, 2):
                 sides = [value[(m + q) * strip : (m + q + 1) * strip] for q in range(2)]
                 high, low = halves(jnp.concatenate(sides, axis=1))
                 stack = jnp.concatenate([high, high, low], axis=0)
                 result = dot(strip_ref[...], stack)
                 for q in range(2):
-                    f_ref[n * BLOCK + m + q, :, lane_of(t)] = result[:, lane_of(q)]
+                    f_ref[n * span + m + q, :, lane_of(t)] = result[:, lane_of(q)]
             return carry
 
-        lax.fori_loop(0, blocks, transform, 0)
+        lax.fori_loop(0, rows // span, transform, 0)
 
         def moments(i, j, carry):
             up, down, total = carry
@@ -350,7 +359,7 @@
         up, down, total = both_ways(0, rows, moments, (zeros, zeros, zeros if t == 0 else ()))
         store_moments(mom_one, t, up, down)
         if t == 0:
-            whole = jnp.concatenate(total, axis=0)
+            whole.append(jnp.concatenate(total, axis=0))
             pl.semaphore_wait(barrier, devices - 1)
         first.append(shares(mom_one, send_one, recv_one, t))
         for copy in first[t]:
@@ -412,7 +421,7 @@
             device_id_type=mesh,
         )
 
-    def over_devices(action):
+    def over_devices(action, part=None):
         def body(d, carry):
             @pl.when(d != me)
             def _():
@@ -420,7 +429,10 @@
 
             return carry
 
-        lax.fori_loop(0, devices, body, 0)
+        start, stop = 0, devices
+        if part is not None:
+            start, stop = part * count_second, (part + 1) * count_second
+        lax.fori_loop(start, stop, body, 0)
 
     def over_owners(t, action):
         def body(k, carry):
@@ -439,7 +451,7 @@
             total = term if total is None else total + term
         return total
 
-    for t in range(tiles):
+    def close_tile(t):
         r, even, odd = weights(0, t), weights(2, t), weights(3, t)
         for copy in first[t]:
             copy.wait()
@@ -468,10 +480,17 @@
         if t == 0:
             for n in range(2):
                 lines[2 * rows + n : 2 * rows + n + 1, :] = jnp.sum(
-                    vec_ref[2 + n] * whole, axis=0, keepdims=True
+                    vec_ref[2 + n] * whole[0], axis=0, keepdims=True
                 )
         sent[t] = lines[...].T
         over_owners(t, lambda t, k: line_copy(t, k).start())
+
+    for t in range(tiles):
+        open_tile(t)
+        if t > 0 and t < tiles - 1:
+            close_tile(t - 1)
+    for t in range(max(tiles - 2, 0), tiles):
+        close_tile(t)
     for copy in faces:
         copy.start()
 
@@ -509,10 +528,10 @@
         factor[1] = jnp.where(zero, 2.0 / strip, gain * (0.5 * lam))
         factor[2] = inverse
         factor[3] = jnp.where(zero, 1.0, 0.0)
-        over_devices(lambda d: line_from(d).wait_recv())
+        modes = None
         own.wait()
-        modes = None
         for i in range(count_first):
+            over_devices(lambda d: line_from(d).wait_recv(), i)
             piece = got[i * count_second : (i + 1) * count_second]
             high, low = halves(piece.reshape(count_second * chunk, width))
             term = dot(high, table[0, i]) + dot(high, table[1, i]) + dot(low, table[0, i])
@@ -552,13 +571,51 @@
             answer[i * count_second : (i + 1) * count_second] = piece.reshape(
                 count_second, chunk, width
             )
-        over_devices(lambda d: back_copy(d).start())
+            over_devices(lambda d: back_copy(d).start(), i)
         kept = pltpu.make_async_copy(
             answer.at[me], back.at[own_tile, pl.ds(place_second * chunk, chunk)], self_sem.at[0]
         )
         kept.start()
         kept.wait()
 
+    tall = strip + 8
+    tall_row = lax.broadcasted_iota(jnp.int32, (24, tall), 0)
+    tall_column = lax.broadcasted_iota(jnp.int32, (24, tall), 1)
+    cell = lax.broadcasted_iota(jnp.int32, (wave, LANES), 0)
+    spot = lax.broadcasted_iota(jnp.int32, (wave, LANES), 1)
+    lane = lax.broadcasted_iota(jnp.int32, (16, LANES), 1)
+    cut[...] = jnp.zeros_like(cut)
+
+
+    def corner(t):
+        slot = (place_first * count_second + t) * count_second + lax.rem(
+            place_second - t + count_second, count_second
+        )
+        x = jnp.clip(anchor_ref[0, slot] - place_first * rows, 0, rows - REG)
+        return x, slot
+
+    def prepare(t, carry):
+        _, slot = corner(t)
+        y = jnp.clip(anchor_ref[1, slot] - place_second * strip, 0, strip - REG) // 8
+        origin = jnp.clip(anchor_ref[2, slot], 0, wave - REG) - 1 + spot
+        origin = jnp.where(origin < 0, origin + wave, origin)
+        origin = jnp.where(origin >= wave, origin - wave, origin)
+        select = jnp.where(cell == origin, 1.0, 0.0).astype(jnp.bfloat16)
+        wave_high = dot(wave_ref[0], select).astype(jnp.bfloat16)
+        windows[t, :wave, :LANES] = wave_high
+        windows[t, wave:, :LANES] = wave_high
+        windows[t, :wave, LANES:] = dot(wave_ref[1], select).astype(jnp.bfloat16)
+        windows[t, wave:, LANES:] = jnp.zeros((wave, LANES), jnp.bfloat16)
+        wanted = tall_row + 8 * y - 8
+        wanted = jnp.where(wanted < 0, wanted + tall, wanted)
+        pick = jnp.where(tall_column == wanted, 1.0, 0.0).astype(jnp.bfloat16)
+        strip_mix[t] = dot(pick, unstrip_ref[...]).astype(jnp.bfloat16)
+        halo_rows[t] = jnp.broadcast_to(
+            jnp.where(wanted[:, :1] >= strip, 1.0, 0.0), halo_rows.shape[1:]
+        )
+        return carry
+
+    lax.fori_loop(0, count_second, prepare, 0)
     second = []
     edge_ref[...] = jnp.zeros_like(edge_ref)
     for t in range(tiles):
@@ -642,52 +699,33 @@
             out_ref[rows + 1, window[g], lane_of(t)] = (r[g] * up[g] + carry_down[g]) * scale[g]
             out_ref[0, window[g], lane_of(t)] = (carry_up[g] + r[g] * down[g]) * scale[g]
 
-    tall = strip + 8
-    tall_row = lax.broadcasted_iota(jnp.int32, (24, tall), 0)
-    tall_column = lax.broadcasted_iota(jnp.int32, (24, tall), 1)
-    cell = lax.broadcasted_iota(jnp.int32, (wave, LANES), 0)
-    spot = lax.broadcasted_iota(jnp.int32, (wave, LANES), 1)
-    lane = lax.broadcasted_iota(jnp.int32, (16, LANES), 1)
-    cut[...] = jnp.zeros_like(cut)
-
-    def patch(t, carry):
-        slot = (place_first * count_second + t) * count_second + lax.rem(
-            place_second - t + count_second, count_second
-        )
-        x = jnp.clip(anchor_ref[0, slot] - place_first * rows, 0, rows - REG)
-        y = jnp.clip(anchor_ref[1, slot] - place_second * strip, 0, strip - REG) // 8
-        origin = jnp.clip(anchor_ref[2, slot], 0, wave - REG) - 1 + spot
-        origin = jnp.where(origin < 0, origin + wave, origin)
-        origin = jnp.where(origin >= wave, origin - wave, origin)
-        select = jnp.where(cell == origin, 1.0, 0.0).astype(jnp.bfloat16)
-        wave_high = dot(wave_ref[0], select).astype(jnp.bfloat16)
-        wave_low = dot(wave_ref[1], select).astype(jnp.bfloat16)
-        table_top = jnp.concatenate([wave_high, wave_low], axis=1)
-        table_low = jnp.concatenate([wave_high, jnp.zeros_like(wave_low)], axis=1)
-        wanted = tall_row + 8 * y - 8
-        wanted = jnp.where(wanted < 0, wanted + tall, wanted)
-        pick = jnp.where(tall_column == wanted, 1.0, 0.0).astype(jnp.bfloat16)
-        mix = dot(pick, unstrip_ref[...]).astype(jnp.bfloat16)
-        halo_row = jnp.where(wanted[:, :1] >= strip, 1.0, 0.0)
+    def patch(t):
+        x, _ = corner(t)
+        mix, halo_row = strip_mix[t], halo_rows[t]
         values = []
         for i in range(PATCH):
             high, low = halves(out_ref[x + i])
             value = dot(mix, jnp.concatenate([high, high, low], axis=0))
             halo = jnp.concatenate([edge_ref[x + i]] * 3, axis=0)
-            values.append(value + halo * halo_row)
+            values.append(value + halo * halo_row[:, :1])
         high, low = halves(jnp.concatenate(values, axis=0))
-        both = dot(high, table_top) + dot(low, table_low)
+        both = dot(jnp.concatenate([high, low], axis=1), windows[t])
         both = both[:, :LANES] + both[:, LANES:]
         for i in range(PATCH):
-            cut[i] = both[24 * i : 24 * i + 24]
+            cut[t, i] = both[24 * i : 24 * i + 24]
         total = jnp.zeros(lane.shape, F32)
         for b in range(PATCH):
-            line = jnp.where(lane < PATCH, cut[:, 7 + b, :], 0.0)
+            line = jnp.where(lane < PATCH, cut[t, :, 7 + b, :], 0.0)
             total = total + (pltpu.roll(line, PATCH * b, 1) if b else line)
-        patches[t + 1] = total
+        return total
+
+    def patch_pair(n, carry):
+        totals = [patch(2 * n + q) for q in range(2)]
+        for q in range(2):
+            patches[2 * n + q + 1] = totals[q]
         return carry
 
-    lax.fori_loop(0, count_second, patch, 0)
+    lax.fori_loop(0, count_second // 2, patch_pair, 0)
     patches[0] = patches[count_second]
     patches[count_second + 1] = patches[1]
     own = pltpu.make_async_copy(
@@ -712,14 +750,14 @@
     unstrip = unstrip_ref[:strip, :]
 
     def restore(n, carry):
-        for m in range(BLOCK):
-            row = n * BLOCK + m + 1
+        for m in range(block):
+            row = n * block + m + 1
             high, low = halves(out_ref[row])
             out_ref[row] = dot(unstrip, jnp.concatenate([high, high, low], axis=0))
         store(n).start()
         return carry
 
-    lax.fori_loop(0, blocks, restore, 0)
+    lax.fori_loop(0, BLOCKS, restore, 0)
     for t in range(tiles):
         over_owners(t, lambda t, k: line_copy(t, k).wait_send())
 
@@ -729,7 +767,7 @@
 
     for copy in faces + moves + [own]:
         copy.wait()
-    for n in range(blocks):
+    for n in range(BLOCKS):
         store(n).wait()
 
 
@@ -942,10 +980,13 @@
             pltpu.VMEM((rows + 2, 8, wave), F32),
             pltpu.VMEM((rows, strip, wave), F32),
             pltpu.VMEM((rows + 2, strip, wave), F32),
-            pltpu.VMEM((rows // BLOCK, BLOCK * strip, 2 * wave), jnp.bfloat16),
+            pltpu.VMEM((rows * strip, 2 * wave), jnp.bfloat16),
             pltpu.VMEM((tiles, 2 * wave, 2 * LANES), jnp.bfloat16),
             pltpu.VMEM((count_second + 2, 16, LANES), F32),
-            pltpu.VMEM((16, 24, LANES), F32),
+            pltpu.VMEM((count_second, 16, 24, LANES), F32),
+            pltpu.VMEM((count_second, 2 * wave, 2 * LANES), jnp.bfloat16),
+            pltpu.VMEM((count_second, 24, 3 * strip), jnp.bfloat16),
+            pltpu.VMEM((count_second, 24, LANES), F32),
             pltpu.VMEM((width, LANES), F32),
             pltpu.VMEM((tiles, LANES, width), F32),
             pltpu.VMEM((devices, chunk, width), F32),
@@ -957,8 +998,8 @@
             pltpu.VMEM((2, count_first, width, 2 * wave), jnp.bfloat16),
             pltpu.VMEM((4, count_second * chunk, wave), F32),
             pltpu.VMEM((6, strip, wave), F32),
-            dma((rows // BLOCK,)),
-            dma((rows // BLOCK,)),
+            dma((BLOCKS,)),
+            dma((BLOCKS,)),
             dma((tiles, count_first)),
             dma((tiles, count_first)),
             dma((tiles, count_first)),

time: 85.8 us -> 79.6 us (0.928)
  Pallas kernels: 84.8 us -> 78.6 us
    pallas_call x1, Pallas kernels: 69.2 us -> 63 us  [poisson(): pl.pallas_call(lambda *refs: grid_kernel((count_first, count_second), *re...]
where the time goes in v7:
time: 79.6 us; the launch traced here: 79.2 us
  Pallas kernels  78.6 us (99%)
    pallas_call x1, Pallas kernels, poisson(): pl.pallas_call(lambda *refs: grid_kernel((count_first, count_second), *re...  63 us
    pallas_call x1, Pallas kernels, local(): pl.pallas_call(subgrid_kernel, grid=(per_device,), in_specs=[smem, smem,...  15.6 us

profile of v7, /device:TPU:0, one launch (start us, length us, event | category | flops | bytes accessed | tf_op | source)
XLA Modules:
  0.0 79.2 jit_solution(10564571965795392922)
XLA Ops:
  0.6 63.0 %shard_map.193 = (f32[96,48,384]{2,1,0:T(8,128)}, f32[8,3,16,128]{3,2,1,0:T(8,128)}, f32[8,32,128]{2,1,0:T(8,128)}, f32[8,32,128]{2,1,0:T(8,128)}) custom-call(s32[3,256]{1,0:T(4,128)} %refs_0_.1, f32[96,48,384]{2,1,0:T(8,128)} %refs_1_.1, f32[48,1]{1,0:T(8,128)} %constant.30.clone.refs_2_, f32[1,384]{1,0:T(1,128)} %constant.31.clone.refs_3_, ...), custom_call_target="tpu_custom_call" | custom-call | tf_op jit(solution)/shard_map/pallas_call | solution.py:969
  63.6 15.6 %shard_map.194 = (f32[8,32,1024]{2,1,0:T(8,128)}, f32[3,8,32,1024]{3,2,1,0:T(8,128)}, f32[96,48,384]{2,1,0:T(8,128)}) custom-call(s32[32]{0:T(128)} %count_ref.1, s32[2,256]{1,0:T(2,128)} %near_ref.1, f32[8,3,16,128]{3,2,1,0:T(8,128)} %get-tuple-element.10.patch_ref, bf16[40,48]{1,0:T(8,128)(2,1)} %constant.36.clone.xt_ref, ...), custom_call_target="tpu_custom_call" | custom-call | tf_op jit(solution)/shard_map/pallas_call | solution.py:1060

commit v8 on v7

--- a/solution.py
+++ b/solution.py
@@ -318,53 +318,6 @@
             down.append(total * norm[g])
         return tuple(up), tuple(down)
 
-    first = []
-    whole = []
-
-    def open_tile(t):
-        r = weights(0, t)
-        span = (2 if t == 0 else 3) * block
-
-        def transform(n, carry):
-            piece = pl.ds(n * span, span)
-            spread = pl.ds(pl.multiple_of(n * span * strip, 8), span * strip)
-            if t == 0:
-                for m in range(span // block):
-                    load(n * (span // block) + m).wait()
-                high, low = halves(f_ref[piece].reshape(span * strip, wave))
-                pair[spread, :wave] = high
-                pair[spread, wave:] = low
-            both = dot(pair[spread], forward[t])
-            value = both[:, :LANES] + both[:, LANES:]
-            for m in range(0, span, 2):
-                sides = [value[(m + q) * strip : (m + q + 1) * strip] for q in range(2)]
-                high, low = halves(jnp.concatenate(sides, axis=1))
-                stack = jnp.concatenate([high, high, low], axis=0)
-                result = dot(strip_ref[...], stack)
-                for q in range(2):
-                    f_ref[n * span + m + q, :, lane_of(t)] = result[:, lane_of(q)]
-            return carry
-
-        lax.fori_loop(0, rows // span, transform, 0)
-
-        def moments(i, j, carry):
-            up, down, total = carry
-            f = row_of(f_ref, i, t)
-            up = step_on(r, up, f)
-            down = step_on(r, down, row_of(f_ref, j, t))
-            if t == 0:
-                total = tuple(total[g] + f[g] for g in range(groups))
-            return up, down, total
-
-        up, down, total = both_ways(0, rows, moments, (zeros, zeros, zeros if t == 0 else ()))
-        store_moments(mom_one, t, up, down)
-        if t == 0:
-            whole.append(jnp.concatenate(total, axis=0))
-            pl.semaphore_wait(barrier, devices - 1)
-        first.append(shares(mom_one, send_one, recv_one, t))
-        for copy in first[t]:
-            copy.start()
-
     face = low_ref.shape[2]
     inner = density_ref.shape[2]
     faces = [
@@ -381,125 +334,46 @@
         )
     ]
 
-    def line_copy(t, k):
-        return pltpu.make_async_remote_copy(
-            src_ref=sent.at[t, pl.ds(k * chunk, chunk)],
-            dst_ref=got.at[me],
-            send_sem=send_line.at[t, k],
-            recv_sem=recv_line.at[me],
-            device_id=(lax.rem(owner_shift(k) + t, count_first), k),
-            device_id_type=mesh,
-        )
-
-    def line_from(d):
-        return pltpu.make_async_remote_copy(
-            src_ref=sent.at[0, pl.ds(0, chunk)],
-            dst_ref=got.at[d],
-            send_sem=self_sem.at[1],
-            recv_sem=recv_line.at[d],
-            device_id=(d // count_second, lax.rem(d, count_second)),
-            device_id_type=mesh,
-        )
-
-    def back_copy(d):
-        return pltpu.make_async_remote_copy(
-            src_ref=answer.at[d],
-            dst_ref=back.at[own_tile, pl.ds(place_second * chunk, chunk)],
-            send_sem=send_back.at[d],
-            recv_sem=recv_back.at[own_tile, place_second],
-            device_id=(d // count_second, lax.rem(d, count_second)),
-            device_id_type=mesh,
-        )
-
-    def back_from(t, k):
-        return pltpu.make_async_remote_copy(
-            src_ref=answer.at[0],
-            dst_ref=back.at[t, pl.ds(k * chunk, chunk)],
-            send_sem=self_sem.at[1],
-            recv_sem=recv_back.at[t, k],
-            device_id=(lax.rem(owner_shift(k) + t, count_first), k),
-            device_id_type=mesh,
-        )
-
-    def over_devices(action, part=None):
-        def body(d, carry):
-            @pl.when(d != me)
-            def _():
-                action(d)
-
-            return carry
-
-        start, stop = 0, devices
-        if part is not None:
-            start, stop = part * count_second, (part + 1) * count_second
-        lax.fori_loop(start, stop, body, 0)
-
-    def over_owners(t, action):
-        def body(k, carry):
-            @pl.when((k != place_second) | (own_tile != t))
-            def _():
-                action(t, k)
-
-            return carry
-
-        lax.fori_loop(0, count_second, body, 0)
-
-    def weighed(values, members, state):
-        total = None
-        for g in members:
-            term = values[g] * state[g]
-            total = term if total is None else total + term
-        return total
-
-    def close_tile(t):
-        r, even, odd = weights(0, t), weights(2, t), weights(3, t)
-        for copy in first[t]:
-            copy.wait()
-        state = carries(mom_one, t)
-
-        def lines_of(add):
-            def body(i, j, carry):
-                up, down = carry
-                up = step_on(r, up, row_of(f_ref, i, t))
-                down = tuple(r[g] * down[g] for g in range(groups))
-                for n, (values, members) in enumerate(((even, even_groups), (odd, odd_groups))):
-                    one = weighed(values, members, up)
-                    two = weighed(values, members, down)
-                    part[n, i] = part[n, i] + one if add else one
-                    part[n, j] = part[n, j] + two if add else two
-                f = row_of(f_ref, j, t)
-                return up, tuple(down[g] + f[g] for g in range(groups))
-
-            return body
-
-        state = both_ways(0, middle, lines_of(False), state)
-        both_ways(middle, rows, lines_of(True), state)
-        lines[:rows, :] = jnp.sum(part[0], axis=1)
-        lines[rows : 2 * rows, :] = jnp.sum(part[1], axis=1)
-        lines[2 * rows :, :] = jnp.zeros((width - 2 * rows, LANES), F32)
-        if t == 0:
-            for n in range(2):
-                lines[2 * rows + n : 2 * rows + n + 1, :] = jnp.sum(
-                    vec_ref[2 + n] * whole[0], axis=0, keepdims=True
-                )
-        sent[t] = lines[...].T
-        over_owners(t, lambda t, k: line_copy(t, k).start())
-
-    for t in range(tiles):
-        open_tile(t)
-        if t > 0 and t < tiles - 1:
-            close_tile(t - 1)
-    for t in range(max(tiles - 2, 0), tiles):
-        close_tile(t)
-    for copy in faces:
-        copy.start()
-
+    tall = strip + 8
+    tall_row = lax.broadcasted_iota(jnp.int32, (24, tall), 0)
+    tall_column = lax.broadcasted_iota(jnp.int32, (24, tall), 1)
+    cell = lax.broadcasted_iota(jnp.int32, (wave, LANES), 0)
+    spot = lax.broadcasted_iota(jnp.int32, (wave, LANES), 1)
+    lane = lax.broadcasted_iota(jnp.int32, (16, LANES), 1)
+    cut[...] = jnp.zeros_like(cut)
+
+
+    def corner(t):
+        slot = (place_first * count_second + t) * count_second + lax.rem(
+            place_second - t + count_second, count_second
+        )
+        x = jnp.clip(anchor_ref[0, slot] - place_first * rows, 0, rows - REG)
+        return x, slot
+
+    def prepare(t, carry):
+        _, slot = corner(t)
+        y = jnp.clip(anchor_ref[1, slot] - place_second * strip, 0, strip - REG) // 8
+        origin = jnp.clip(anchor_ref[2, slot], 0, wave - REG) - 1 + spot
+        origin = jnp.where(origin < 0, origin + wave, origin)
+        origin = jnp.where(origin >= wave, origin - wave, origin)
+        select = jnp.where(cell == origin, 1.0, 0.0).astype(jnp.bfloat16)
+        wave_high = dot(wave_ref[0], select).astype(jnp.bfloat16)
+        windows[t, :wave, :LANES] = wave_high
+        windows[t, wave:, :LANES] = wave_high
+        windows[t, :wave, LANES:] = dot(wave_ref[1], select).astype(jnp.bfloat16)
+        windows[t, wave:, LANES:] = jnp.zeros((wave, LANES), jnp.bfloat16)
+        wanted = tall_row + 8 * y - 8
+        wanted = jnp.where(wanted < 0, wanted + tall, wanted)
+        pick = jnp.where(tall_column == wanted, 1.0, 0.0).astype(jnp.bfloat16)
+        strip_mix[t] = dot(pick, unstrip_ref[...]).astype(jnp.bfloat16)
+        halo_rows[t] = jnp.broadcast_to(
+            jnp.where(wanted[:, :1] >= strip, 1.0, 0.0), halo_rows.shape[1:]
+        )
+        return carry
+
+    lax.fori_loop(0, count_second, prepare, 0)
     @pl.when(is_owner)
     def _():
-        own = pltpu.make_async_copy(
-            sent.at[own_tile, pl.ds(place_second * chunk, chunk)], got.at[me], self_sem.at[0]
-        )
-        own.start()
         table[...] = jnp.zeros_like(table)
         for i in range(count_first):
             for n in range(2):
@@ -528,6 +402,170 @@
         factor[1] = jnp.where(zero, 2.0 / strip, gain * (0.5 * lam))
         factor[2] = inverse
         factor[3] = jnp.where(zero, 1.0, 0.0)
+
+    first = []
+    whole = []
+
+    def open_tile(t):
+        r = weights(0, t)
+        span = (2 if t == 0 else 3) * block
+
+        def transform(n, carry):
+            piece = pl.ds(n * span, span)
+            spread = pl.ds(pl.multiple_of(n * span * strip, 8), span * strip)
+            if t == 0:
+                for m in range(span // block):
+                    load(n * (span // block) + m).wait()
+                high, low = halves(f_ref[piece].reshape(span * strip, wave))
+                pair[spread, :wave] = high
+                pair[spread, wave:] = low
+            both = dot(pair[spread], forward[t])
+            value = both[:, :LANES] + both[:, LANES:]
+            for m in range(0, span, 2):
+                sides = [value[(m + q) * strip : (m + q + 1) * strip] for q in range(2)]
+                high, low = halves(jnp.concatenate(sides, axis=1))
+                stack = jnp.concatenate([high, high, low], axis=0)
+                result = dot(strip_ref[...], stack)
+                for q in range(2):
+                    f_ref[n * span + m + q, :, lane_of(t)] = result[:, lane_of(q)]
+            return carry
+
+        lax.fori_loop(0, rows // span, transform, 0)
+
+        def moments(i, j, carry):
+            up, down, total = carry
+            f = row_of(f_ref, i, t)
+            up = step_on(r, up, f)
+            down = step_on(r, down, row_of(f_ref, j, t))
+            if t == 0:
+                total = tuple(total[g] + f[g] for g in range(groups))
+            return up, down, total
+
+        up, down, total = both_ways(0, rows, moments, (zeros, zeros, zeros if t == 0 else ()))
+        store_moments(mom_one, t, up, down)
+        if t == 0:
+            whole.append(jnp.concatenate(total, axis=0))
+            pl.semaphore_wait(barrier, devices - 1)
+        first.append(shares(mom_one, send_one, recv_one, t))
+        for copy in first[t] + (faces if t == 0 else []):
+            copy.start()
+
+    def line_copy(t, k):
+        return pltpu.make_async_remote_copy(
+            src_ref=sent.at[t, pl.ds(k * chunk, chunk)],
+            dst_ref=got.at[me],
+            send_sem=send_line.at[t, k],
+            recv_sem=recv_line.at[me],
+            device_id=(lax.rem(owner_shift(k) + t, count_first), k),
+            device_id_type=mesh,
+        )
+
+    def line_from(d):
+        return pltpu.make_async_remote_copy(
+            src_ref=sent.at[0, pl.ds(0, chunk)],
+            dst_ref=got.at[d],
+            send_sem=self_sem.at[1],
+            recv_sem=recv_line.at[d],
+            device_id=(d // count_second, lax.rem(d, count_second)),
+            device_id_type=mesh,
+        )
+
+    def back_copy(d):
+        return pltpu.make_async_remote_copy(
+            src_ref=answer.at[d],
+            dst_ref=back.at[own_tile, pl.ds(place_second * chunk, chunk)],
+            send_sem=send_back.at[d],
+            recv_sem=recv_back.at[own_tile, place_second],
+            device_id=(d // count_second, lax.rem(d, count_second)),
+            device_id_type=mesh,
+        )
+
+    def back_from(t, k):
+        return pltpu.make_async_remote_copy(
+            src_ref=answer.at[0],
+            dst_ref=back.at[t, pl.ds(k * chunk, chunk)],
+            send_sem=self_sem.at[1],
+            recv_sem=recv_back.at[t, k],
+            device_id=(lax.rem(owner_shift(k) + t, count_first), k),
+            device_id_type=mesh,
+        )
+
+    def over_devices(action, part=None):
+        def body(d, carry):
+            @pl.when(d != me)
+            def _():
+                action(d)
+
+            return carry
+
+        start, stop = 0, devices
+        if part is not None:
+            start, stop = part * count_second, (part + 1) * count_second
+        lax.fori_loop(start, stop, body, 0)
+
+    def over_owners(t, action):
+        def body(k, carry):
+            @pl.when((k != place_second) | (own_tile != t))
+            def _():
+                action(t, k)
+
+            return carry
+
+        lax.fori_loop(0, count_second, body, 0)
+
+    def weighed(values, members, state):
+        total = None
+        for g in members:
+            term = values[g] * state[g]
+            total = term if total is None else total + term
+        return total
+
+    def close_tile(t):
+        r, even, odd = weights(0, t), weights(2, t), weights(3, t)
+        for copy in first[t]:
+            copy.wait()
+        state = carries(mom_one, t)
+
+        def lines_of(add):
+            def body(i, j, carry):
+                up, down = carry
+                up = step_on(r, up, row_of(f_ref, i, t))
+                down = tuple(r[g] * down[g] for g in range(groups))
+                for n, (values, members) in enumerate(((even, even_groups), (odd, odd_groups))):
+                    one = weighed(values, members, up)
+                    two = weighed(values, members, down)
+                    part[n, i] = part[n, i] + one if add else one
+                    part[n, j] = part[n, j] + two if add else two
+                f = row_of(f_ref, j, t)
+                return up, tuple(down[g] + f[g] for g in range(groups))
+
+            return body
+
+        state = both_ways(0, middle, lines_of(False), state)
+        both_ways(middle, rows, lines_of(True), state)
+        lines[:rows, :] = jnp.sum(part[0], axis=1)
+        lines[rows : 2 * rows, :] = jnp.sum(part[1], axis=1)
+        lines[2 * rows :, :] = jnp.zeros((width - 2 * rows, LANES), F32)
+        if t == 0:
+            for n in range(2):
+                lines[2 * rows + n : 2 * rows + n + 1, :] = jnp.sum(
+                    vec_ref[2 + n] * whole[0], axis=0, keepdims=True
+                )
+        sent[t] = lines[...].T
+        over_owners(t, lambda t, k: line_copy(t, k).start())
+
+    for t in range(tiles):
+        open_tile(t)
+        if t > 0 and t < tiles - 1:
+            close_tile(t - 1)
+    for t in range(max(tiles - 2, 0), tiles):
+        close_tile(t)
+    @pl.when(is_owner)
+    def _():
+        own = pltpu.make_async_copy(
+            sent.at[own_tile, pl.ds(place_second * chunk, chunk)], got.at[me], self_sem.at[0]
+        )
+        own.start()
         modes = None
         own.wait()
         for i in range(count_first):
@@ -552,7 +590,8 @@
         lever = jnp.sum(jnp.where(lane == 2 * rows + 1, sums, 0.0), axis=1, keepdims=True)
         k = np.arange(strip)
         bow = 0.5 * (k * k - (strip - 1) * k) - strip / 4
-        mean = jnp.where(own_eig[:chunk] <= 0.0, sigma, 0.0) * (1.0 / (wave * wave))
+        first_eig = own_ref[pl.ds(own_tile * LANES + place_second * chunk, chunk), :]
+        mean = jnp.where(first_eig <= 0.0, sigma, 0.0) * (1.0 / (wave * wave))
         gauge = lever - mean * float(wave * count_second * bow.sum())
         gauge = gauge * float(1.0 / (bow[0] * np.sqrt(wave * count_second)))
         tall = lambda value: jnp.concatenate([value] * count_second, axis=0)
@@ -578,44 +617,6 @@
         kept.start()
         kept.wait()
 
-    tall = strip + 8
-    tall_row = lax.broadcasted_iota(jnp.int32, (24, tall), 0)
-    tall_column = lax.broadcasted_iota(jnp.int32, (24, tall), 1)
-    cell = lax.broadcasted_iota(jnp.int32, (wave, LANES), 0)
-    spot = lax.broadcasted_iota(jnp.int32, (wave, LANES), 1)
-    lane = lax.broadcasted_iota(jnp.int32, (16, LANES), 1)
-    cut[...] = jnp.zeros_like(cut)
-
-
-    def corner(t):
-        slot = (place_first * count_second + t) * count_second + lax.rem(
-            place_second - t + count_second, count_second
-        )
-        x = jnp.clip(anchor_ref[0, slot] - place_first * rows, 0, rows - REG)
-        return x, slot
-
-    def prepare(t, carry):
-        _, slot = corner(t)
-        y = jnp.clip(anchor_ref[1, slot] - place_second * strip, 0, strip - REG) // 8
-        origin = jnp.clip(anchor_ref[2, slot], 0, wave - REG) - 1 + spot
-        origin = jnp.where(origin < 0, origin + wave, origin)
-        origin = jnp.where(origin >= wave, origin - wave, origin)
-        select = jnp.where(cell == origin, 1.0, 0.0).astype(jnp.bfloat16)
-        wave_high = dot(wave_ref[0], select).astype(jnp.bfloat16)
-        windows[t, :wave, :LANES] = wave_high
-        windows[t, wave:, :LANES] = wave_high
-        windows[t, :wave, LANES:] = dot(wave_ref[1], select).astype(jnp.bfloat16)
-        windows[t, wave:, LANES:] = jnp.zeros((wave, LANES), jnp.bfloat16)
-        wanted = tall_row + 8 * y - 8
-        wanted = jnp.where(wanted < 0, wanted + tall, wanted)
-        pick = jnp.where(tall_column == wanted, 1.0, 0.0).astype(jnp.bfloat16)
-        strip_mix[t] = dot(pick, unstrip_ref[...]).astype(jnp.bfloat16)
-        halo_rows[t] = jnp.broadcast_to(
-            jnp.where(wanted[:, :1] >= strip, 1.0, 0.0), halo_rows.shape[1:]
-        )
-        return carry
-
-    lax.fori_loop(0, count_second, prepare, 0)
     second = []
     edge_ref[...] = jnp.zeros_like(edge_ref)
     for t in range(tiles):

time: 79.6 us -> 79.9 us (level)
  no operation moved by 1% of the time
where the time goes in v8:
time: 79.9 us; the launch traced here: 79.6 us
  Pallas kernels  78.9 us (99%)
    pallas_call x1, Pallas kernels, poisson(): pl.pallas_call(lambda *refs: grid_kernel((count_first, count_second), *re...  63.3 us
    pallas_call x1, Pallas kernels, local(): pl.pallas_call(subgrid_kernel, grid=(per_device,), in_specs=[smem, smem,...  15.6 us

profile of v8, /device:TPU:0, one launch (start us, length us, event | category | flops | bytes accessed | tf_op | source)
XLA Modules:
  0.0 79.6 jit_solution(15084214962578588605)
XLA Ops:
  0.6 63.3 %shard_map.193 = (f32[96,48,384]{2,1,0:T(8,128)}, f32[8,3,16,128]{3,2,1,0:T(8,128)}, f32[8,32,128]{2,1,0:T(8,128)}, f32[8,32,128]{2,1,0:T(8,128)}) custom-call(s32[3,256]{1,0:T(4,128)} %refs_0_.1, f32[96,48,384]{2,1,0:T(8,128)} %refs_1_.1, f32[48,1]{1,0:T(8,128)} %constant.30.clone.refs_2_, f32[1,384]{1,0:T(1,128)} %constant.31.clone.refs_3_, ...), custom_call_target="tpu_custom_call" | custom-call | tf_op jit(solution)/shard_map/pallas_call | solution.py:970
  64.0 15.6 %shard_map.194 = (f32[8,32,1024]{2,1,0:T(8,128)}, f32[3,8,32,1024]{3,2,1,0:T(8,128)}, f32[96,48,384]{2,1,0:T(8,128)}) custom-call(s32[32]{0:T(128)} %count_ref.1, s32[2,256]{1,0:T(2,128)} %near_ref.1, f32[8,3,16,128]{3,2,1,0:T(8,128)} %get-tuple-element.10.patch_ref, bf16[40,48]{1,0:T(8,128)(2,1)} %constant.36.clone.xt_ref, ...), custom_call_target="tpu_custom_call" | custom-call | tf_op jit(solution)/shard_map/pallas_call | solution.py:1061

commit v9 on v8

--- a/solution.py
+++ b/solution.py
@@ -371,7 +371,6 @@
         )
         return carry
 
-    lax.fori_loop(0, count_second, prepare, 0)
     @pl.when(is_owner)
     def _():
         table[...] = jnp.zeros_like(table)
@@ -617,6 +616,7 @@
         kept.start()
         kept.wait()
 
+    lax.fori_loop(0, count_second, prepare, 0)
     second = []
     edge_ref[...] = jnp.zeros_like(edge_ref)
     for t in range(tiles):

time: 79.9 us -> 77.8 us (0.974)
  Pallas kernels: 78.9 us -> 76.7 us
    pallas_call x1, Pallas kernels: 63.3 us -> 61.2 us  [poisson(): pl.pallas_call(lambda *refs: grid_kernel((count_first, count_second), *re...]
where the time goes in v9:
time: 77.8 us; the launch traced here: 77.4 us
  Pallas kernels  76.7 us (99%)
    pallas_call x1, Pallas kernels, poisson(): pl.pallas_call(lambda *refs: grid_kernel((count_first, count_second), *re...  61.2 us
    pallas_call x1, Pallas kernels, local(): pl.pallas_call(subgrid_kernel, grid=(per_device,), in_specs=[smem, smem,...  15.6 us

profile of v9, /device:TPU:0, one launch (start us, length us, event | category | flops | bytes accessed | tf_op | source)
XLA Modules:
  0.0 77.4 jit_solution(13472598694539452230)
XLA Ops:
  0.6 61.2 %shard_map.193 = (f32[96,48,384]{2,1,0:T(8,128)}, f32[8,3,16,128]{3,2,1,0:T(8,128)}, f32[8,32,128]{2,1,0:T(8,128)}, f32[8,32,128]{2,1,0:T(8,128)}) custom-call(s32[3,256]{1,0:T(4,128)} %refs_0_.1, f32[96,48,384]{2,1,0:T(8,128)} %refs_1_.1, f32[48,1]{1,0:T(8,128)} %constant.30.clone.refs_2_, f32[1,384]{1,0:T(1,128)} %constant.31.clone.refs_3_, ...), custom_call_target="tpu_custom_call" | custom-call | tf_op jit(solution)/shard_map/pallas_call | solution.py:970
  61.8 15.6 %shard_map.194 = (f32[8,32,1024]{2,1,0:T(8,128)}, f32[3,8,32,1024]{3,2,1,0:T(8,128)}, f32[96,48,384]{2,1,0:T(8,128)}) custom-call(s32[32]{0:T(128)} %count_ref.1, s32[2,256]{1,0:T(2,128)} %near_ref.1, f32[8,3,16,128]{3,2,1,0:T(8,128)} %get-tuple-element.10.patch_ref, bf16[40,48]{1,0:T(8,128)(2,1)} %constant.36.clone.xt_ref, ...), custom_call_target="tpu_custom_call" | custom-call | tf_op jit(solution)/shard_map/pallas_call | solution.py:1061

commit v10 on v9

--- a/solution.py
+++ b/solution.py
@@ -402,6 +402,11 @@
         factor[2] = inverse
         factor[3] = jnp.where(zero, 1.0, 0.0)
 
+    def inside(condition, action):
+        @pl.when(condition)
+        def _():
+            action()
+
     first = []
     whole = []
 
@@ -446,8 +451,11 @@
             whole.append(jnp.concatenate(total, axis=0))
             pl.semaphore_wait(barrier, devices - 1)
         first.append(shares(mom_one, send_one, recv_one, t))
-        for copy in first[t] + (faces if t == 0 else []):
+        for copy in first[t]:
             copy.start()
+        if t == 0:
+            inside(place_second < count_second - 1, faces[0].start)
+            inside(place_second > 0, faces[1].start)
 
     def line_copy(t, k):
         return pltpu.make_async_remote_copy(
@@ -720,13 +728,13 @@
             total = total + (pltpu.roll(line, PATCH * b, 1) if b else line)
         return total
 
-    def patch_pair(n, carry):
-        totals = [patch(2 * n + q) for q in range(2)]
-        for q in range(2):
-            patches[2 * n + q + 1] = totals[q]
+    def patch_group(n, carry):
+        totals = [patch(4 * n + q) for q in range(4)]
+        for q in range(4):
+            patches[4 * n + q + 1] = totals[q]
         return carry
 
-    lax.fori_loop(0, count_second // 2, patch_pair, 0)
+    lax.fori_loop(0, count_second // 4, patch_group, 0)
     patches[0] = patches[count_second]
     patches[count_second + 1] = patches[1]
     own = pltpu.make_async_copy(
@@ -766,7 +774,11 @@
     def _():
         over_devices(lambda d: back_copy(d).wait_send())
 
-    for copy in faces + moves + [own]:
+    inside(place_second < count_second - 1, faces[0].wait_send)
+    inside(place_second > 0, faces[0].wait_recv)
+    inside(place_second > 0, faces[1].wait_send)
+    inside(place_second < count_second - 1, faces[1].wait_recv)
+    for copy in moves + [own]:
         copy.wait()
     for n in range(BLOCKS):
         store(n).wait()

time: 77.8 us -> 77.4 us (level)
  no operation moved by 1% of the time
where the time goes in v10:
time: 77.4 us; the launch traced here: 77 us
  Pallas kernels  76.3 us (99%)
    pallas_call x1, Pallas kernels, poisson(): pl.pallas_call(lambda *refs: grid_kernel((count_first, count_second), *re...  60.7 us
    pallas_call x1, Pallas kernels, local(): pl.pallas_call(subgrid_kernel, grid=(per_device,), in_specs=[smem, smem,...  15.6 us

profile of v10, /device:TPU:0, one launch (start us, length us, event | category | flops | bytes accessed | tf_op | source)
XLA Modules:
  0.0 77.0 jit_solution(14603472649350514435)
XLA Ops:
  0.6 60.7 %shard_map.193 = (f32[96,48,384]{2,1,0:T(8,128)}, f32[8,3,16,128]{3,2,1,0:T(8,128)}, f32[8,32,128]{2,1,0:T(8,128)}, f32[8,32,128]{2,1,0:T(8,128)}) custom-call(s32[3,256]{1,0:T(4,128)} %refs_0_.1, f32[96,48,384]{2,1,0:T(8,128)} %refs_1_.1, f32[48,1]{1,0:T(8,128)} %constant.30.clone.refs_2_, f32[1,384]{1,0:T(1,128)} %constant.31.clone.refs_3_, ...), custom_call_target="tpu_custom_call" | custom-call | tf_op jit(solution)/shard_map/pallas_call | solution.py:982
  61.4 15.6 %shard_map.194 = (f32[8,32,1024]{2,1,0:T(8,128)}, f32[3,8,32,1024]{3,2,1,0:T(8,128)}, f32[96,48,384]{2,1,0:T(8,128)}) custom-call(s32[32]{0:T(128)} %count_ref.1, s32[2,256]{1,0:T(2,128)} %near_ref.1, f32[8,3,16,128]{3,2,1,0:T(8,128)} %get-tuple-element.10.patch_ref, bf16[40,48]{1,0:T(8,128)(2,1)} %constant.36.clone.xt_ref, ...), custom_call_target="tpu_custom_call" | custom-call | tf_op jit(solution)/shard_map/pallas_call | solution.py:1073
